TPU v7x, 32 devices: a whole 2x2x4 slice. The times are simulated.
32 devices in a mesh: energy: 16 (over z, x, core), mode: 2 (over y).
Axes of the slice: x: 2, y: 2, z: 4, core: 2. Of those that a mesh axis runs over, the one named last changes fastest.
Arguments:
- spectral: float32 [16, 896, 896], P('energy', 'mode'), may hold values from -6 to 6
- coupling: bfloat16 [2, 896, 896], P('mode'), may hold values from -0.1875 to 0.1875
- offsets: int32 [2], P('mode'), may hold values from 1 to 2, as said below
- occupation: int32 [2, 16], P('mode', 'energy'), may hold values from 0 to 3
Outputs:
- self_energy: float32 [16, 896, 896], P('energy', 'mode')
Inputs may be any that keep to these rules, and one draw needn't show every extreme that they name: `offsets`: each offset from 1 to 2 belongs to exactly 1 modes.
All inputs are finite; a program needn't handle non-finite values.
Results may differ from a plain program's by a relative error of at most 0.0041.
Values sent between devices are 32-bit elements; how exact they have to be, the bound alone decides.
No kernel may reach another device: no remote copies, remote signals or barrier semaphores. Data moves between devices by JAX's collectives and lax.ppermute only.
A program may use at most 64 MiB of HBM per device.

v0:
```python
import jax
import jax.numpy as jnp
from jax import lax
from jax.sharding import PartitionSpec as P

KMAX = 2


def passed_along(value, axis, steps):
    count = lax.axis_size(axis)
    first, last = (max(0, -steps), min(count, count - steps))
    return lax.ppermute(value, axis, [(source, source + steps) for source in range(first, last)])


def collect_rim(own_block, max_offset):
    per_device = own_block.shape[0]
    farthest = -(-max_offset // per_device)
    requests = []
    for distance in range(farthest, 0, -1):
        requests.append((distance, max(0, distance * per_device - max_offset), per_device))
    for distance in range(1, farthest + 1):
        requests.append((-distance, 0, min(per_device, max_offset - (distance - 1) * per_device)))
    lower_parts = []
    upper_parts = []
    for shift_by, first_row, last_row in requests:
        arrived = passed_along(own_block, "energy", shift_by)
        if shift_by > 0:
            lower_parts.append(arrived)
        else:
            upper_parts.append(arrived)
    return jnp.concatenate(lower_parts + [own_block] + upper_parts, axis=0)


def shards(spectral, coupling, offsets, occupation):
    max_offset = KMAX
    full_block = lax.all_gather(spectral, "mode", axis=1, tiled=True)
    window = collect_rim(full_block, max_offset)
    per_device = spectral.shape[0]
    window_len = window.shape[0]
    position = lax.broadcasted_iota(jnp.int32, (1, per_device, window_len), 2)
    energy_pos = lax.broadcasted_iota(jnp.int32, (1, per_device, window_len), 1) + max_offset
    offset_col = offsets[:, None, None]
    emission = (occupation + 1).astype(jnp.float32)[:, :, None]
    absorption = occupation.astype(jnp.float32)[:, :, None]
    weights_table = jnp.where(position == energy_pos - offset_col, emission, 0.0)
    weights_table = weights_table + jnp.where(position == energy_pos + offset_col, absorption, 0.0)
    combined = jnp.einsum(
        "mew,wij->meij", weights_table, window, precision=lax.Precision.HIGHEST
    ).astype(jnp.bfloat16)
    coupled = jnp.einsum(
        "mij,mejk->meik", coupling, combined, preferred_element_type=jnp.float32
    ).astype(jnp.bfloat16)
    partial_sum = jnp.einsum("meik,mlk->eil", coupled, coupling, preferred_element_type=jnp.float32)
    modes_all = coupling.shape[0] * lax.axis_size("mode")
    summed = lax.psum_scatter(partial_sum, "mode", scatter_dimension=1, tiled=True)
    return summed / modes_all


def solution(mesh):
    return jax.shard_map(
        shards,
        mesh=mesh,
        in_specs=(P("energy", "mode", None), P("mode", None, None), P("mode"), P("mode", "energy")),
        out_specs=P("energy", "mode", None),
        check_vma=False,
    )
```

profile of v0, /device:TPU:0, one launch (start us, length us, event | category | flops | bytes accessed | tf_op | source)
XLA Modules:
  0.0 364.9 jit_solution(18186890064561788735)
XLA Ops:
  6.5 0.0 copy-start
  6.5 0.0 all-gather.2.cloned.1.call-start
  6.5 0.7 all-gather.2.cloned.1.call-update
  7.3 0.0 reduce-scatter.2.cloned.1.call-start
  7.3 50.0 %all-gather.2.cloned.1.call-done = f32[1,896,896]{2,1,0:T(8,128)} async-done(((f32[1,448,896]{2,1,0:T(8,128)}), f32[1,896,896]{2,1,0:T(8,128)}) %all-gather.2.cloned.1.call-update) | async-done | bytes 3211280 | tf_op jit(solution)/shard_map/all_gather | solution.py:36
  57.3 3.6 collective-permute-start
  60.9 1.5 collective-permute-start.1
  62.4 1.3 collective-permute-start.2
  63.7 1.3 collective-permute-start.3
  66.3 167.8 %collective-permute-done = f32[1,896,896]{2,1,0:T(8,128)S(1)} collective-permute-done((f32[1,896,896]{2,1,0:T(8,128)}, f32[1,896,896]{2,1,0:T(8,128)S(1)}, u32[]{:S(2)}, u32[]{:S(2)}) %collective-permute-start) | collective-permute-done | bytes 3211296 | tf_op jit(solution)/shard_map/ppermute | solution.py:12
  234.1 0.2 constant_dynamic-update-slice_fusion.4
  234.3 0.0 collective-permute-done.1
  234.3 0.2 constant_dynamic-update-slice_fusion.3
  234.5 1.7 copy-done.1
  236.2 0.2 constant_dynamic-update-slice_fusion.2
  236.4 0.0 collective-permute-done.2
  236.4 0.2 constant_dynamic-update-slice_fusion.1
  236.6 0.0 collective-permute-done.3
  236.6 0.2 constant_dynamic-update-slice_fusion
  236.9 35.2 %fusion = bf16[1,896,896]{2,0,1:T(2,128)(2,1)} fusion(f32[5,896,896]{2,1,0:T(8,128)S(1)} %constant_dynamic-update-slice_fusion, f32[]{:T(128)} %bitcast.3, s32[]{:T(128)} %bitcast.2, f32[]{:T(128)} %bitcast.1, s32[]{:T(128)} %bitcast), kind=kOutput, calls=%fused_computation | convolution fusion | flops 48168984 | bytes 17661968 | tf_op jit(solution)/shard_map/mew,wij->meij/dot_general | solution.py:47
  272.1 7.5 %convolution_bitcast_fusion = f32[1,896,896]{2,1,0:T(8,128)} fusion(bf16[1,896,896]{2,1,0:T(8,128)(2,1)S(1)} %copy-done, bf16[1,896,896]{2,0,1:T(2,128)(2,1)} %fusion), kind=kOutput, calls=%fused_computation.3 | convolution fusion | flops 2878095360 | bytes 6422528 | tf_op jit(solution)/shard_map/meik,mlk->eil/dot_general | solution.py:53
  279.6 0.0 reduce-scatter.2.cloned.1.call-update
  279.6 75.7 %reduce-scatter.2.cloned.1.call-done = f32[1,448,896]{2,1,0:T(8,128)} async-done(((f32[1,896,896]{2,1,0:T(8,128)}), f32[1,448,896]{2,1,0:T(8,128)}) %reduce-scatter.2.cloned.1.call-update) | async-done | bytes 1605648 | tf_op jit(solution)/shard_map/reduce_scatter | solution.py:55
  355.4 2.7 broadcast_multiply_fusion
  (2 shorter events, 0.0 us)
Async XLA Ops:
  6.5 265.6 %copy-start = (bf16[1,896,896]{2,1,0:T(8,128)(2,1)S(1)}, bf16[1,896,896]{2,1,0:T(8,128)(2,1)}, u32[]{:S(2)}) copy-start(bf16[1,896,896]{2,1,0:T(8,128)(2,1)} %param.5) | copy-start | bytes 4816900
  6.5 50.7 %all-gather.2.cloned.1.call-start = ((), (), s32[]{:S(2)}) async-start(), calls=%async_computation.1 | async-start | bytes 4816896 | tf_op jit(solution)/shard_map/all_gather | solution.py:36
  7.3 348.1 %reduce-scatter.2.cloned.1.call-start = ((), (), s32[]{:S(2)}) async-start(), calls=%async_computation.2 | async-start | bytes 4816896 | tf_op jit(solution)/shard_map/reduce_scatter | solution.py:55
  57.3 176.8 %collective-permute-start = (f32[1,896,896]{2,1,0:T(8,128)}, f32[1,896,896]{2,1,0:T(8,128)S(1)}, u32[]{:S(2)}, u32[]{:S(2)}) collective-permute-start(f32[1,896,896]{2,1,0:T(8,128)} %all-gather.2.cloned.1.call-done), channel_id=1, source_target_pairs={{0,4},{2,6},{4,8},{6,10},{8,12},{10,14},{12,16},{14,18},{16,20},{1... | collective-permute-start | bytes 9633800 | tf_op jit(solution)/shard_map/ppermute | solution.py:12
  60.9 173.4 %collective-permute-start.1 = (f32[1,896,896]{2,1,0:T(8,128)}, f32[1,896,896]{2,1,0:T(8,128)S(1)}, u32[]{:S(2)}, u32[]{:S(2)}) collective-permute-start(f32[1,896,896]{2,1,0:T(8,128)} %all-gather.2.cloned.1.call-done), channel_id=1, source_target_pairs={{0,2},{2,4},{4,6},{6,8},{8,10},{10,12},{12,14},{14,16},{16,18},{18... | collective-permute-start | bytes 9633800 | tf_op jit(solution)/shard_map/ppermute | solution.py:12
  62.4 174.0 %collective-permute-start.2 = (f32[1,896,896]{2,1,0:T(8,128)}, f32[1,896,896]{2,1,0:T(8,128)S(1)}, u32[]{:S(2)}, u32[]{:S(2)}) collective-permute-start(f32[1,896,896]{2,1,0:T(8,128)} %all-gather.2.cloned.1.call-done), channel_id=1, source_target_pairs={{2,0},{4,2},{6,4},{8,6},{10,8},{12,10},{14,12},{16,14},{18,16},{20... | collective-permute-start | bytes 9633800 | tf_op jit(solution)/shard_map/ppermute | solution.py:12
  63.7 173.0 %collective-permute-start.3 = (f32[1,896,896]{2,1,0:T(8,128)}, f32[1,896,896]{2,1,0:T(8,128)S(1)}, u32[]{:S(2)}, u32[]{:S(2)}) collective-permute-start(f32[1,896,896]{2,1,0:T(8,128)} %all-gather.2.cloned.1.call-done), channel_id=1, source_target_pairs={{4,0},{6,2},{8,4},{10,6},{12,8},{14,10},{16,12},{18,14},{20,16},{2... | collective-permute-start | bytes 9633800 | tf_op jit(solution)/shard_map/ppermute | solution.py:12
  234.3 1.9 copy-start.1
Sparse Core Ops, SparseCore 0:
  8.9 48.3 all-gather.1
  279.7 75.5 reduce-scatter.1
where the time goes:
time: 365 us
  waiting for transfers between devices  294 us (81%)
  matrix products  42.7 us (12%)
  between operations  14.8 us (4%)
  starting transfers between devices  7.69 us (2%)
    ppermute x4, waiting for transfers between devices, passed_along(): lax.ppermute(value, axis, [(source, source + steps) for source in range(f...  168 us
    reduce_scatter x1, waiting for transfers between devices, shards(): lax.psum_scatter(partial_sum, 'mode', scatter_dimension=1, tiled=True)  75.7 us
    all_gather x1, waiting for transfers between devices, shards(): full_block = lax.all_gather(spectral, 'mode', axis=1, tiled=True)  50 us
    dot_general x1, matrix products, shards(): jnp.einsum('mew,wij->meij', weights_table, window, precision=lax.Precisio...  35.2 us
    ppermute x4, starting transfers between devices, passed_along(): lax.ppermute(value, axis, [(source, source + steps) for source in range(f...  7.65 us
    dot_general x1, matrix products, shards(): jnp.einsum('meik,mlk->eil', coupled, coupling, preferred_element_type=jnp...  7.5 us
  transfers between devices with their start and end apart: 6, of which 3 were waited for; matrix products, arithmetic and copies ran while one was open for 0% of the time, Pallas kernels for 0%

commit v1 on v0

v1 whole, which is shorter than its diff:
```python
import functools

import jax
import jax.numpy as jnp
from jax import lax
from jax.experimental import pallas as pl
from jax.experimental.pallas import tpu as pltpu
from jax.sharding import PartitionSpec as P


VMEM = pl.BlockSpec(memory_space=pltpu.VMEM)
SMEM = pl.BlockSpec(memory_space=pltpu.SMEM)
LOCAL_BYTES = 12 * 2**20
SWAP = [(0, 1), (1, 0)]
INPUT_WIDTH = 256
OUTPUT_CUTS = (256,)


def cuts(extent, width):
    return [(start, min(start + width, extent)) for start in range(0, extent, width)]


def permute_energy(value, target_of):
    count = lax.axis_size("energy")
    pairs = [(source, target_of(source)) for source in range(count)]
    pairs = [(source, target) for source, target in pairs if target is not None and 0 <= target < count]
    return lax.ppermute(value, "energy", pairs)


def partner(energy):
    return energy ^ 1


def across(energy):
    return energy ^ 2


def onward(energy):
    return energy + 4 if energy & 2 == 0 else energy - 4


def straight(energy):
    return energy ^ 1 if (energy >> 1) & 1 == energy & 1 else None


def crossed(energy):
    return energy ^ 1 if (energy >> 1) & 1 != energy & 1 else None


def local_call(kernel, outputs, scalars, arrays):
    held = [pltpu.with_memory_space_constraint(each, pltpu.VMEM) for each in arrays]
    return pl.pallas_call(
        kernel,
        out_shape=[pltpu.VMEM(shape, dtype) for shape, dtype in outputs],
        in_specs=[SMEM] * len(scalars) + [VMEM] * len(held),
        out_specs=[VMEM] * len(outputs),
        compiler_params=pltpu.CompilerParams(vmem_limit_bytes=LOCAL_BYTES),
    )(*scalars, *held)


def take_columns(matrix_ref, out_ref):
    rows = out_ref.shape[1]
    mode = lax.axis_index("mode")

    @pl.when(mode == 0)
    def _():
        out_ref[...] = matrix_ref[:, :rows]

    @pl.when(mode != 0)
    def _():
        out_ref[...] = matrix_ref[:, rows:]


def cut_kernel(columns, own_ref, *refs):
    pieces, sem = refs[:-1], refs[-1]
    copies = [
        pltpu.make_async_copy(own_ref.at[0, :, first:last], piece, sem.at[index])
        for index, ((first, last), piece) in enumerate(zip(columns, pieces))
    ]
    for copy in copies:
        copy.start()
    for copy in copies:
        copy.wait()


def widen_kernel(offset_ref, level_ref, matrix_ref, wide_ref, numbers_ref):
    rows = wide_ref.shape[0]
    core = lax.axis_index("energy") & 1
    wide_ref[...] = matrix_ref[pl.ds(pl.multiple_of(core * rows, rows), rows), :].astype(wide_ref.dtype)
    row = lax.broadcasted_iota(jnp.int32, numbers_ref.shape, 0)
    numbers_ref[...] = jnp.where(row == 0, offset_ref[0], level_ref[0, 0])


def columns_kernel(matrix_ref, out_ref):
    take_columns(matrix_ref, out_ref)


def join_kernel(mine_ref, other_ref, out_ref, left_ref):
    rows = mine_ref.shape[0]
    core = lax.axis_index("energy") & 1
    out_ref[pl.ds(pl.multiple_of(core * rows, rows), rows), :] = mine_ref[...].astype(out_ref.dtype)
    out_ref[pl.ds(pl.multiple_of((1 - core) * rows, rows), rows), :] = other_ref[...].astype(out_ref.dtype)
    take_columns(out_ref, left_ref)


def left_kernel(columns, partner_ref, across_ref, onward_ref, straight_ref, crossed_ref, *refs):
    modes = len(refs) // 3
    numbers, lefts, outs = refs[:modes], refs[modes : 2 * modes], refs[2 * modes :]
    energy = lax.axis_index("energy")
    step = 1 - 2 * (energy & 1)
    far = 2 - 4 * ((energy >> 1) & 1)
    sources = (
        (partner_ref[:, columns[0] : columns[1]], step),
        (across_ref[...], far),
        (onward_ref[...], -far),
        (straight_ref[...] + crossed_ref[...], -step),
    )
    for number, left, out in zip(numbers, lefts, outs):
        offset, level = number[0:1, 0:1], number[1:2, 0:1]
        total = None
        for source, distance in sources:
            below = jnp.where(distance < 0, 1, 0)
            weight = jnp.where(offset == jnp.abs(distance), level + below, 0).astype(jnp.float32)
            total = source * weight if total is None else total + source * weight
        product = jnp.dot(left[...], total.astype(jnp.bfloat16), preferred_element_type=jnp.float32)
        out[...] = product.astype(jnp.bfloat16)


def right_kernel(scale, columns, targets, away, *refs):
    modes = 2
    out_ref = refs[-1]
    couplings = refs[:modes]
    pieces = refs[modes:-1]
    rows = out_ref.shape[0]
    mode = lax.axis_index("mode")
    start = pl.multiple_of((1 - mode if away else mode) * rows, rows)
    low, high = targets
    total = None
    for mode in range(modes):
        for index, (first, last) in enumerate(columns):
            left = pieces[mode * len(columns) + index][pl.ds(start, rows), :]
            term = lax.dot_general(
                left,
                couplings[mode][low:high, first:last],
                (((1,), (1,)), ((), ())),
                preferred_element_type=jnp.float32,
            )
            total = term if total is None else total + term
    out_ref[...] = total * scale


def shards(spectral, coupling, offsets, occupation):
    rows, orbitals = spectral.shape[1:]
    matrix = coupling[0]
    modes = lax.axis_size("mode")
    columns = cuts(orbitals, INPUT_WIDTH)

    own_piece = pl.pallas_call(
        functools.partial(cut_kernel, columns),
        out_shape=[pltpu.VMEM((rows, last - first), jnp.float32) for first, last in columns],
        in_specs=[pl.BlockSpec(memory_space=pl.ANY)],
        out_specs=[VMEM] * len(columns),
        scratch_shapes=[pltpu.SemaphoreType.DMA((len(columns),))],
        compiler_params=pltpu.CompilerParams(vmem_limit_bytes=LOCAL_BYTES),
        name="cut",
    )(spectral)
    across_piece, onward_piece, straight_piece, crossed_piece = [], [], [], []
    for index in range(len(columns)):
        across_piece.append(permute_energy(own_piece[index], across))

    wide, numbers = local_call(
        widen_kernel, [((orbitals // 2, orbitals), jnp.float32), ((8, 128), jnp.int32)], [offsets, occupation], [matrix]
    )
    half_mine = lax.ppermute(wide, "mode", SWAP)
    half_other = permute_energy(half_mine, partner)
    other_numbers = lax.ppermute(numbers, "mode", SWAP)
    partner_piece = permute_energy(spectral[0], partner)

    for index in range(len(columns)):
        onward_piece.append(permute_energy(across_piece[index], onward))
        straight_piece.append(permute_energy(across_piece[index], straight))
        crossed_piece.append(permute_energy(onward_piece[index], crossed))

    left_shape = ((orbitals, rows), matrix.dtype)
    (own_left,) = local_call(columns_kernel, [left_shape], [], [matrix])
    other_matrix, other_left = local_call(
        join_kernel, [(matrix.shape, matrix.dtype), left_shape], [], [half_mine, half_other]
    )
    matrices = (matrix, other_matrix)

    pieces = [[], []]
    for index, (first, last) in enumerate(columns):
        results = local_call(
            functools.partial(left_kernel, (first, last)),
            [((orbitals, last - first), jnp.bfloat16)] * 2,
            [],
            [
                partner_piece,
                across_piece[index],
                onward_piece[index],
                straight_piece[index],
                crossed_piece[index],
                numbers,
                other_numbers,
                own_left,
                other_left,
            ],
        )
        for mode_index in range(2):
            pieces[mode_index].append(results[mode_index])

    def right(away, targets):
        (result,) = local_call(
            functools.partial(right_kernel, 1.0 / modes, columns, targets, away),
            [((rows, targets[1] - targets[0]), jnp.float32)],
            [],
            [*matrices, *pieces[0], *pieces[1]],
        )
        return result

    bounds = (0, *OUTPUT_CUTS, orbitals)
    arrived = []
    for targets in zip(bounds[:-1], bounds[1:]):
        sent = right(True, targets)
        arrived.append(lax.ppermute(sent, "mode", SWAP))
    kept = right(False, (0, orbitals))
    return (kept + jnp.concatenate(arrived, axis=1))[None]


def solution(mesh):
    return jax.shard_map(
        shards,
        mesh=mesh,
        in_specs=(P("energy", "mode", None), P("mode", None, None), P("mode"), P("mode", "energy")),
        out_specs=P("energy", "mode", None),
        check_vma=False,
    )
```

time: 365 us -> 133 us (0.36)
  waiting for transfers between devices: 294 us -> 80.2 us
  matrix products: 42.7 us -> 0 us
  starting transfers between devices: 7.69 us -> 38.5 us
  between operations: 14.8 us -> 1.59 us
  Pallas kernels: 0 us -> 8.03 us
    ppermute x4 -> x22, waiting for transfers between devices: 168 us -> 80.2 us  [the longest x2 32.7 us: shards(): arrived.append(lax.ppermute(sent, 'mode', SWAP))]
    reduce_scatter x1 -> x0, waiting for transfers between devices: 75.7 us -> none  [shards(): lax.psum_scatter(partial_sum, 'mode', scatter_dimension=1, tiled=True)]
    all_gather x1 -> x0, waiting for transfers between devices: 50 us -> none  [shards(): full_block = lax.all_gather(spectral, 'mode', axis=1, tiled=True)]
    dot_general x2 -> x0, matrix products: 42.7 us -> none  [the longest x1 35.2 us: shards(): jnp.einsum('mew,wij->meij', weights_table, window, precision=lax.Precisio...]
    ppermute x4 -> x22, starting transfers between devices: 7.65 us -> 38.5 us  [the longest x18 33.2 us: permute_energy(): return lax.ppermute(value, 'energy', pairs)]
    pallas_call x0 -> x11, Pallas kernels: none -> 8.03 us  [the longest x10 7.88 us: local_call(): pl.pallas_call(kernel, out_shape=[pltpu.VMEM(shape, dtype) for shape, dty...]
  transfers between devices with their start and end apart: 6 -> 22, of which waited for: 3 -> 6; matrix products, arithmetic and copies ran while one was open for 0% -> 0% of each run, Pallas kernels for 0% -> 4%
where the time goes in v1:
time: 133 us; the launch traced here: 132 us
  waiting for transfers between devices  80.2 us (60%)
  starting transfers between devices  38.5 us (29%)
  Pallas kernels  8.03 us (6%)
  local copies, waits for them, and re-layouts  2.83 us (2%)
  between operations  1.59 us (1%)
    ppermute x18, starting transfers between devices, permute_energy(): return lax.ppermute(value, 'energy', pairs)  33.2 us
    ppermute x2, waiting for transfers between devices, shards(): arrived.append(lax.ppermute(sent, 'mode', SWAP))  32.7 us
    ppermute x1, waiting for transfers between devices, shards(): other_numbers = lax.ppermute(numbers, 'mode', SWAP)  29.5 us
    ppermute x18, waiting for transfers between devices, permute_energy(): return lax.ppermute(value, 'energy', pairs)  17.9 us
    pallas_call x10, Pallas kernels, local_call(): pl.pallas_call(kernel, out_shape=[pltpu.VMEM(shape, dtype) for shape, dty...  7.88 us
    ppermute x1, starting transfers between devices, shards(): half_mine = lax.ppermute(wide, 'mode', SWAP)  3.06 us
    unnamed x6, local copies, waits for them, and re-layouts  2.83 us
  transfers between devices with their start and end apart: 22, of which 6 were waited for; matrix products, arithmetic and copies ran while one was open for 0% of the time, Pallas kernels for 4%

profile of v1, /device:TPU:0, one launch (start us, length us, event | category | flops | bytes accessed | tf_op | source)
XLA Modules:
  0.0 132.5 jit_solution(12042573814266418904)
XLA Ops:
  1.3 1.4 %copy-done = bf16[1,896,896]{2,1,0:T(8,128)(2,1)S(1)} copy-done((bf16[1,896,896]{2,1,0:T(8,128)(2,1)S(1)}, bf16[1,896,896]{2,1,0:T(8,128)(2,1)}, u32[]{:S(2)}) %copy-start) | copy-done | bytes 1605656
  2.8 3.1 %collective-permute-start = (f32[448,896]{1,0:T(8,128)S(1)}, f32[448,896]{1,0:T(8,128)S(1)}, u32[]{:S(2)}, u32[]{:S(2)}) collective-permute-start(f32[448,896]{1,0:T(8,128)S(1)} %get-tuple-element.21), channel_id=1, source_target_pairs={{0,1},{1,0},{2,3},{3,2},{4,5},{5,4},{6,7},{7,6},{8,9},{9,8},{10,11... | collective-permute-start | bytes 4816904 | tf_op jit(solution)/shard_map/ppermute | solution.py:174
  5.9 1.4 %copy-done.2 = f32[1,448,896]{2,1,0:T(8,128)S(1)} copy-done((f32[1,448,896]{2,1,0:T(8,128)S(1)}, f32[1,448,896]{2,1,0:T(8,128)}, u32[]{:S(2)}) %copy-start.2) | copy-done | bytes 1605656
  7.5 1.6 %collective-permute-start.3 = (f32[448,256]{1,0:T(8,128)S(1)}, f32[448,256]{1,0:T(8,128)S(1)}, u32[]{:S(2)}, u32[]{:S(2)}) collective-permute-start(f32[448,256]{1,0:T(8,128)S(1)} %get-tuple-element.23), channel_id=1, source_target_pairs={{0,4},{2,6},{4,0},{6,2},{8,12},{10,14},{12,8},{14,10},{16,20},{18,... | collective-permute-start | bytes 1376264 | tf_op jit(solution)/shard_map/ppermute | solution.py:27
  9.7 1.9 %collective-permute-start.8 = (f32[448,256]{1,0:T(8,128)S(1)}, f32[448,256]{1,0:T(8,128)S(1)}, u32[]{:S(2)}, u32[]{:S(2)}) collective-permute-start(f32[448,256]{1,0:T(8,128)S(1)} %get-tuple-element.27), channel_id=1, source_target_pairs={{0,4},{2,6},{4,0},{6,2},{8,12},{10,14},{12,8},{14,10},{16,20},{18,... | collective-permute-start | bytes 1376264 | tf_op jit(solution)/shard_map/ppermute | solution.py:27
  11.6 29.5 %collective-permute-done.7.refs_1_ = s32[8,128]{1,0:T(8,128)S(1)} collective-permute-done((s32[8,128]{1,0:T(8,128)S(1)}, s32[8,128]{1,0:T(8,128)S(1)}, u32[]{:S(2)}, u32[]{:S(2)}) %collective-permute-start.7) | collective-permute-done | bytes 4128 | tf_op jit(solution)/shard_map/ppermute | solution.py:176
  41.1 1.7 %collective-permute-start.12 = (f32[448,256]{1,0:T(8,128)S(1)}, f32[448,256]{1,0:T(8,128)S(1)}, u32[]{:S(2)}, u32[]{:S(2)}) collective-permute-start(f32[448,256]{1,0:T(8,128)S(1)} %get-tuple-element.29), channel_id=1, source_target_pairs={{0,4},{2,6},{4,0},{6,2},{8,12},{10,14},{12,8},{14,10},{16,20},{18,... | collective-permute-start | bytes 1376264 | tf_op jit(solution)/shard_map/ppermute | solution.py:27
  43.3 3.5 %collective-permute-start.17 = (f32[448,128]{1,0:T(8,128)S(1)}, f32[448,128]{1,0:T(8,128)S(1)}, u32[]{:S(2)}, u32[]{:S(2)}) collective-permute-start(f32[448,128]{1,0:T(8,128)S(1)} %collective-permute-done.16.across_ref), channel_id=1, source_target_pairs={{0,8},{2,10},{8,16},{10,18},{12,4},{14,6},{16,24},{18,26},{20,12},... | collective-permute-start | bytes 688136 | tf_op jit(solution)/shard_map/ppermute | solution.py:27
  46.8 3.5 %collective-permute-start.4 = (f32[448,256]{1,0:T(8,128)S(1)}, f32[448,256]{1,0:T(8,128)S(1)}, u32[]{:S(2)}, u32[]{:S(2)}) collective-permute-start(f32[448,256]{1,0:T(8,128)S(1)} %collective-permute-done.3.across_ref), channel_id=1, source_target_pairs={{0,8},{2,10},{8,16},{10,18},{12,4},{14,6},{16,24},{18,26},{20,12},... | collective-permute-start | bytes 1376264 | tf_op jit(solution)/shard_map/ppermute | solution.py:27
  50.3 2.4 %collective-permute-done.12.across_ref = f32[448,256]{1,0:T(8,128)S(1)} collective-permute-done((f32[448,256]{1,0:T(8,128)S(1)}, f32[448,256]{1,0:T(8,128)S(1)}, u32[]{:S(2)}, u32[]{:S(2)}) %collective-permute-start.12) | collective-permute-done | bytes 458784 | tf_op jit(solution)/shard_map/ppermute | solution.py:27
  52.8 1.3 collective-permute-start.5
  54.1 3.5 %collective-permute-start.9 = (f32[448,256]{1,0:T(8,128)S(1)}, f32[448,256]{1,0:T(8,128)S(1)}, u32[]{:S(2)}, u32[]{:S(2)}) collective-permute-start(f32[448,256]{1,0:T(8,128)S(1)} %collective-permute-done.8.across_ref), channel_id=1, source_target_pairs={{0,8},{2,10},{8,16},{10,18},{12,4},{14,6},{16,24},{18,26},{20,12},... | collective-permute-start | bytes 1376264 | tf_op jit(solution)/shard_map/ppermute | solution.py:27
  57.5 5.1 %collective-permute-done.4.onward_ref = f32[448,256]{1,0:T(8,128)S(1)} collective-permute-done((f32[448,256]{1,0:T(8,128)S(1)}, f32[448,256]{1,0:T(8,128)S(1)}, u32[]{:S(2)}, u32[]{:S(2)}) %collective-permute-start.4) | collective-permute-done | bytes 458784 | tf_op jit(solution)/shard_map/ppermute | solution.py:27
  62.6 1.3 collective-permute-start.10
  63.9 4.4 %collective-permute-start.13 = (f32[448,256]{1,0:T(8,128)S(1)}, f32[448,256]{1,0:T(8,128)S(1)}, u32[]{:S(2)}, u32[]{:S(2)}) collective-permute-start(f32[448,256]{1,0:T(8,128)S(1)} %collective-permute-done.12.across_ref), channel_id=1, source_target_pairs={{0,8},{2,10},{8,16},{10,18},{12,4},{14,6},{16,24},{18,26},{20,12},... | collective-permute-start | bytes 1376264 | tf_op jit(solution)/shard_map/ppermute | solution.py:27
  68.3 4.1 %collective-permute-done.9.onward_ref = f32[448,256]{1,0:T(8,128)S(1)} collective-permute-done((f32[448,256]{1,0:T(8,128)S(1)}, f32[448,256]{1,0:T(8,128)S(1)}, u32[]{:S(2)}, u32[]{:S(2)}) %collective-permute-start.9) | collective-permute-done | bytes 458784 | tf_op jit(solution)/shard_map/ppermute | solution.py:27
  75.0 6.3 %collective-permute-done.13.onward_ref = f32[448,256]{1,0:T(8,128)S(1)} collective-permute-done((f32[448,256]{1,0:T(8,128)S(1)}, f32[448,256]{1,0:T(8,128)S(1)}, u32[]{:S(2)}, u32[]{:S(2)}) %collective-permute-start.13) | collective-permute-done | bytes 458784 | tf_op jit(solution)/shard_map/ppermute | solution.py:27
  81.4 1.3 collective-permute-start.14
  84.0 3.1 %collective-permute-start.18 = (f32[448,128]{1,0:T(8,128)S(1)}, f32[448,128]{1,0:T(8,128)S(1)}, u32[]{:S(2)}, u32[]{:S(2)}) collective-permute-start(f32[448,128]{1,0:T(8,128)S(1)} %collective-permute-done.16.across_ref), channel_id=1, source_target_pairs={{0,2},{6,4},{8,10},{14,12},{16,18},{22,20},{24,26},{30,28},{1,3},{... | collective-permute-start | bytes 688136 | tf_op jit(solution)/shard_map/ppermute | solution.py:27
  92.0 1.6 %shard_map.55 = f32[448,640]{1,0:T(8,128)S(1)} custom-call(bf16[896,896]{1,0:T(8,128)(2,1)S(1)} %bitcast.6, bf16[896,896]{1,0:T(8,128)(2,1)S(1)} %get-tuple-element.22.refs_1_, bf16[896,256]{1,0:T(8,128)(2,1)S(1)} %get-tuple-element.26.refs_2_, bf16[896,256]{1,0:T(8,128)(2,1)S(1)} %get-tuple-element.28.refs_3_, ...), custom_call_target="tpu_custom_call" | custom-call | tf_op jit(solution)/shard_map/pallas_call | solution.py:52
  93.6 2.1 %collective-permute-start.21 = (f32[448,640]{1,0:T(8,128)S(1)}, f32[448,640]{1,0:T(8,128)S(1)}, u32[]{:S(2)}, u32[]{:S(2)}) collective-permute-start(f32[448,640]{1,0:T(8,128)S(1)} %shard_map.55), channel_id=1, source_target_pairs={{0,1},{1,0},{2,3},{3,2},{4,5},{5,4},{6,7},{7,6},{8,9},{9,8},{10,11... | collective-permute-start | bytes 3440648 | tf_op jit(solution)/shard_map/ppermute | solution.py:225
  96.4 2.0 %shard_map.53 = f32[448,896]{1,0:T(8,128)S(1)} custom-call(bf16[896,896]{1,0:T(8,128)(2,1)S(1)} %bitcast.8, bf16[896,896]{1,0:T(8,128)(2,1)S(1)} %get-tuple-element.22.refs_1_, bf16[896,256]{1,0:T(8,128)(2,1)S(1)} %get-tuple-element.26.refs_2_, bf16[896,256]{1,0:T(8,128)(2,1)S(1)} %get-tuple-element.28.refs_3_, ...), custom_call_target="tpu_custom_call" | custom-call | tf_op jit(solution)/shard_map/pallas_call | solution.py:52
  98.4 32.7 %collective-permute-done.20 = f32[448,256]{1,0:T(8,128)S(1)} collective-permute-done((f32[448,256]{1,0:T(8,128)S(1)}, f32[448,256]{1,0:T(8,128)S(1)}, u32[]{:S(2)}, u32[]{:S(2)}) %collective-permute-start.20) | collective-permute-done | bytes 458784 | tf_op jit(solution)/shard_map/ppermute | solution.py:225
  131.2 1.3 fusion
  (38 shorter events, 10.9 us)
Async XLA Ops:
  1.3 1.4 %copy-start = (bf16[1,896,896]{2,1,0:T(8,128)(2,1)S(1)}, bf16[1,896,896]{2,1,0:T(8,128)(2,1)}, u32[]{:S(2)}) copy-start(bf16[1,896,896]{2,1,0:T(8,128)(2,1)} %param.5) | copy-start | bytes 4816900
  2.7 85.7 %copy-start.1 = (bf16[1,896,896]{2,1,0:T(8,128)(2,1)S(1)}, bf16[1,896,896]{2,1,0:T(8,128)(2,1)}, u32[]{:S(2)}) copy-start(bf16[1,896,896]{2,1,0:T(8,128)(2,1)} %param.5) | copy-start | bytes 4816900
  2.8 40.0 %collective-permute-start = (f32[448,896]{1,0:T(8,128)S(1)}, f32[448,896]{1,0:T(8,128)S(1)}, u32[]{:S(2)}, u32[]{:S(2)}) collective-permute-start(f32[448,896]{1,0:T(8,128)S(1)} %get-tuple-element.21), channel_id=1, source_target_pairs={{0,1},{1,0},{2,3},{3,2},{4,5},{5,4},{6,7},{7,6},{8,9},{9,8},{10,11... | collective-permute-start | bytes 4816904 | tf_op jit(solution)/shard_map/ppermute | solution.py:174
  7.5 35.8 %collective-permute-start.3 = (f32[448,256]{1,0:T(8,128)S(1)}, f32[448,256]{1,0:T(8,128)S(1)}, u32[]{:S(2)}, u32[]{:S(2)}) collective-permute-start(f32[448,256]{1,0:T(8,128)S(1)} %get-tuple-element.23), channel_id=1, source_target_pairs={{0,4},{2,6},{4,0},{6,2},{8,12},{10,14},{12,8},{14,10},{16,20},{18,... | collective-permute-start | bytes 1376264 | tf_op jit(solution)/shard_map/ppermute | solution.py:27
  9.0 33.8 %collective-permute-start.16 = (f32[448,128]{1,0:T(8,128)S(1)}, f32[448,128]{1,0:T(8,128)S(1)}, u32[]{:S(2)}, u32[]{:S(2)}) collective-permute-start(f32[448,128]{1,0:T(8,128)S(1)} %get-tuple-element.31), channel_id=1, source_target_pairs={{0,4},{2,6},{4,0},{6,2},{8,12},{10,14},{12,8},{14,10},{16,20},{18,... | collective-permute-start | bytes 688136 | tf_op jit(solution)/shard_map/ppermute | solution.py:27
  9.6 31.5 %collective-permute-start.7 = (s32[8,128]{1,0:T(8,128)S(1)}, s32[8,128]{1,0:T(8,128)S(1)}, u32[]{:S(2)}, u32[]{:S(2)}) collective-permute-start(s32[8,128]{1,0:T(8,128)S(1)} %get-tuple-element.24.refs_0_), channel_id=1, source_target_pairs={{0,1},{1,0},{2,3},{3,2},{4,5},{5,4},{6,7},{7,6},{8,9},{9,8},{10,11... | collective-permute-start | bytes 12296 | tf_op jit(solution)/shard_map/ppermute | solution.py:176
  9.7 37.1 %collective-permute-start.8 = (f32[448,256]{1,0:T(8,128)S(1)}, f32[448,256]{1,0:T(8,128)S(1)}, u32[]{:S(2)}, u32[]{:S(2)}) collective-permute-start(f32[448,256]{1,0:T(8,128)S(1)} %get-tuple-element.27), channel_id=1, source_target_pairs={{0,4},{2,6},{4,0},{6,2},{8,12},{10,14},{12,8},{14,10},{16,20},{18,... | collective-permute-start | bytes 1376264 | tf_op jit(solution)/shard_map/ppermute | solution.py:27
  41.1 11.7 %collective-permute-start.12 = (f32[448,256]{1,0:T(8,128)S(1)}, f32[448,256]{1,0:T(8,128)S(1)}, u32[]{:S(2)}, u32[]{:S(2)}) collective-permute-start(f32[448,256]{1,0:T(8,128)S(1)} %get-tuple-element.29), channel_id=1, source_target_pairs={{0,4},{2,6},{4,0},{6,2},{8,12},{10,14},{12,8},{14,10},{16,20},{18,... | collective-permute-start | bytes 1376264 | tf_op jit(solution)/shard_map/ppermute | solution.py:27
  42.8 41.2 %collective-permute-start.2 = (f32[448,896]{1,0:T(8,128)S(1)}, f32[448,896]{1,0:T(8,128)S(1)}, u32[]{:S(2)}, u32[]{:S(2)}) collective-permute-start(f32[448,896]{1,0:T(8,128)S(1)} %bitcast.9), channel_id=1, source_target_pairs={{0,2},{2,0},{4,6},{6,4},{8,10},{10,8},{12,14},{14,12},{16,18},{18,... | collective-permute-start | bytes 4816904 | tf_op jit(solution)/shard_map/ppermute | solution.py:27
  42.8 44.3 %collective-permute-start.1 = (f32[448,896]{1,0:T(8,128)S(1)}, f32[448,896]{1,0:T(8,128)S(1)}, u32[]{:S(2)}, u32[]{:S(2)}) collective-permute-start(f32[448,896]{1,0:T(8,128)S(1)} %collective-permute-done.mine_ref), channel_id=1, source_target_pairs={{0,2},{2,0},{4,6},{6,4},{8,10},{10,8},{12,14},{14,12},{16,18},{18,... | collective-permute-start | bytes 4816904 | tf_op jit(solution)/shard_map/ppermute | solution.py:27
  43.3 10.8 %collective-permute-start.17 = (f32[448,128]{1,0:T(8,128)S(1)}, f32[448,128]{1,0:T(8,128)S(1)}, u32[]{:S(2)}, u32[]{:S(2)}) collective-permute-start(f32[448,128]{1,0:T(8,128)S(1)} %collective-permute-done.16.across_ref), channel_id=1, source_target_pairs={{0,8},{2,10},{8,16},{10,18},{12,4},{14,6},{16,24},{18,26},{20,12},... | collective-permute-start | bytes 688136 | tf_op jit(solution)/shard_map/ppermute | solution.py:27
  46.8 15.8 %collective-permute-start.4 = (f32[448,256]{1,0:T(8,128)S(1)}, f32[448,256]{1,0:T(8,128)S(1)}, u32[]{:S(2)}, u32[]{:S(2)}) collective-permute-start(f32[448,256]{1,0:T(8,128)S(1)} %collective-permute-done.3.across_ref), channel_id=1, source_target_pairs={{0,8},{2,10},{8,16},{10,18},{12,4},{14,6},{16,24},{18,26},{20,12},... | collective-permute-start | bytes 1376264 | tf_op jit(solution)/shard_map/ppermute | solution.py:27
  52.8 11.2 %collective-permute-start.5 = (f32[448,256]{1,0:T(8,128)S(1)}, f32[448,256]{1,0:T(8,128)S(1)}, u32[]{:S(2)}, u32[]{:S(2)}) collective-permute-start(f32[448,256]{1,0:T(8,128)S(1)} %collective-permute-done.3.across_ref), channel_id=1, source_target_pairs={{0,2},{6,4},{8,10},{14,12},{16,18},{22,20},{24,26},{30,28},{1,3},{... | collective-permute-start | bytes 1376264 | tf_op jit(solution)/shard_map/ppermute | solution.py:27
  54.1 18.3 %collective-permute-start.9 = (f32[448,256]{1,0:T(8,128)S(1)}, f32[448,256]{1,0:T(8,128)S(1)}, u32[]{:S(2)}, u32[]{:S(2)}) collective-permute-start(f32[448,256]{1,0:T(8,128)S(1)} %collective-permute-done.8.across_ref), channel_id=1, source_target_pairs={{0,8},{2,10},{8,16},{10,18},{12,4},{14,6},{16,24},{18,26},{20,12},... | collective-permute-start | bytes 1376264 | tf_op jit(solution)/shard_map/ppermute | solution.py:27
  62.6 11.1 %collective-permute-start.10 = (f32[448,256]{1,0:T(8,128)S(1)}, f32[448,256]{1,0:T(8,128)S(1)}, u32[]{:S(2)}, u32[]{:S(2)}) collective-permute-start(f32[448,256]{1,0:T(8,128)S(1)} %collective-permute-done.8.across_ref), channel_id=1, source_target_pairs={{0,2},{6,4},{8,10},{14,12},{16,18},{22,20},{24,26},{30,28},{1,3},{... | collective-permute-start | bytes 1376264 | tf_op jit(solution)/shard_map/ppermute | solution.py:27
  63.9 17.4 %collective-permute-start.13 = (f32[448,256]{1,0:T(8,128)S(1)}, f32[448,256]{1,0:T(8,128)S(1)}, u32[]{:S(2)}, u32[]{:S(2)}) collective-permute-start(f32[448,256]{1,0:T(8,128)S(1)} %collective-permute-done.12.across_ref), channel_id=1, source_target_pairs={{0,8},{2,10},{8,16},{10,18},{12,4},{14,6},{16,24},{18,26},{20,12},... | collective-permute-start | bytes 1376264 | tf_op jit(solution)/shard_map/ppermute | solution.py:27
  72.4 10.2 %collective-permute-start.6 = (f32[448,256]{1,0:T(8,128)S(1)}, f32[448,256]{1,0:T(8,128)S(1)}, u32[]{:S(2)}, u32[]{:S(2)}) collective-permute-start(f32[448,256]{1,0:T(8,128)S(1)} %collective-permute-done.4.onward_ref), channel_id=1, source_target_pairs={{2,0},{4,6},{10,8},{12,14},{18,16},{20,22},{26,24},{28,30},{3,1},{... | collective-permute-start | bytes 1376264 | tf_op jit(solution)/shard_map/ppermute | solution.py:27
  73.7 15.8 %collective-permute-start.11 = (f32[448,256]{1,0:T(8,128)S(1)}, f32[448,256]{1,0:T(8,128)S(1)}, u32[]{:S(2)}, u32[]{:S(2)}) collective-permute-start(f32[448,256]{1,0:T(8,128)S(1)} %collective-permute-done.9.onward_ref), channel_id=1, source_target_pairs={{2,0},{4,6},{10,8},{12,14},{18,16},{20,22},{26,24},{28,30},{3,1},{... | collective-permute-start | bytes 1376264 | tf_op jit(solution)/shard_map/ppermute | solution.py:27
  81.4 9.0 %collective-permute-start.14 = (f32[448,256]{1,0:T(8,128)S(1)}, f32[448,256]{1,0:T(8,128)S(1)}, u32[]{:S(2)}, u32[]{:S(2)}) collective-permute-start(f32[448,256]{1,0:T(8,128)S(1)} %collective-permute-done.12.across_ref), channel_id=1, source_target_pairs={{0,2},{6,4},{8,10},{14,12},{16,18},{22,20},{24,26},{30,28},{1,3},{... | collective-permute-start | bytes 1376264 | tf_op jit(solution)/shard_map/ppermute | solution.py:27
  82.7 7.7 %collective-permute-start.15 = (f32[448,256]{1,0:T(8,128)S(1)}, f32[448,256]{1,0:T(8,128)S(1)}, u32[]{:S(2)}, u32[]{:S(2)}) collective-permute-start(f32[448,256]{1,0:T(8,128)S(1)} %collective-permute-done.13.onward_ref), channel_id=1, source_target_pairs={{2,0},{4,6},{10,8},{12,14},{18,16},{20,22},{26,24},{28,30},{3,1},{... | collective-permute-start | bytes 1376264 | tf_op jit(solution)/shard_map/ppermute | solution.py:27
  84.0 7.2 %collective-permute-start.18 = (f32[448,128]{1,0:T(8,128)S(1)}, f32[448,128]{1,0:T(8,128)S(1)}, u32[]{:S(2)}, u32[]{:S(2)}) collective-permute-start(f32[448,128]{1,0:T(8,128)S(1)} %collective-permute-done.16.across_ref), channel_id=1, source_target_pairs={{0,2},{6,4},{8,10},{14,12},{16,18},{22,20},{24,26},{30,28},{1,3},{... | collective-permute-start | bytes 688136 | tf_op jit(solution)/shard_map/ppermute | solution.py:27
  87.1 4.2 %collective-permute-start.19 = (f32[448,128]{1,0:T(8,128)S(1)}, f32[448,128]{1,0:T(8,128)S(1)}, u32[]{:S(2)}, u32[]{:S(2)}) collective-permute-start(f32[448,128]{1,0:T(8,128)S(1)} %collective-permute-done.17.onward_ref), channel_id=1, source_target_pairs={{2,0},{4,6},{10,8},{12,14},{18,16},{20,22},{26,24},{28,30},{3,1},{... | collective-permute-start | bytes 688136 | tf_op jit(solution)/shard_map/ppermute | solution.py:27
  93.6 37.6 %collective-permute-start.21 = (f32[448,640]{1,0:T(8,128)S(1)}, f32[448,640]{1,0:T(8,128)S(1)}, u32[]{:S(2)}, u32[]{:S(2)}) collective-permute-start(f32[448,640]{1,0:T(8,128)S(1)} %shard_map.55), channel_id=1, source_target_pairs={{0,1},{1,0},{2,3},{3,2},{4,5},{5,4},{6,7},{7,6},{8,9},{9,8},{10,11... | collective-permute-start | bytes 3440648 | tf_op jit(solution)/shard_map/ppermute | solution.py:225
  96.3 34.9 %collective-permute-start.20 = (f32[448,256]{1,0:T(8,128)S(1)}, f32[448,256]{1,0:T(8,128)S(1)}, u32[]{:S(2)}, u32[]{:S(2)}) collective-permute-start(f32[448,256]{1,0:T(8,128)S(1)} %shard_map.54), channel_id=1, source_target_pairs={{0,1},{1,0},{2,3},{3,2},{4,5},{5,4},{6,7},{7,6},{8,9},{9,8},{10,11... | collective-permute-start | bytes 1376264 | tf_op jit(solution)/shard_map/ppermute | solution.py:225
  (1 other events, 1.4 us)

commit v2 on v0

v2 whole, which is shorter than its diff:
```python
import functools

import jax
import jax.numpy as jnp
from jax import lax
from jax.experimental import pallas as pl
from jax.experimental.pallas import tpu as pltpu
from jax.sharding import PartitionSpec as P


VMEM = pl.BlockSpec(memory_space=pltpu.VMEM)
SMEM = pl.BlockSpec(memory_space=pltpu.SMEM)
LOCAL_BYTES = 12 * 2**20
SWAP = [(0, 1), (1, 0)]
WIDTH = 256
OUT_FIRST = 256
SECOND = ((0, 1), (1, 2), (2, 4))


def cuts(extent, width):
    return [(start, min(start + width, extent)) for start in range(0, extent, width)]


def detour(energy):
    return energy - 4 if energy & 2 == 0 else energy + 4


def is_early(energy):
    return (energy ^ (energy >> 1)) & 1


def permute_energy(value, target_of, early=None):
    count = lax.axis_size("energy")
    pairs = [(source, target_of(source)) for source in range(count) if early is None or is_early(source) == early]
    return lax.ppermute(value, "energy", [(source, target) for source, target in pairs if 0 <= target < count])


def permute_mode(value, early):
    count, modes = lax.axis_size("energy"), lax.axis_size("mode")
    pairs = [
        (energy * modes + mode, energy * modes + other)
        for energy in range(count)
        if is_early(energy) == early
        for mode, other in SWAP
    ]
    return lax.ppermute(value, ("energy", "mode"), pairs)


def partner(energy):
    return energy ^ 1


def across(energy):
    return energy ^ 2


def onward(energy):
    return energy + 4 if energy & 2 == 0 else energy - 4


def local_call(kernel, outputs, scalars, arrays):
    held = [pltpu.with_memory_space_constraint(each, pltpu.VMEM) for each in arrays]
    return pl.pallas_call(
        kernel,
        out_shape=[pltpu.VMEM(shape, dtype) for shape, dtype in outputs],
        in_specs=[SMEM] * len(scalars) + [VMEM] * len(held),
        out_specs=[VMEM] * len(outputs),
        compiler_params=pltpu.CompilerParams(vmem_limit_bytes=LOCAL_BYTES),
    )(*scalars, *held)


def take_columns(matrix_ref, out_ref):
    rows = out_ref.shape[1]
    mode = lax.axis_index("mode")

    @pl.when(mode == 0)
    def _():
        out_ref[...] = matrix_ref[:, :rows]

    @pl.when(mode != 0)
    def _():
        out_ref[...] = matrix_ref[:, rows:]


def cut_kernel(columns, own_ref, *refs):
    pieces, sem = refs[:-1], refs[-1]
    copies = [
        pltpu.make_async_copy(own_ref.at[0, :, first:last], piece, sem.at[index])
        for index, ((first, last), piece) in enumerate(zip(columns, pieces))
    ]
    for copy in copies:
        copy.start()
    for copy in copies:
        copy.wait()


def merge_kernel(*refs):
    at = 0
    for piece in refs[:-1]:
        width = piece.shape[1]
        refs[-1][:, at : at + width] = piece[...]
        at += width


def part_of(matrix_ref, part, index):
    at = ((lax.axis_index("energy") & 1) * 2 + index) * part
    return matrix_ref[pl.ds(pl.multiple_of(at, part), part), :]


def widen_kernel(matrix_ref, out_ref):
    out_ref[...] = part_of(matrix_ref, out_ref.shape[0], 0).astype(out_ref.dtype)


def widen_more_kernel(offset_ref, level_ref, matrix_ref, out_ref):
    orbitals = matrix_ref.shape[0]
    part = orbitals // 4
    out_ref[0:part, :] = part_of(matrix_ref, part, 1).astype(out_ref.dtype)
    row = lax.broadcasted_iota(jnp.int32, (out_ref.shape[0] - part, orbitals), 0)
    out_ref[part:, :] = jnp.where(row == 0, offset_ref[0], level_ref[0, 0]).astype(out_ref.dtype)


def columns_kernel(matrix_ref, out_ref):
    take_columns(matrix_ref, out_ref)


def join_kernel(*refs):
    halves, (out_ref, left_ref) = refs[:-2], refs[-2:]
    part = out_ref.shape[0] // 4
    core = lax.axis_index("energy") & 1
    for index, half in enumerate(halves):
        owner = core if index < 2 else 1 - core
        at = pl.multiple_of((2 * owner + index % 2) * part, part)
        out_ref[pl.ds(at, part), :] = half[0:part, :].astype(out_ref.dtype)
    take_columns(out_ref, left_ref)


def piece_view(refs, starts, first, last):
    for ref, start in zip(refs, starts):
        if start <= first and last <= start + ref.shape[1]:
            return ref[:, first - start : last - start]
    raise ValueError((first, last, starts))


def left_kernel(tiles, layout, early, number, left, *refs):
    out, combined = refs[-2:]
    rows = combined.shape[0]
    split, at = [], 0
    for starts in layout:
        split.append((refs[at : at + len(starts)], starts))
        at += len(starts)
    energy = lax.axis_index("energy")

    @pl.when(is_early(energy) == early)
    def _():
        step = 1 - 2 * (energy & 1)
        far = 2 - 4 * ((energy >> 1) & 1)
        told = left.shape[0] // 4
        start = pl.multiple_of((1 - lax.axis_index("mode")) * rows, rows)
        offset, level = number[told : told + 1, 0:1], number[told + 1 : told + 2, 0:1]

        def weight(distance):
            gap = jnp.abs(distance).astype(jnp.float32)
            below = jnp.where(distance < 0, 1, 0).astype(jnp.float32)
            return jnp.where(offset == gap, level + below, 0.0)

        weights = [weight(distance) for distance in (step, far, -far, -step)]
        for first, last in tiles:
            total = None
            for (pieces, starts), factor in zip(split, weights):
                term = piece_view(pieces, starts, first, last) * factor
                total = term if total is None else total + term
            total = total.astype(jnp.bfloat16)
            span = slice(first - tiles[0][0], last - tiles[0][0])
            combined[:, span] = total
            product = jnp.dot(left[pl.ds(start, rows), :], total, preferred_element_type=jnp.float32)
            out[:, span] = product.astype(jnp.bfloat16)


def right_product(couplings, pieces, columns, targets):
    low, high = targets
    total = None
    for coupling, lefts in zip(couplings, pieces):
        for left, (first, last) in zip(lefts, columns):
            term = lax.dot_general(
                left, coupling[low:high, first:last], (((1,), (1,)), ((), ())), preferred_element_type=jnp.float32
            )
            total = term if total is None else total + term
    return total


def send_kernel(scale, columns, targets, early, *refs):
    pieces, out_ref = refs[2:-1], refs[-1]
    many = len(columns)

    @pl.when(is_early(lax.axis_index("energy")) == early)
    def _():
        lefts = [[piece[...] for piece in pieces[mode * many : (mode + 1) * many]] for mode in range(2)]
        out_ref[...] = right_product(refs[:2], lefts, columns, targets) * scale


def keep_kernel(scale, columns, targets, *refs):
    couplings, lefts, out_ref = refs[:2], refs[2:4], refs[-1]
    rows = out_ref.shape[0]
    start = pl.multiple_of(lax.axis_index("mode") * rows, rows)
    many = len(columns)
    for early in range(2):
        pieces = refs[4 + 2 * many * early : 4 + 2 * many * (early + 1)]

        @pl.when(is_early(lax.axis_index("energy")) == early)
        def _(pieces=pieces):
            held = [
                [
                    jnp.dot(
                        left[pl.ds(start, rows), :], piece[...], preferred_element_type=jnp.float32
                    ).astype(jnp.bfloat16)
                    for piece in pieces[mode * many : (mode + 1) * many]
                ]
                for mode, left in enumerate(lefts)
            ]
            out_ref[...] = right_product(couplings, held, columns, targets) * scale


def finish_kernel(columns, *refs):
    kept_ref, early_ref, late_ref = refs[:3]
    out_ref, total_ref, sem = refs[-3:]
    first, last = columns
    total_ref[...] = kept_ref[:, first:last] + (early_ref[...] + late_ref[...])
    copy = pltpu.make_async_copy(total_ref, out_ref.at[0, :, first:last], sem)
    copy.start()
    copy.wait()


def finish(columns, kept, early, late, before):
    rows, orbitals = kept.shape
    held = [pltpu.with_memory_space_constraint(each, pltpu.VMEM) for each in (kept, early, late)]
    return pl.pallas_call(
        functools.partial(finish_kernel, columns),
        out_shape=jax.ShapeDtypeStruct((1, rows, orbitals), kept.dtype),
        in_specs=[VMEM] * 3 + [pl.BlockSpec(memory_space=pl.ANY)] * len(before),
        out_specs=pl.BlockSpec(memory_space=pl.ANY),
        scratch_shapes=[pltpu.VMEM((rows, columns[1] - columns[0]), kept.dtype), pltpu.SemaphoreType.DMA],
        input_output_aliases={3: 0} if before else {},
        compiler_params=pltpu.CompilerParams(vmem_limit_bytes=LOCAL_BYTES),
        name="finish",
    )(*held, *before)


def cut(spectral, columns):
    return pl.pallas_call(
        functools.partial(cut_kernel, columns),
        out_shape=[pltpu.VMEM((spectral.shape[1], last - first), jnp.float32) for first, last in columns],
        in_specs=[pl.BlockSpec(memory_space=pl.ANY)],
        out_specs=[VMEM] * len(columns),
        scratch_shapes=[pltpu.SemaphoreType.DMA((len(columns),))],
        compiler_params=pltpu.CompilerParams(vmem_limit_bytes=LOCAL_BYTES),
    )(spectral)


def merged(pieces):
    if len(pieces) == 1:
        return pieces[0]
    rows = pieces[0].shape[0]
    return local_call(merge_kernel, [((rows, sum(each.shape[1] for each in pieces)), jnp.float32)], [], pieces)[0]


def shards(spectral, coupling, offsets, occupation):
    rows, orbitals = spectral.shape[1:]
    matrix = coupling[0]
    scale = 1.0 / lax.axis_size("mode")
    tiles = cuts(orbitals, WIDTH)
    half = len(tiles) // 2
    sides = ((0, half), (half, len(tiles)))

    own_piece = cut(spectral, tiles[:1])
    across_piece = [permute_energy(own_piece[0], across)]
    own_piece += cut(spectral, tiles[1:])
    for index in range(1, len(tiles)):
        across_piece.append(permute_energy(own_piece[index], across))

    part = orbitals // 4
    (wide,) = local_call(widen_kernel, [((part, orbitals), jnp.float32)], [], [matrix])
    (wide_rest,) = local_call(widen_more_kernel, [((part + 8, orbitals), jnp.float32)], [offsets, occupation], [matrix])
    told = lax.ppermute(wide, "mode", SWAP)
    told_rest = lax.ppermute(wide_rest, "mode", SWAP)
    swapped = permute_energy(told, partner)
    swapped_rest = permute_energy(told_rest, partner)
    partner_piece = permute_energy(spectral[0], partner)

    first_piece = []
    for index in range(len(tiles) - 1):
        first_piece.append(permute_energy(across_piece[index], onward, early=1))
    aside = permute_energy(own_piece[-1], detour, early=0)
    first_piece.append(permute_energy(aside, across, early=0))
    second_piece = []
    for low, high in SECOND:
        second_piece.append(permute_energy(merged(across_piece[low:high]), onward, early=0))
    straight_piece = []
    for low, high in sides:
        straight_piece.append(permute_energy(merged(across_piece[low:high]), partner, early=0))
    crossed_piece = permute_energy(merged(first_piece), partner, early=1)

    left_shape = ((orbitals, rows), matrix.dtype)
    (own_left,) = local_call(columns_kernel, [left_shape], [], [matrix])
    other_matrix, other_left = local_call(
        join_kernel, [(matrix.shape, matrix.dtype), left_shape], [], [told, told_rest, swapped, swapped_rest]
    )
    matrices = (matrix, other_matrix)

    starts = [first for first, last in tiles]

    def left(which, low, high, early, onward_pieces, onward_starts, back_piece, back_start):
        number, columns = ((wide_rest, own_left), (told_rest, other_left))[which]
        layout = ([0], starts[low:high], onward_starts, [back_start])
        width = tiles[high - 1][1] - tiles[low][0]
        return local_call(
            functools.partial(left_kernel, tiles[low:high], layout, early),
            [((rows, width), jnp.bfloat16)] * 2,
            [],
            [number, columns, partner_piece, *across_piece[low:high], *onward_pieces, back_piece],
        )

    early_pieces, late_pieces = [], []
    for which in range(2):
        for index, (low, high) in enumerate(sides):
            early_pieces.append(
                left(
                    which, low, high, 1,
                    first_piece[low:high], starts[low:high], straight_piece[index], starts[low],
                )
            )
            seconds = [each for each, (begin, end) in enumerate(SECOND) if low <= begin and end <= high]
            late_pieces.append(
                left(
                    which, low, high, 0,
                    [second_piece[each] for each in seconds], [starts[SECOND[each][0]] for each in seconds],
                    crossed_piece, 0,
                )
            )
    columns = [(tiles[low][0], tiles[high - 1][1]) for low, high in sides]

    bounds = ((0, OUT_FIRST), (OUT_FIRST, orbitals))
    arrived = []
    for early, pieces in ((1, early_pieces), (0, late_pieces)):
        got = []
        for targets in bounds:
            (sent,) = local_call(
                functools.partial(send_kernel, scale, columns, targets, early),
                [((rows, targets[1] - targets[0]), jnp.float32)],
                [],
                [*matrices, *(left for left, combined in pieces)],
            )
            got.append(permute_mode(sent, early))
        arrived.append(got)
    combined = [each for pieces in (late_pieces, early_pieces) for left, each in pieces]
    (kept,) = local_call(
        functools.partial(keep_kernel, scale, columns, (0, orbitals)),
        [((rows, orbitals), jnp.float32)],
        [],
        [*matrices, own_left, other_left, *combined],
    )
    result = []
    for index, targets in enumerate(bounds):
        result = [finish(targets, kept, arrived[0][index], arrived[1][index], result)]
    return result[0]


def solution(mesh):
    return jax.shard_map(
        shards,
        mesh=mesh,
        in_specs=(P("energy", "mode", None), P("mode", None, None), P("mode"), P("mode", "energy")),
        out_specs=P("energy", "mode", None),
        check_vma=False,
    )
```

time: 365 us -> 107 us (0.29)
  waiting for transfers between devices: 294 us -> 50.8 us
  matrix products: 42.7 us -> 0 us
  starting transfers between devices: 7.69 us -> 40.4 us
  Pallas kernels: 0 us -> 13.2 us
  between operations: 14.8 us -> 1.85 us
    ppermute x4 -> x24, waiting for transfers between devices: 168 us -> 50.8 us  [the longest x18 34.5 us: permute_energy(): lax.ppermute(value, 'energy', [(source, target) for source, target in pai...]
    reduce_scatter x1 -> x0, waiting for transfers between devices: 75.7 us -> none  [shards(): lax.psum_scatter(partial_sum, 'mode', scatter_dimension=1, tiled=True)]
    all_gather x1 -> x0, waiting for transfers between devices: 50 us -> none  [shards(): full_block = lax.all_gather(spectral, 'mode', axis=1, tiled=True)]
    dot_general x2 -> x0, matrix products: 42.7 us -> none  [the longest x1 35.2 us: shards(): jnp.einsum('mew,wij->meij', weights_table, window, precision=lax.Precisio...]
    ppermute x4 -> x24, starting transfers between devices: 7.65 us -> 40.4 us  [the longest x18 29 us: permute_energy(): lax.ppermute(value, 'energy', [(source, target) for source, target in pai...]
    pallas_call x0 -> x24, Pallas kernels: none -> 13.2 us  [the longest x20 8.68 us: local_call(): pl.pallas_call(kernel, out_shape=[pltpu.VMEM(shape, dtype) for shape, dty...]
  transfers between devices with their start and end apart: 6 -> 24, of which waited for: 3 -> 8; matrix products, arithmetic and copies ran while one was open for 0% -> 0% of each run, Pallas kernels for 0% -> 10%
where the time goes in v2:
time: 107 us; the launch traced here: 106 us
  waiting for transfers between devices  50.8 us (47%)
  starting transfers between devices  40.4 us (38%)
  Pallas kernels  13.2 us (12%)
  between operations  1.85 us (2%)
    ppermute x18, waiting for transfers between devices, permute_energy(): lax.ppermute(value, 'energy', [(source, target) for source, target in pai...  34.5 us
    ppermute x18, starting transfers between devices, permute_energy(): lax.ppermute(value, 'energy', [(source, target) for source, target in pai...  29 us
    ppermute x4, waiting for transfers between devices, permute_mode(): return lax.ppermute(value, ('energy', 'mode'), pairs)  12.2 us
    pallas_call x20, Pallas kernels, local_call(): pl.pallas_call(kernel, out_shape=[pltpu.VMEM(shape, dtype) for shape, dty...  8.68 us
    ppermute x4, starting transfers between devices, permute_mode(): return lax.ppermute(value, ('energy', 'mode'), pairs)  7.27 us
    ppermute x1, waiting for transfers between devices, shards(): told_rest = lax.ppermute(wide_rest, 'mode', SWAP)  4.08 us
    pallas_call x2, Pallas kernels, cut(): pl.pallas_call(functools.partial(cut_kernel, columns), out_shape=[pltpu.V...  2.39 us
  transfers between devices with their start and end apart: 24, of which 8 were waited for; matrix products, arithmetic and copies ran while one was open for 0% of the time, Pallas kernels for 10%

profile of v2, /device:TPU:0, one launch (start us, length us, event | category | flops | bytes accessed | tf_op | source)
XLA Modules:
  0.0 106.2 jit_solution(11929411725370544719)
XLA Ops:
  1.2 3.0 %collective-permute-start.5 = (f32[448,256]{1,0:T(8,128)S(1)}, f32[448,256]{1,0:T(8,128)S(1)}, u32[]{:S(2)}, u32[]{:S(2)}) collective-permute-start(f32[448,256]{1,0:T(8,128)S(1)} %shard_map.50), channel_id=1, source_target_pairs={{0,4},{2,6},{4,0},{6,2},{8,12},{10,14},{12,8},{14,10},{16,20},{18,... | collective-permute-start | bytes 1376264 | tf_op jit(solution)/shard_map/ppermute | solution.py:35
  5.5 2.0 %collective-permute-start.11 = (f32[448,256]{1,0:T(8,128)S(1)}, f32[448,256]{1,0:T(8,128)S(1)}, u32[]{:S(2)}, u32[]{:S(2)}) collective-permute-start(f32[448,256]{1,0:T(8,128)S(1)} %get-tuple-element.29), channel_id=1, source_target_pairs={{0,4},{2,6},{4,0},{6,2},{8,12},{10,14},{12,8},{14,10},{16,20},{18,... | collective-permute-start | bytes 1376264 | tf_op jit(solution)/shard_map/ppermute | solution.py:35
  8.8 6.7 %collective-permute-done.5.refs_1_.refs_0_ = f32[448,256]{1,0:T(8,128)S(1)} collective-permute-done((f32[448,256]{1,0:T(8,128)S(1)}, f32[448,256]{1,0:T(8,128)S(1)}, u32[]{:S(2)}, u32[]{:S(2)}) %collective-permute-start.5) | collective-permute-done | bytes 458784 | tf_op jit(solution)/shard_map/ppermute | solution.py:35
  16.3 2.1 %collective-permute-start = (f32[224,896]{1,0:T(8,128)S(1)}, f32[224,896]{1,0:T(8,128)S(1)}, u32[]{:S(2)}, u32[]{:S(2)}) collective-permute-start(f32[224,896]{1,0:T(8,128)S(1)} %shard_map.46), channel_id=1, source_target_pairs={{0,1},{1,0},{2,3},{3,2},{4,5},{5,4},{6,7},{7,6},{8,9},{9,8},{10,11... | collective-permute-start | bytes 2408456 | tf_op jit(solution)/shard_map/ppermute | solution.py:283
  18.4 4.0 %collective-permute-start.14 = (f32[448,128]{1,0:T(8,128)S(1)}, f32[448,128]{1,0:T(8,128)S(1)}, u32[]{:S(2)}, u32[]{:S(2)}) collective-permute-start(f32[448,128]{1,0:T(8,128)S(1)} %collective-permute-done.13), channel_id=1, source_target_pairs={{0,4},{6,2},{8,12},{14,10},{16,20},{22,18},{24,28},{30,26},{1,5},{... | collective-permute-start | bytes 688136 | tf_op jit(solution)/shard_map/ppermute | solution.py:35
  22.5 2.9 %collective-permute-done.6.refs_2_.refs_1_ = f32[448,256]{1,0:T(8,128)S(1)} collective-permute-done((f32[448,256]{1,0:T(8,128)S(1)}, f32[448,256]{1,0:T(8,128)S(1)}, u32[]{:S(2)}, u32[]{:S(2)}) %collective-permute-start.6) | collective-permute-done | bytes 458784 | tf_op jit(solution)/shard_map/ppermute | solution.py:35
  27.4 7.8 %collective-permute-done.11.refs_0_.refs_1_ = f32[448,256]{1,0:T(8,128)S(1)} collective-permute-done((f32[448,256]{1,0:T(8,128)S(1)}, f32[448,256]{1,0:T(8,128)S(1)}, u32[]{:S(2)}, u32[]{:S(2)}) %collective-permute-start.11) | collective-permute-done | bytes 458784 | tf_op jit(solution)/shard_map/ppermute | solution.py:35
  35.2 2.0 %collective-permute-start.1 = (f32[232,896]{1,0:T(8,128)S(1)}, f32[232,896]{1,0:T(8,128)S(1)}, u32[]{:S(2)}, u32[]{:S(2)}) collective-permute-start(f32[232,896]{1,0:T(8,128)S(1)} %shard_map.47.number), channel_id=1, source_target_pairs={{0,1},{1,0},{2,3},{3,2},{4,5},{5,4},{6,7},{7,6},{8,9},{9,8},{10,11... | collective-permute-start | bytes 2494472 | tf_op jit(solution)/shard_map/ppermute | solution.py:284
  38.0 2.5 %collective-permute-start.4 = (f32[448,896]{1,0:T(8,128)}, f32[448,896]{1,0:T(8,128)S(1)}, u32[]{:S(2)}, u32[]{:S(2)}) collective-permute-start(f32[448,896]{1,0:T(8,128)} %bitcast.1), channel_id=1, source_target_pairs={{0,2},{2,0},{4,6},{6,4},{8,10},{10,8},{12,14},{14,12},{16,18},{18,... | collective-permute-start | bytes 4816904 | tf_op jit(solution)/shard_map/ppermute | solution.py:35
  40.7 1.3 %collective-permute-start.15 = (f32[448,896]{1,0:T(8,128)S(1)}, f32[448,896]{1,0:T(8,128)S(1)}, u32[]{:S(2)}, u32[]{:S(2)}) collective-permute-start(f32[448,896]{1,0:T(8,128)S(1)} %shard_map.52), channel_id=1, source_target_pairs={{2,0},{4,6},{10,8},{12,14},{18,16},{20,22},{26,24},{28,30},{3,1},{... | collective-permute-start | bytes 4816904 | tf_op jit(solution)/shard_map/ppermute | solution.py:35
  42.0 6.1 %collective-permute-done.16.refs_1_.refs_2_ = f32[448,128]{1,0:T(8,128)S(1)} collective-permute-done((f32[448,128]{1,0:T(8,128)S(1)}, f32[448,128]{1,0:T(8,128)S(1)}, u32[]{:S(2)}, u32[]{:S(2)}) %collective-permute-start.16) | collective-permute-done | bytes 229408 | tf_op jit(solution)/shard_map/ppermute | solution.py:35
  48.1 1.3 %collective-permute-start.18 = (f32[448,512]{1,0:T(8,128)S(1)}, f32[448,512]{1,0:T(8,128)S(1)}, u32[]{:S(2)}, u32[]{:S(2)}) collective-permute-start(f32[448,512]{1,0:T(8,128)S(1)} %shard_map.58), channel_id=1, source_target_pairs={{0,2},{6,4},{8,10},{14,12},{16,18},{22,20},{24,26},{30,28},{1,3},{... | collective-permute-start | bytes 2752520 | tf_op jit(solution)/shard_map/ppermute | solution.py:35
  49.5 1.3 %collective-permute-start.19 = (f32[448,384]{1,0:T(8,128)S(1)}, f32[448,384]{1,0:T(8,128)S(1)}, u32[]{:S(2)}, u32[]{:S(2)}) collective-permute-start(f32[448,384]{1,0:T(8,128)S(1)} %shard_map.54), channel_id=1, source_target_pairs={{0,2},{6,4},{8,10},{14,12},{16,18},{22,20},{24,26},{30,28},{1,3},{... | collective-permute-start | bytes 2064392 | tf_op jit(solution)/shard_map/ppermute | solution.py:35
  50.8 4.1 %collective-permute-done.1.refs_1_.number = f32[232,896]{1,0:T(8,128)S(1)} collective-permute-done((f32[232,896]{1,0:T(8,128)S(1)}, f32[232,896]{1,0:T(8,128)S(1)}, u32[]{:S(2)}, u32[]{:S(2)}) %collective-permute-start.1) | collective-permute-done | bytes 831520 | tf_op jit(solution)/shard_map/ppermute | solution.py:284
  55.4 3.5 %collective-permute-start.17 = (f32[448,384]{1,0:T(8,128)S(1)}, f32[448,384]{1,0:T(8,128)S(1)}, u32[]{:S(2)}, u32[]{:S(2)}) collective-permute-start(f32[448,384]{1,0:T(8,128)S(1)} %shard_map.54), channel_id=1, source_target_pairs={{0,8},{8,16},{14,6},{16,24},{22,14},{30,22},{1,9},{9,17},{15,7},{1... | collective-permute-start | bytes 2064392 | tf_op jit(solution)/shard_map/ppermute | solution.py:35
  59.0 3.5 %collective-permute-start.7 = (f32[448,256]{1,0:T(8,128)S(1)}, f32[448,256]{1,0:T(8,128)S(1)}, u32[]{:S(2)}, u32[]{:S(2)}) collective-permute-start(f32[448,256]{1,0:T(8,128)S(1)} %collective-permute-done.5.refs_1_.refs_0_), channel_id=1, source_target_pairs={{0,8},{8,16},{14,6},{16,24},{22,14},{30,22},{1,9},{9,17},{15,7},{1... | collective-permute-start | bytes 1376264 | tf_op jit(solution)/shard_map/ppermute | solution.py:35
  62.4 2.6 %collective-permute-start.8 = (f32[448,256]{1,0:T(8,128)S(1)}, f32[448,256]{1,0:T(8,128)S(1)}, u32[]{:S(2)}, u32[]{:S(2)}) collective-permute-start(f32[448,256]{1,0:T(8,128)S(1)} %collective-permute-done.6.refs_2_.refs_1_), channel_id=1, source_target_pairs={{0,8},{8,16},{14,6},{16,24},{22,14},{30,22},{1,9},{9,17},{15,7},{1... | collective-permute-start | bytes 1376264 | tf_op jit(solution)/shard_map/ppermute | solution.py:35
  66.3 6.0 %collective-permute-done.7.refs_3_ = f32[448,256]{1,0:T(8,128)S(1)} collective-permute-done((f32[448,256]{1,0:T(8,128)S(1)}, f32[448,256]{1,0:T(8,128)S(1)}, u32[]{:S(2)}, u32[]{:S(2)}) %collective-permute-start.7) | collective-permute-done | bytes 458784 | tf_op jit(solution)/shard_map/ppermute | solution.py:35
  72.3 4.9 %collective-permute-done.8.refs_4_ = f32[448,256]{1,0:T(8,128)S(1)} collective-permute-done((f32[448,256]{1,0:T(8,128)S(1)}, f32[448,256]{1,0:T(8,128)S(1)}, u32[]{:S(2)}, u32[]{:S(2)}) %collective-permute-start.8) | collective-permute-done | bytes 458784 | tf_op jit(solution)/shard_map/ppermute | solution.py:35
  79.7 1.6 %shard_map.65 = f32[448,640]{1,0:T(8,128)S(1)} custom-call(bf16[896,896]{1,0:T(8,128)(2,1)S(1)} %bitcast.6, bf16[896,896]{1,0:T(8,128)(2,1)S(1)} %get-tuple-element.26.refs_1_, bf16[448,512]{1,0:T(8,128)(2,1)S(1)} %get-tuple-element.43.refs_2_, bf16[448,384]{1,0:T(8,128)(2,1)S(1)} %get-tuple-element.44.refs_3_, ...), custom_call_target="tpu_custom_call" | custom-call | tf_op jit(solution)/shard_map/pallas_call | solution.py:63
  81.3 3.4 %collective-permute-start.21 = (f32[448,640]{1,0:T(8,128)S(1)}, f32[448,640]{1,0:T(8,128)S(1)}, u32[]{:S(2)}, u32[]{:S(2)}) collective-permute-start(f32[448,640]{1,0:T(8,128)S(1)} %shard_map.65), channel_id=1, source_target_pairs={{0,1},{1,0},{6,7},{7,6},{8,9},{9,8},{14,15},{15,14},{16,17},{17,16... | collective-permute-start | bytes 3440648 | tf_op jit(solution)/shard_map/ppermute | solution.py:46
  86.1 2.4 %collective-permute-start.23 = (f32[448,256]{1,0:T(8,128)S(1)}, f32[448,256]{1,0:T(8,128)S(1)}, u32[]{:S(2)}, u32[]{:S(2)}) collective-permute-start(f32[448,256]{1,0:T(8,128)S(1)} %shard_map.67), channel_id=1, source_target_pairs={{0,1},{1,0},{6,7},{7,6},{8,9},{9,8},{14,15},{15,14},{16,17},{17,16... | collective-permute-start | bytes 1376264 | tf_op jit(solution)/shard_map/ppermute | solution.py:46
  88.5 3.2 %shard_map.63.refs_0_ = f32[448,896]{1,0:T(8,128)S(1)} custom-call(bf16[896,896]{1,0:T(8,128)(2,1)S(1)} %bitcast.9, bf16[896,896]{1,0:T(8,128)(2,1)S(1)} %get-tuple-element.26.refs_1_, bf16[896,448]{1,0:T(8,128)(2,1)S(1)} %shard_map.49.left.refs_2_, bf16[896,448]{1,0:T(8,128)(2,1)S(1)} %get-tuple-element.27.left.refs_3_, ...), custom_call_target="tpu_custom_call" | custom-call | tf_op jit(solution)/shard_map/pallas_call | solution.py:63
  91.7 12.2 %collective-permute-done.23.refs_2_ = f32[448,256]{1,0:T(8,128)S(1)} collective-permute-done((f32[448,256]{1,0:T(8,128)S(1)}, f32[448,256]{1,0:T(8,128)S(1)}, u32[]{:S(2)}, u32[]{:S(2)}) %collective-permute-start.23) | collective-permute-done | bytes 458784 | tf_op jit(solution)/shard_map/ppermute | solution.py:46
  (50 shorter events, 13.8 us)
Async XLA Ops:
  1.2 14.4 %collective-permute-start.5 = (f32[448,256]{1,0:T(8,128)S(1)}, f32[448,256]{1,0:T(8,128)S(1)}, u32[]{:S(2)}, u32[]{:S(2)}) collective-permute-start(f32[448,256]{1,0:T(8,128)S(1)} %shard_map.50), channel_id=1, source_target_pairs={{0,4},{2,6},{4,0},{6,2},{8,12},{10,14},{12,8},{14,10},{16,20},{18,... | collective-permute-start | bytes 1376264 | tf_op jit(solution)/shard_map/ppermute | solution.py:35
  5.4 19.9 %collective-permute-start.6 = (f32[448,256]{1,0:T(8,128)S(1)}, f32[448,256]{1,0:T(8,128)S(1)}, u32[]{:S(2)}, u32[]{:S(2)}) collective-permute-start(f32[448,256]{1,0:T(8,128)S(1)} %get-tuple-element.28), channel_id=1, source_target_pairs={{0,4},{2,6},{4,0},{6,2},{8,12},{10,14},{12,8},{14,10},{16,20},{18,... | collective-permute-start | bytes 1376264 | tf_op jit(solution)/shard_map/ppermute | solution.py:35
  5.5 29.7 %collective-permute-start.11 = (f32[448,256]{1,0:T(8,128)S(1)}, f32[448,256]{1,0:T(8,128)S(1)}, u32[]{:S(2)}, u32[]{:S(2)}) collective-permute-start(f32[448,256]{1,0:T(8,128)S(1)} %get-tuple-element.29), channel_id=1, source_target_pairs={{0,4},{2,6},{4,0},{6,2},{8,12},{10,14},{12,8},{14,10},{16,20},{18,... | collective-permute-start | bytes 1376264 | tf_op jit(solution)/shard_map/ppermute | solution.py:35
  7.5 10.9 %collective-permute-start.13 = (f32[448,128]{1,0:T(8,128)S(1)}, f32[448,128]{1,0:T(8,128)S(1)}, u32[]{:S(2)}, u32[]{:S(2)}) collective-permute-start(f32[448,128]{1,0:T(8,128)S(1)} %get-tuple-element.30), channel_id=1, source_target_pairs={{6,14},{8,0},{14,22},{16,8},{22,30},{24,16},{7,15},{9,1},{15,23},{... | collective-permute-start | bytes 688136 | tf_op jit(solution)/shard_map/ppermute | solution.py:35
  15.6 22.4 %collective-permute-start.9 = (f32[448,256]{1,0:T(8,128)S(1)}, f32[448,256]{1,0:T(8,128)S(1)}, u32[]{:S(2)}, u32[]{:S(2)}) collective-permute-start(f32[448,256]{1,0:T(8,128)S(1)} %collective-permute-done.5.refs_1_.refs_0_), channel_id=1, source_target_pairs={{2,10},{10,18},{12,4},{18,26},{20,12},{28,20},{3,11},{11,19},{13,5... | collective-permute-start | bytes 1376264 | tf_op jit(solution)/shard_map/ppermute | solution.py:35
  16.3 33.2 %collective-permute-start = (f32[224,896]{1,0:T(8,128)S(1)}, f32[224,896]{1,0:T(8,128)S(1)}, u32[]{:S(2)}, u32[]{:S(2)}) collective-permute-start(f32[224,896]{1,0:T(8,128)S(1)} %shard_map.46), channel_id=1, source_target_pairs={{0,1},{1,0},{2,3},{3,2},{4,5},{5,4},{6,7},{7,6},{8,9},{9,8},{10,11... | collective-permute-start | bytes 2408456 | tf_op jit(solution)/shard_map/ppermute | solution.py:283
  18.4 18.8 %collective-permute-start.14 = (f32[448,128]{1,0:T(8,128)S(1)}, f32[448,128]{1,0:T(8,128)S(1)}, u32[]{:S(2)}, u32[]{:S(2)}) collective-permute-start(f32[448,128]{1,0:T(8,128)S(1)} %collective-permute-done.13), channel_id=1, source_target_pairs={{0,4},{6,2},{8,12},{14,10},{16,20},{22,18},{24,28},{30,26},{1,5},{... | collective-permute-start | bytes 688136 | tf_op jit(solution)/shard_map/ppermute | solution.py:35
  25.4 15.1 %collective-permute-start.10 = (f32[448,256]{1,0:T(8,128)S(1)}, f32[448,256]{1,0:T(8,128)S(1)}, u32[]{:S(2)}, u32[]{:S(2)}) collective-permute-start(f32[448,256]{1,0:T(8,128)S(1)} %collective-permute-done.6.refs_2_.refs_1_), channel_id=1, source_target_pairs={{2,10},{10,18},{12,4},{18,26},{20,12},{28,20},{3,11},{11,19},{13,5... | collective-permute-start | bytes 1376264 | tf_op jit(solution)/shard_map/ppermute | solution.py:35
  35.2 19.7 %collective-permute-start.1 = (f32[232,896]{1,0:T(8,128)S(1)}, f32[232,896]{1,0:T(8,128)S(1)}, u32[]{:S(2)}, u32[]{:S(2)}) collective-permute-start(f32[232,896]{1,0:T(8,128)S(1)} %shard_map.47.number), channel_id=1, source_target_pairs={{0,1},{1,0},{2,3},{3,2},{4,5},{5,4},{6,7},{7,6},{8,9},{9,8},{10,11... | collective-permute-start | bytes 2494472 | tf_op jit(solution)/shard_map/ppermute | solution.py:284
  37.3 3.3 %collective-permute-start.12 = (f32[448,256]{1,0:T(8,128)S(1)}, f32[448,256]{1,0:T(8,128)S(1)}, u32[]{:S(2)}, u32[]{:S(2)}) collective-permute-start(f32[448,256]{1,0:T(8,128)S(1)} %collective-permute-done.11.refs_0_.refs_1_), channel_id=1, source_target_pairs={{2,10},{10,18},{12,4},{18,26},{20,12},{28,20},{3,11},{11,19},{13,5... | collective-permute-start | bytes 1376264 | tf_op jit(solution)/shard_map/ppermute | solution.py:35
  38.0 24.5 %collective-permute-start.4 = (f32[448,896]{1,0:T(8,128)}, f32[448,896]{1,0:T(8,128)S(1)}, u32[]{:S(2)}, u32[]{:S(2)}) collective-permute-start(f32[448,896]{1,0:T(8,128)} %bitcast.1), channel_id=1, source_target_pairs={{0,2},{2,0},{4,6},{6,4},{8,10},{10,8},{12,14},{14,12},{16,18},{18,... | collective-permute-start | bytes 4816904 | tf_op jit(solution)/shard_map/ppermute | solution.py:35
  40.5 7.6 %collective-permute-start.16 = (f32[448,128]{1,0:T(8,128)S(1)}, f32[448,128]{1,0:T(8,128)S(1)}, u32[]{:S(2)}, u32[]{:S(2)}) collective-permute-start(f32[448,128]{1,0:T(8,128)S(1)} %get-tuple-element.30), channel_id=1, source_target_pairs={{0,4},{2,6},{4,0},{6,2},{8,12},{10,14},{12,8},{14,10},{16,20},{18,... | collective-permute-start | bytes 688136 | tf_op jit(solution)/shard_map/ppermute | solution.py:35
  40.7 36.5 %collective-permute-start.15 = (f32[448,896]{1,0:T(8,128)S(1)}, f32[448,896]{1,0:T(8,128)S(1)}, u32[]{:S(2)}, u32[]{:S(2)}) collective-permute-start(f32[448,896]{1,0:T(8,128)S(1)} %shard_map.52), channel_id=1, source_target_pairs={{2,0},{4,6},{10,8},{12,14},{18,16},{20,22},{26,24},{28,30},{3,1},{... | collective-permute-start | bytes 4816904 | tf_op jit(solution)/shard_map/ppermute | solution.py:35
  48.1 7.4 %collective-permute-start.18 = (f32[448,512]{1,0:T(8,128)S(1)}, f32[448,512]{1,0:T(8,128)S(1)}, u32[]{:S(2)}, u32[]{:S(2)}) collective-permute-start(f32[448,512]{1,0:T(8,128)S(1)} %shard_map.58), channel_id=1, source_target_pairs={{0,2},{6,4},{8,10},{14,12},{16,18},{22,20},{24,26},{30,28},{1,3},{... | collective-permute-start | bytes 2752520 | tf_op jit(solution)/shard_map/ppermute | solution.py:35
  49.5 5.4 %collective-permute-start.19 = (f32[448,384]{1,0:T(8,128)S(1)}, f32[448,384]{1,0:T(8,128)S(1)}, u32[]{:S(2)}, u32[]{:S(2)}) collective-permute-start(f32[448,384]{1,0:T(8,128)S(1)} %shard_map.54), channel_id=1, source_target_pairs={{0,2},{6,4},{8,10},{14,12},{16,18},{22,20},{24,26},{30,28},{1,3},{... | collective-permute-start | bytes 2064392 | tf_op jit(solution)/shard_map/ppermute | solution.py:35
  54.9 4.0 %collective-permute-start.2 = (f32[224,896]{1,0:T(8,128)S(1)}, f32[224,896]{1,0:T(8,128)S(1)}, u32[]{:S(2)}, u32[]{:S(2)}) collective-permute-start(f32[224,896]{1,0:T(8,128)S(1)} %collective-permute-done.refs_0_), channel_id=1, source_target_pairs={{0,2},{2,0},{4,6},{6,4},{8,10},{10,8},{12,14},{14,12},{16,18},{18,... | collective-permute-start | bytes 2408456 | tf_op jit(solution)/shard_map/ppermute | solution.py:35
  54.9 10.2 %collective-permute-start.3 = (f32[232,896]{1,0:T(8,128)S(1)}, f32[232,896]{1,0:T(8,128)S(1)}, u32[]{:S(2)}, u32[]{:S(2)}) collective-permute-start(f32[232,896]{1,0:T(8,128)S(1)} %collective-permute-done.1.refs_1_.number), channel_id=1, source_target_pairs={{0,2},{2,0},{4,6},{6,4},{8,10},{10,8},{12,14},{14,12},{16,18},{18,... | collective-permute-start | bytes 2494472 | tf_op jit(solution)/shard_map/ppermute | solution.py:35
  55.4 23.0 %collective-permute-start.17 = (f32[448,384]{1,0:T(8,128)S(1)}, f32[448,384]{1,0:T(8,128)S(1)}, u32[]{:S(2)}, u32[]{:S(2)}) collective-permute-start(f32[448,384]{1,0:T(8,128)S(1)} %shard_map.54), channel_id=1, source_target_pairs={{0,8},{8,16},{14,6},{16,24},{22,14},{30,22},{1,9},{9,17},{15,7},{1... | collective-permute-start | bytes 2064392 | tf_op jit(solution)/shard_map/ppermute | solution.py:35
  59.0 13.3 %collective-permute-start.7 = (f32[448,256]{1,0:T(8,128)S(1)}, f32[448,256]{1,0:T(8,128)S(1)}, u32[]{:S(2)}, u32[]{:S(2)}) collective-permute-start(f32[448,256]{1,0:T(8,128)S(1)} %collective-permute-done.5.refs_1_.refs_0_), channel_id=1, source_target_pairs={{0,8},{8,16},{14,6},{16,24},{22,14},{30,22},{1,9},{9,17},{15,7},{1... | collective-permute-start | bytes 1376264 | tf_op jit(solution)/shard_map/ppermute | solution.py:35
  62.4 14.7 %collective-permute-start.8 = (f32[448,256]{1,0:T(8,128)S(1)}, f32[448,256]{1,0:T(8,128)S(1)}, u32[]{:S(2)}, u32[]{:S(2)}) collective-permute-start(f32[448,256]{1,0:T(8,128)S(1)} %collective-permute-done.6.refs_2_.refs_1_), channel_id=1, source_target_pairs={{0,8},{8,16},{14,6},{16,24},{22,14},{30,22},{1,9},{9,17},{15,7},{1... | collective-permute-start | bytes 1376264 | tf_op jit(solution)/shard_map/ppermute | solution.py:35
  65.5 39.3 %collective-permute-start.20 = (f32[448,640]{1,0:T(8,128)S(1)}, f32[448,640]{1,0:T(8,128)S(1)}, u32[]{:S(2)}, u32[]{:S(2)}) collective-permute-start(f32[448,640]{1,0:T(8,128)S(1)} %shard_map.64), channel_id=1, source_target_pairs={{2,3},{3,2},{4,5},{5,4},{10,11},{11,10},{12,13},{13,12},{18,19},{1... | collective-permute-start | bytes 3440648 | tf_op jit(solution)/shard_map/ppermute | solution.py:46
  81.3 23.5 %collective-permute-start.21 = (f32[448,640]{1,0:T(8,128)S(1)}, f32[448,640]{1,0:T(8,128)S(1)}, u32[]{:S(2)}, u32[]{:S(2)}) collective-permute-start(f32[448,640]{1,0:T(8,128)S(1)} %shard_map.65), channel_id=1, source_target_pairs={{0,1},{1,0},{6,7},{7,6},{8,9},{9,8},{14,15},{15,14},{16,17},{17,16... | collective-permute-start | bytes 3440648 | tf_op jit(solution)/shard_map/ppermute | solution.py:46
  84.8 7.0 %collective-permute-start.22 = (f32[448,256]{1,0:T(8,128)S(1)}, f32[448,256]{1,0:T(8,128)S(1)}, u32[]{:S(2)}, u32[]{:S(2)}) collective-permute-start(f32[448,256]{1,0:T(8,128)S(1)} %shard_map.66), channel_id=1, source_target_pairs={{2,3},{3,2},{4,5},{5,4},{10,11},{11,10},{12,13},{13,12},{18,19},{1... | collective-permute-start | bytes 1376264 | tf_op jit(solution)/shard_map/ppermute | solution.py:46
  86.1 17.8 %collective-permute-start.23 = (f32[448,256]{1,0:T(8,128)S(1)}, f32[448,256]{1,0:T(8,128)S(1)}, u32[]{:S(2)}, u32[]{:S(2)}) collective-permute-start(f32[448,256]{1,0:T(8,128)S(1)} %shard_map.67), channel_id=1, source_target_pairs={{0,1},{1,0},{6,7},{7,6},{8,9},{9,8},{14,15},{15,14},{16,17},{17,16... | collective-permute-start | bytes 1376264 | tf_op jit(solution)/shard_map/ppermute | solution.py:46
  (1 other events, 16.2 us)

commit v3 on v0

v3 whole, which is shorter than its diff:
```python
import functools

import jax
import jax.numpy as jnp
from jax import lax
from jax.experimental import pallas as pl
from jax.experimental.pallas import tpu as pltpu
from jax.sharding import PartitionSpec as P


ANY = pl.BlockSpec(memory_space=pl.ANY)
VMEM = pl.BlockSpec(memory_space=pltpu.VMEM)
SMEM = pl.BlockSpec(memory_space=pltpu.SMEM)
LOCAL = pltpu.CompilerParams(vmem_limit_bytes=12 * 2**20)
SWAP = [(0, 1), (1, 0)]
LANES = 128


def tiles_of(columns):
    tiles, first = [], 0
    while first < columns:
        last = min(columns, first + (2 * LANES if columns - first > 3 * LANES else LANES))
        tiles.append((first, last))
        first = last
    return tiles


def is_early(energy):
    return (energy ^ (energy >> 1)) & 1


def partner(energy):
    return energy ^ 1


def across(energy):
    return energy ^ 2


def onward(energy):
    return energy + 4 if energy & 2 == 0 else energy - 4


def detour(energy):
    return energy - 4 if energy & 2 == 0 else energy + 4


def permute_energy(value, target_of, early=None):
    count = lax.axis_size("energy")
    pairs = [(source, target_of(source)) for source in range(count) if early is None or is_early(source) == early]
    return lax.ppermute(value, "energy", [(source, target) for source, target in pairs if 0 <= target < count])


def permute_mode(value, early):
    count, modes = lax.axis_size("energy"), lax.axis_size("mode")
    pairs = [
        (energy * modes + mode, energy * modes + other)
        for energy in range(count)
        if is_early(energy) == early
        for mode, other in SWAP
    ]
    return lax.ppermute(value, ("energy", "mode"), pairs)


def local_call(kernel, outputs, scalars, arrays):
    held = [pltpu.with_memory_space_constraint(each, pltpu.VMEM) for each in arrays]
    return pl.pallas_call(
        kernel,
        out_shape=[pltpu.VMEM(shape, dtype) for shape, dtype in outputs],
        in_specs=[SMEM] * len(scalars) + [VMEM] * len(held),
        out_specs=[VMEM] * len(outputs),
        compiler_params=LOCAL,
    )(*scalars, *held)


def own_mode():
    return lax.axis_index("mode")


def block(index, rows):
    return pl.ds(pl.multiple_of(index * rows, rows), rows)


def cut_kernel(columns, own_ref, *refs):
    pieces, sem = refs[:-1], refs[-1]
    copies = [
        pltpu.make_async_copy(own_ref.at[0, :, first:last], piece, sem.at[index])
        for index, ((first, last), piece) in enumerate(zip(columns, pieces))
    ]
    for copy in copies:
        copy.start()
    for copy in copies:
        copy.wait()


def cut(spectral, columns):
    return pl.pallas_call(
        functools.partial(cut_kernel, columns),
        out_shape=[pltpu.VMEM((spectral.shape[1], last - first), jnp.float32) for first, last in columns],
        in_specs=[ANY],
        out_specs=[VMEM] * len(columns),
        scratch_shapes=[pltpu.SemaphoreType.DMA((len(columns),))],
        compiler_params=LOCAL,
    )(spectral)


def merge_kernel(*refs):
    at = 0
    for piece in refs[:-1]:
        width = piece.shape[1]
        refs[-1][:, at : at + width] = piece[...]
        at += width


def merged(pieces):
    if len(pieces) == 1:
        return pieces[0]
    rows = pieces[0].shape[0]
    return local_call(merge_kernel, [((rows, sum(each.shape[1] for each in pieces)), jnp.float32)], [], pieces)[0]


def widened(matrix_ref, which, part):
    start = 2 * which + (lax.axis_index("energy") & 1)
    return matrix_ref[block(start, part), :].astype(jnp.float32)


def widen_kernel(offset_ref, level_ref, matrix_ref, out_ref):
    orbitals = matrix_ref.shape[0]
    part = orbitals // 4
    out_ref[0:part, :] = widened(matrix_ref, own_mode(), part)
    row = lax.broadcasted_iota(jnp.int32, (out_ref.shape[0] - part, orbitals), 0)
    out_ref[part:, :] = jnp.where(row == 0, offset_ref[0], level_ref[0, 0]).astype(out_ref.dtype)


def widen_more_kernel(matrix_ref, out_ref):
    out_ref[...] = widened(matrix_ref, 1 - own_mode(), out_ref.shape[0])


def take_columns(matrix_ref, out_ref):
    rows = out_ref.shape[1]

    @pl.when(own_mode() == 0)
    def _():
        out_ref[...] = matrix_ref[:, :rows]

    @pl.when(own_mode() != 0)
    def _():
        out_ref[...] = matrix_ref[:, rows:]


def columns_kernel(matrix_ref, near_ref, far_ref):
    rows = near_ref.shape[0]
    take_columns(matrix_ref.at[block(1 - own_mode(), rows), :], near_ref)
    take_columns(matrix_ref.at[block(own_mode(), rows), :], far_ref)


def join_rows(mine_ref, other_ref, out_ref):
    part = out_ref.shape[0] // 2
    core = lax.axis_index("energy") & 1
    out_ref[block(core, part), :] = mine_ref[0:part, :].astype(out_ref.dtype)
    out_ref[block(1 - core, part), :] = other_ref[0:part, :].astype(out_ref.dtype)


def join_kernel(mine_ref, other_ref, out_ref, left_ref):
    join_rows(mine_ref, other_ref, out_ref)
    take_columns(out_ref, left_ref)


def join_more_kernel(near_ref, mine_ref, other_ref, out_ref, left_ref):
    rows = near_ref.shape[0]
    out_ref[block(1 - own_mode(), rows), :] = near_ref[...]
    far = out_ref.at[block(own_mode(), rows), :]
    join_rows(mine_ref, other_ref, far)
    take_columns(far, left_ref)


def piece_view(refs, starts, first, last):
    for ref, start in zip(refs, starts):
        if start <= first and last <= start + ref.shape[1]:
            return ref[:, first - start : last - start]
    raise ValueError((first, last, starts))


def split_sources(refs, layout):
    split, at = [], 0
    for starts in layout:
        split.append((refs[at : at + len(starts)], starts))
        at += len(starts)
    return split


def combine(tiles, split, number, combined):
    energy = lax.axis_index("energy")
    step = 1 - 2 * (energy & 1)
    far = 2 - 4 * ((energy >> 1) & 1)
    told = number.shape[0] - 8
    offset, level = number[told : told + 1, 0:1], number[told + 1 : told + 2, 0:1]

    def weight(distance):
        gap = jnp.abs(distance).astype(jnp.float32)
        below = jnp.where(distance < 0, 1, 0).astype(jnp.float32)
        return jnp.where(offset == gap, level + below, 0.0)

    weights = [weight(distance) for distance in (step, far, -far, -step)]
    for first, last in tiles:
        total = None
        for (pieces, starts), factor in zip(split, weights):
            term = piece_view(pieces, starts, first, last) * factor
            total = term if total is None else total + term
        combined[:, first - tiles[0][0] : last - tiles[0][0]] = total.astype(jnp.bfloat16)


def left_kernel(tiles, layout, early, number, left, *refs):
    out, combined = refs[-2:]

    @pl.when(is_early(lax.axis_index("energy")) == early)
    def _():
        combine(tiles, split_sources(refs, layout), number, combined)
        out[...] = jnp.dot(left[...], combined[...], preferred_element_type=jnp.float32).astype(jnp.bfloat16)


def left_send_kernel(tiles, layout, early, scale, before, own_ref, near_ref, *refs):
    numbers, lefts, refs = refs[:2], refs[2:4], refs[4:]
    done, refs = refs[: 2 * len(before)], refs[2 * len(before) :]
    out_ref, outs, combined = refs[-5], refs[-4:-2], refs[-2:]

    @pl.when(is_early(lax.axis_index("energy")) == early)
    def _():
        pieces = []
        for mode in range(2):
            combine(tiles, split_sources(refs, layout), numbers[mode], combined[mode])
            product = jnp.dot(lefts[mode][...], combined[mode][...], preferred_element_type=jnp.float32)
            product = product.astype(jnp.bfloat16)
            outs[mode][...] = product
            pieces.append([each[...] for each in done[mode * len(before) : (mode + 1) * len(before)]] + [product])
        columns = [*before, (tiles[0][0], tiles[-1][1])]
        out_ref[...] = right_product(send_couplings(0, own_ref, near_ref, out_ref), pieces, columns) * scale


def right_product(couplings, pieces, columns):
    total = None
    for coupling, lefts in zip(couplings, pieces):
        for left, (first, last) in zip(lefts, columns):
            term = lax.dot_general(
                left, coupling[:, first:last], (((1,), (1,)), ((), ())), preferred_element_type=jnp.float32
            )
            total = term if total is None else total + term
    return total


def output_span(mode, index, rows, orbitals):
    whole = rows // LANES * LANES
    if index == 0:
        return mode * (orbitals - whole), whole
    return (1 - mode) * whole, orbitals - whole


def send_couplings(index, own_ref, other_ref, out_ref):
    orbitals, rows = own_ref.shape[0], out_ref.shape[0]
    target = 1 - own_mode()
    start, width = output_span(target, index, rows, orbitals)
    own = own_ref.at[pl.ds(pl.multiple_of(start, LANES), width), :]
    if other_ref.shape[0] == rows:
        start = start - target * rows
    return own, other_ref.at[pl.ds(pl.multiple_of(start, LANES // 2), width), :]


def send_kernel(scale, columns, early, own_ref, other_ref, *refs):
    pieces, out_ref = refs[:-1], refs[-1]
    many = len(columns)

    @pl.when(is_early(lax.axis_index("energy")) == early)
    def _():
        lefts = [[piece[...] for piece in pieces[mode * many : (mode + 1) * many]] for mode in range(2)]
        out_ref[...] = right_product(send_couplings(1, own_ref, other_ref, out_ref), lefts, columns) * scale


def keep_kernel(scale, variants, own_ref, other_ref, *refs):
    lefts, pieces, outs = refs[:2], refs[2:-2], refs[-2:]
    orbitals = own_ref.shape[0]
    at = 0
    for early, columns in variants:
        many = len(columns)
        group = pieces[at : at + 2 * many]
        at += 2 * many

        @pl.when(is_early(lax.axis_index("energy")) == early)
        def _(group=group, many=many, columns=columns):
            held = [
                [
                    jnp.dot(left[...], piece[...], preferred_element_type=jnp.float32).astype(jnp.bfloat16)
                    for piece in group[mode * many : (mode + 1) * many]
                ]
                for mode, left in enumerate(lefts)
            ]
            for index, out_ref in enumerate(outs):
                start, width = output_span(own_mode(), index, out_ref.shape[0], orbitals)
                span = pl.ds(pl.multiple_of(start, LANES), width)
                couplings = (own_ref.at[span, :], other_ref.at[span, :])
                out_ref[...] = right_product(couplings, held, columns) * scale


def finish_kernel(index, *refs):
    kept_ref, early_ref, late_ref = refs[:3]
    out_ref, piece_ref, sem = refs[-3:]
    piece_ref[...] = kept_ref[...] + (early_ref[...] + late_ref[...])
    for mode in range(2):

        @pl.when(own_mode() == mode)
        def _(mode=mode):
            start, width = output_span(mode, index, out_ref.shape[1], out_ref.shape[2])
            copy = pltpu.make_async_copy(piece_ref, out_ref.at[0, :, start : start + width], sem)
            copy.start()
            copy.wait()


def finish(index, result, before, *arrays):
    held = [pltpu.with_memory_space_constraint(each, pltpu.VMEM) for each in arrays]
    return pl.pallas_call(
        functools.partial(finish_kernel, index),
        out_shape=result,
        in_specs=[VMEM] * len(held) + [ANY] * len(before),
        out_specs=ANY,
        scratch_shapes=[pltpu.VMEM(arrays[0].shape, arrays[0].dtype), pltpu.SemaphoreType.DMA],
        input_output_aliases={len(held): 0} if before else {},
        compiler_params=LOCAL,
        name="finish",
    )(*held, *before)


def shards(spectral, coupling, offsets, occupation):
    rows, orbitals = spectral.shape[1:]
    matrix = coupling[0]
    scale = 1.0 / lax.axis_size("mode")
    tiles = tiles_of(orbitals)
    many = len(tiles)
    sides = ((0, many - 2), (many - 2, many))
    seconds = ((0, 1), (1, many))

    own_piece = cut(spectral, tiles[:1])
    across_piece = [permute_energy(own_piece[0], across)]
    own_piece += cut(spectral, tiles[1:])
    for index in range(1, many):
        across_piece.append(permute_energy(own_piece[index], across))

    part = orbitals // 4
    (wide,) = local_call(widen_kernel, [((part + 8, orbitals), jnp.float32)], [offsets, occupation], [matrix])
    (wide_more,) = local_call(widen_more_kernel, [((part, orbitals), jnp.float32)], [], [matrix])
    told = lax.ppermute(wide, "mode", SWAP)
    told_more = lax.ppermute(wide_more, "mode", SWAP)
    swapped = permute_energy(told, partner)
    swapped_more = permute_energy(told_more, partner)
    partner_piece = permute_energy(spectral[0], partner)

    first_piece = []
    for index in range(many - 1):
        first_piece.append(permute_energy(across_piece[index], onward, early=1))
    aside = permute_energy(own_piece[-1], detour, early=0)
    first_piece.append(permute_energy(aside, across, early=0))
    second_piece = []
    for low, high in seconds:
        second_piece.append(permute_energy(merged(across_piece[low:high]), onward, early=0))
    straight_piece = []
    for low, high in sides:
        straight_piece.append(permute_energy(merged(across_piece[low:high]), partner, early=0))
    crossed_piece = permute_energy(merged(first_piece), partner, early=1)

    square, strip = ((rows, rows), matrix.dtype), ((rows, orbitals), matrix.dtype)
    own_near_left, own_far_left = local_call(columns_kernel, [square] * 2, [], [matrix])
    near, near_left = local_call(join_kernel, [strip, square], [], [told, swapped])
    other_matrix, far_left = local_call(
        join_more_kernel, [(matrix.shape, matrix.dtype), square], [], [near, told_more, swapped_more]
    )

    starts = [first for first, last in tiles]
    widths = [output_span(0, index, rows, orbitals)[1] for index in range(2)]
    numbers, near_lefts = (wide, told), (own_near_left, near_left)
    ready, last = sides
    ready_columns, last_columns = [(tiles[low][0], tiles[high - 1][1]) for low, high in sides]

    def width(span):
        return span[1] - span[0]

    def left(which, low, high):
        layout = ([0], starts[low:high], starts[low:high], [starts[low]])
        return local_call(
            functools.partial(left_kernel, tiles[low:high], layout, 1),
            [((rows, width(ready_columns)), jnp.bfloat16)] * 2,
            [],
            [
                numbers[which], near_lefts[which], partner_piece,
                *across_piece[low:high], *first_piece[low:high], straight_piece[0],
            ],
        )

    def left_send(early, low, high, before, done, onward_pieces, onward_starts, back_piece):
        layout = ([0], starts[low:high], onward_starts, [starts[low]])
        wide_columns = tiles[high - 1][1] - tiles[low][0]
        return local_call(
            functools.partial(left_send_kernel, tiles[low:high], layout, early, scale, before),
            [((rows, widths[0]), jnp.float32)] + [((rows, wide_columns), jnp.bfloat16)] * 4,
            [],
            [
                matrix, near, *numbers, *near_lefts, *done, partner_piece,
                *across_piece[low:high], *onward_pieces, back_piece,
            ],
        )

    early_left = [left(which, *ready) for which in range(2)]
    early = left_send(
        1, *last, [ready_columns], [each for each, combined in early_left],
        first_piece[last[0] : last[1]], starts[last[0] : last[1]], straight_piece[1],
    )
    late = left_send(0, 0, many, [], [], second_piece, [starts[low] for low, high in seconds], crossed_piece)
    early_columns, late_columns = [ready_columns, last_columns], [(0, orbitals)]
    early_coupled = [early_left[0][0], early[1], early_left[1][0], early[2]]
    early_combined = [early_left[0][1], early[3], early_left[1][1], early[4]]
    late_coupled, late_combined = late[1:3], late[3:5]

    arrived = []
    for which, first_sent, columns, coupled in (
        (1, early[0], early_columns, early_coupled),
        (0, late[0], late_columns, late_coupled),
    ):
        got = [permute_mode(first_sent, which)]
        (sent,) = local_call(
            functools.partial(send_kernel, scale, columns, which),
            [((rows, widths[1]), jnp.float32)],
            [],
            [matrix, other_matrix, *coupled],
        )
        got.append(permute_mode(sent, which))
        arrived.append(got)
    kept = local_call(
        functools.partial(keep_kernel, scale, ((1, early_columns), (0, late_columns))),
        [((rows, each), jnp.float32) for each in widths],
        [],
        [matrix, other_matrix, own_far_left, far_left, *early_combined, *late_combined],
    )

    shape = jax.ShapeDtypeStruct(spectral.shape, jnp.float32)
    result = []
    for index in range(2):
        result = [finish(index, shape, result, kept[index], arrived[0][index], arrived[1][index])]
    return result[0]


def solution(mesh):
    return jax.shard_map(
        shards,
        mesh=mesh,
        in_specs=(P("energy", "mode", None), P("mode", None, None), P("mode"), P("mode", "energy")),
        out_specs=P("energy", "mode", None),
        check_vma=False,
    )
```

time: 365 us -> 126 us (0.35)
  waiting for transfers between devices: 294 us -> 69.3 us
  matrix products: 42.7 us -> 0 us
  starting transfers between devices: 7.69 us -> 41.9 us
  between operations: 14.8 us -> 1.86 us
  Pallas kernels: 0 us -> 12.3 us
    ppermute x4 -> x25, waiting for transfers between devices: 168 us -> 69.3 us  [the longest x19 30.7 us: permute_energy(): lax.ppermute(value, 'energy', [(source, target) for source, target in pai...]
    reduce_scatter x1 -> x0, waiting for transfers between devices: 75.7 us -> none  [shards(): lax.psum_scatter(partial_sum, 'mode', scatter_dimension=1, tiled=True)]
    all_gather x1 -> x0, waiting for transfers between devices: 50 us -> none  [shards(): full_block = lax.all_gather(spectral, 'mode', axis=1, tiled=True)]
    dot_general x2 -> x0, matrix products: 42.7 us -> none  [the longest x1 35.2 us: shards(): jnp.einsum('mew,wij->meij', weights_table, window, precision=lax.Precisio...]
    ppermute x4 -> x25, starting transfers between devices: 7.65 us -> 41.9 us  [the longest x19 31.8 us: permute_energy(): lax.ppermute(value, 'energy', [(source, target) for source, target in pai...]
    pallas_call x0 -> x20, Pallas kernels: none -> 12.3 us  [the longest x16 7.73 us: local_call(): pl.pallas_call(kernel, out_shape=[pltpu.VMEM(shape, dtype) for shape, dty...]
  transfers between devices with their start and end apart: 6 -> 25, of which waited for: 3 -> 7; matrix products, arithmetic and copies ran while one was open for 0% -> 0% of each run, Pallas kernels for 0% -> 8%
where the time goes in v3:
time: 126 us; the launch traced here: 125 us
  waiting for transfers between devices  69.3 us (55%)
  starting transfers between devices  41.9 us (33%)
  Pallas kernels  12.3 us (10%)
  between operations  1.86 us (1%)
    ppermute x19, starting transfers between devices, permute_energy(): lax.ppermute(value, 'energy', [(source, target) for source, target in pai...  31.8 us
    ppermute x19, waiting for transfers between devices, permute_energy(): lax.ppermute(value, 'energy', [(source, target) for source, target in pai...  30.7 us
    ppermute x4, waiting for transfers between devices, permute_mode(): return lax.ppermute(value, ('energy', 'mode'), pairs)  15.1 us
    ppermute x1, waiting for transfers between devices, shards(): told_more = lax.ppermute(wide_more, 'mode', SWAP)  13.7 us
    ppermute x1, waiting for transfers between devices, shards(): told = lax.ppermute(wide, 'mode', SWAP)  9.81 us
    pallas_call x16, Pallas kernels, local_call(): pl.pallas_call(kernel, out_shape=[pltpu.VMEM(shape, dtype) for shape, dty...  7.73 us
    ppermute x4, starting transfers between devices, permute_mode(): return lax.ppermute(value, ('energy', 'mode'), pairs)  7.27 us
  transfers between devices with their start and end apart: 25, of which 7 were waited for; matrix products, arithmetic and copies ran while one was open for 0% of the time, Pallas kernels for 8%

profile of v3, /device:TPU:0, one launch (start us, length us, event | category | flops | bytes accessed | tf_op | source)
XLA Modules:
  0.0 125.4 jit_solution(13534013193195393826)
XLA Ops:
  0.0 1.4 %shard_map.52 = (f32[448,256]{1,0:T(8,128)S(1)}, f32[448,128]{1,0:T(8,128)S(1)}, f32[448,128]{1,0:T(8,128)S(1)}, f32[448,128]{1,0:T(8,128)S(1)}) custom-call(f32[1,448,896]{2,1,0:T(8,128)} %own_ref.3), custom_call_target="tpu_custom_call" | custom-call | tf_op jit(solution)/shard_map/pallas_call | solution.py:97
  1.4 3.0 %collective-permute-start.6 = (f32[448,256]{1,0:T(8,128)S(1)}, f32[448,256]{1,0:T(8,128)S(1)}, u32[]{:S(2)}, u32[]{:S(2)}) collective-permute-start(f32[448,256]{1,0:T(8,128)S(1)} %get-tuple-element.36), channel_id=1, source_target_pairs={{0,4},{2,6},{4,0},{6,2},{8,12},{10,14},{12,8},{14,10},{16,20},{18,... | collective-permute-start | bytes 1376264 | tf_op jit(solution)/shard_map/ppermute | solution.py:51
  4.5 1.9 %collective-permute-start.12 = (f32[448,128]{1,0:T(8,128)S(1)}, f32[448,128]{1,0:T(8,128)S(1)}, u32[]{:S(2)}, u32[]{:S(2)}) collective-permute-start(f32[448,128]{1,0:T(8,128)S(1)} %get-tuple-element.42), channel_id=1, source_target_pairs={{0,4},{2,6},{4,0},{6,2},{8,12},{10,14},{12,8},{14,10},{16,20},{18,... | collective-permute-start | bytes 688136 | tf_op jit(solution)/shard_map/ppermute | solution.py:51
  6.5 1.3 %collective-permute-start.15 = (f32[448,128]{1,0:T(8,128)S(1)}, f32[448,128]{1,0:T(8,128)S(1)}, u32[]{:S(2)}, u32[]{:S(2)}) collective-permute-start(f32[448,128]{1,0:T(8,128)S(1)} %get-tuple-element.43), channel_id=1, source_target_pairs={{6,14},{8,0},{14,22},{16,8},{22,30},{24,16},{7,15},{9,1},{15,23},{... | collective-permute-start | bytes 688136 | tf_op jit(solution)/shard_map/ppermute | solution.py:51
  8.9 11.9 %collective-permute-done.7.refs_2_.refs_3_.refs_1_.refs_7_ = f32[448,128]{1,0:T(8,128)S(1)} collective-permute-done((f32[448,128]{1,0:T(8,128)S(1)}, f32[448,128]{1,0:T(8,128)S(1)}, u32[]{:S(2)}, u32[]{:S(2)}) %collective-permute-start.7) | collective-permute-done | bytes 229408 | tf_op jit(solution)/shard_map/ppermute | solution.py:51
  20.8 4.9 %collective-permute-done.12.refs_0_.refs_7_.refs_2_.refs_8_ = f32[448,128]{1,0:T(8,128)S(1)} collective-permute-done((f32[448,128]{1,0:T(8,128)S(1)}, f32[448,128]{1,0:T(8,128)S(1)}, u32[]{:S(2)}, u32[]{:S(2)}) %collective-permute-start.12) | collective-permute-done | bytes 229408 | tf_op jit(solution)/shard_map/ppermute | solution.py:51
  27.7 9.7 %collective-permute-start.16 = (f32[448,128]{1,0:T(8,128)S(1)}, f32[448,128]{1,0:T(8,128)S(1)}, u32[]{:S(2)}, u32[]{:S(2)}) collective-permute-start(f32[448,128]{1,0:T(8,128)S(1)} %collective-permute-done.15), channel_id=1, source_target_pairs={{0,4},{6,2},{8,12},{14,10},{16,20},{22,18},{24,28},{30,26},{1,5},{... | collective-permute-start | bytes 688136 | tf_op jit(solution)/shard_map/ppermute | solution.py:51
  38.9 1.6 %collective-permute-start = (f32[232,896]{1,0:T(8,128)S(1)}, f32[232,896]{1,0:T(8,128)S(1)}, u32[]{:S(2)}, u32[]{:S(2)}) collective-permute-start(f32[232,896]{1,0:T(8,128)S(1)} %shard_map.46.number.refs_0_), channel_id=1, source_target_pairs={{0,1},{1,0},{2,3},{3,2},{4,5},{5,4},{6,7},{7,6},{8,9},{9,8},{10,11... | collective-permute-start | bytes 2494472 | tf_op jit(solution)/shard_map/ppermute | solution.py:349
  41.3 1.3 %collective-permute-start.2 = (f32[224,896]{1,0:T(8,128)S(1)}, f32[224,896]{1,0:T(8,128)S(1)}, u32[]{:S(2)}, u32[]{:S(2)}) collective-permute-start(f32[224,896]{1,0:T(8,128)S(1)} %shard_map.48), channel_id=1, source_target_pairs={{0,1},{1,0},{2,3},{3,2},{4,5},{5,4},{6,7},{7,6},{8,9},{9,8},{10,11... | collective-permute-start | bytes 2408456 | tf_op jit(solution)/shard_map/ppermute | solution.py:350
  42.5 2.5 %collective-permute-start.13 = (f32[448,128]{1,0:T(8,128)S(1)}, f32[448,128]{1,0:T(8,128)S(1)}, u32[]{:S(2)}, u32[]{:S(2)}) collective-permute-start(f32[448,128]{1,0:T(8,128)S(1)} %get-tuple-element.43), channel_id=1, source_target_pairs={{0,4},{2,6},{4,0},{6,2},{8,12},{10,14},{12,8},{14,10},{16,20},{18,... | collective-permute-start | bytes 688136 | tf_op jit(solution)/shard_map/ppermute | solution.py:51
  45.1 1.9 %collective-permute-start.11 = (f32[448,640]{1,0:T(8,128)S(1)}, f32[448,640]{1,0:T(8,128)S(1)}, u32[]{:S(2)}, u32[]{:S(2)}) collective-permute-start(f32[448,640]{1,0:T(8,128)S(1)} %shard_map.53), channel_id=1, source_target_pairs={{0,2},{6,4},{8,10},{14,12},{16,18},{22,20},{24,26},{30,28},{1,3},{... | collective-permute-start | bytes 3440648 | tf_op jit(solution)/shard_map/ppermute | solution.py:51
  47.1 2.1 %collective-permute-done.13.refs_1_.refs_8_.refs_3_.refs_9_ = f32[448,128]{1,0:T(8,128)S(1)} collective-permute-done((f32[448,128]{1,0:T(8,128)S(1)}, f32[448,128]{1,0:T(8,128)S(1)}, u32[]{:S(2)}, u32[]{:S(2)}) %collective-permute-start.13) | collective-permute-done | bytes 229408 | tf_op jit(solution)/shard_map/ppermute | solution.py:51
  49.2 1.3 %collective-permute-start.20 = (f32[448,896]{1,0:T(8,128)S(1)}, f32[448,896]{1,0:T(8,128)S(1)}, u32[]{:S(2)}, u32[]{:S(2)}) collective-permute-start(f32[448,896]{1,0:T(8,128)S(1)} %shard_map.59), channel_id=1, source_target_pairs={{2,0},{4,6},{10,8},{12,14},{18,16},{20,22},{26,24},{28,30},{3,1},{... | collective-permute-start | bytes 4816904 | tf_op jit(solution)/shard_map/ppermute | solution.py:51
  50.5 9.8 %collective-permute-done.mine_ref.number.refs_1_ = f32[232,896]{1,0:T(8,128)S(1)} collective-permute-done((f32[232,896]{1,0:T(8,128)S(1)}, f32[232,896]{1,0:T(8,128)S(1)}, u32[]{:S(2)}, u32[]{:S(2)}) %collective-permute-start) | collective-permute-done | bytes 831520 | tf_op jit(solution)/shard_map/ppermute | solution.py:349
  60.4 13.7 %collective-permute-done.2.mine_ref = f32[224,896]{1,0:T(8,128)S(1)} collective-permute-done((f32[224,896]{1,0:T(8,128)S(1)}, f32[224,896]{1,0:T(8,128)S(1)}, u32[]{:S(2)}, u32[]{:S(2)}) %collective-permute-start.2) | collective-permute-done | bytes 802848 | tf_op jit(solution)/shard_map/ppermute | solution.py:350
  74.1 2.2 %collective-permute-start.19 = (f32[448,640]{1,0:T(8,128)S(1)}, f32[448,640]{1,0:T(8,128)S(1)}, u32[]{:S(2)}, u32[]{:S(2)}) collective-permute-start(f32[448,640]{1,0:T(8,128)S(1)} %shard_map.58), channel_id=1, source_target_pairs={{0,8},{8,16},{14,6},{16,24},{22,14},{30,22},{1,9},{9,17},{15,7},{1... | collective-permute-start | bytes 3440648 | tf_op jit(solution)/shard_map/ppermute | solution.py:51
  76.5 2.4 %collective-permute-start.17 = (f32[448,256]{1,0:T(8,128)S(1)}, f32[448,256]{1,0:T(8,128)S(1)}, u32[]{:S(2)}, u32[]{:S(2)}) collective-permute-start(f32[448,256]{1,0:T(8,128)S(1)} %shard_map.56), channel_id=1, source_target_pairs={{0,2},{6,4},{8,10},{14,12},{16,18},{22,20},{24,26},{30,28},{1,3},{... | collective-permute-start | bytes 1376264 | tf_op jit(solution)/shard_map/ppermute | solution.py:51
  78.9 2.6 %collective-permute-start.18 = (f32[448,256]{1,0:T(8,128)S(1)}, f32[448,256]{1,0:T(8,128)S(1)}, u32[]{:S(2)}, u32[]{:S(2)}) collective-permute-start(f32[448,256]{1,0:T(8,128)S(1)} %collective-permute-done.5.refs_0_.refs_1_.refs_5_), channel_id=1, source_target_pairs={{0,8},{8,16},{14,6},{16,24},{22,14},{30,22},{1,9},{9,17},{15,7},{1... | collective-permute-start | bytes 1376264 | tf_op jit(solution)/shard_map/ppermute | solution.py:51
  82.8 11.7 %collective-permute-done.18.refs_10_ = f32[448,256]{1,0:T(8,128)S(1)} collective-permute-done((f32[448,256]{1,0:T(8,128)S(1)}, f32[448,256]{1,0:T(8,128)S(1)}, u32[]{:S(2)}, u32[]{:S(2)}) %collective-permute-start.18) | collective-permute-done | bytes 458784 | tf_op jit(solution)/shard_map/ppermute | solution.py:51
  94.5 2.5 %shard_map.60 = (f32[448,384]{1,0:T(8,128)S(1)}, bf16[448,896]{1,0:T(8,128)(2,1)S(1)}, bf16[448,896]{1,0:T(8,128)(2,1)S(1)}, bf16[448,896]{1,0:T(8,128)(2,1)S(1)}, bf16[448,896]{1,0:T(8,128)(2,1)S(1)}) custom-call(bf16[896,896]{1,0:T(8,128)(2,1)S(1)} %bitcast.7, bf16[448,896]{1,0:T(8,128)(2,1)S(1)} %get-tuple-element.31.near_ref, ...), custom_call_target="tpu_custom_call" | custom-call | tf_op jit(solution)/shard_map/pallas_call | solution.py:67
  98.2 3.4 %collective-permute-start.22 = (f32[448,512]{1,0:T(8,128)S(1)}, f32[448,512]{1,0:T(8,128)S(1)}, u32[]{:S(2)}, u32[]{:S(2)}) collective-permute-start(f32[448,512]{1,0:T(8,128)S(1)} %shard_map.63), channel_id=1, source_target_pairs={{0,1},{1,0},{6,7},{7,6},{8,9},{9,8},{14,15},{15,14},{16,17},{17,16... | collective-permute-start | bytes 2752520 | tf_op jit(solution)/shard_map/ppermute | solution.py:62
  102.4 2.4 %collective-permute-start.24 = (f32[448,384]{1,0:T(8,128)S(1)}, f32[448,384]{1,0:T(8,128)S(1)}, u32[]{:S(2)}, u32[]{:S(2)}) collective-permute-start(f32[448,384]{1,0:T(8,128)S(1)} %get-tuple-element.56), channel_id=1, source_target_pairs={{0,1},{1,0},{6,7},{7,6},{8,9},{9,8},{14,15},{15,14},{16,17},{17,16... | collective-permute-start | bytes 2064392 | tf_op jit(solution)/shard_map/ppermute | solution.py:62
  104.8 3.2 %shard_map.61 = (f32[448,384]{1,0:T(8,128)S(1)}, f32[448,512]{1,0:T(8,128)S(1)}) custom-call(bf16[896,896]{1,0:T(8,128)(2,1)S(1)} %bitcast.9, bf16[896,896]{1,0:T(8,128)(2,1)S(1)} %get-tuple-element.32.other_ref, bf16[448,448]{1,0:T(8,128)(2,1)S(1)} %get-tuple-element.33.refs_0_, bf16[448,448]{1,0:T(8,128)(2,1)S(1)} %get-tuple-element.34.refs_1_, ...), custom_call_target="tpu_custom_call" | custom-call | tf_op jit(solution)/shard_map/pallas_call | solution.py:67
  108.0 15.1 %collective-permute-done.24.refs_2_ = f32[448,384]{1,0:T(8,128)S(1)} collective-permute-done((f32[448,384]{1,0:T(8,128)S(1)}, f32[448,384]{1,0:T(8,128)S(1)}, u32[]{:S(2)}, u32[]{:S(2)}) %collective-permute-start.24) | collective-permute-done | bytes 688160 | tf_op jit(solution)/shard_map/ppermute | solution.py:62
  (48 shorter events, 9.6 us)
Async XLA Ops:
  1.4 25.6 %collective-permute-start.6 = (f32[448,256]{1,0:T(8,128)S(1)}, f32[448,256]{1,0:T(8,128)S(1)}, u32[]{:S(2)}, u32[]{:S(2)}) collective-permute-start(f32[448,256]{1,0:T(8,128)S(1)} %get-tuple-element.36), channel_id=1, source_target_pairs={{0,4},{2,6},{4,0},{6,2},{8,12},{10,14},{12,8},{14,10},{16,20},{18,... | collective-permute-start | bytes 1376264 | tf_op jit(solution)/shard_map/ppermute | solution.py:51
  4.5 16.3 %collective-permute-start.7 = (f32[448,128]{1,0:T(8,128)S(1)}, f32[448,128]{1,0:T(8,128)S(1)}, u32[]{:S(2)}, u32[]{:S(2)}) collective-permute-start(f32[448,128]{1,0:T(8,128)S(1)} %get-tuple-element.37), channel_id=1, source_target_pairs={{0,4},{2,6},{4,0},{6,2},{8,12},{10,14},{12,8},{14,10},{16,20},{18,... | collective-permute-start | bytes 688136 | tf_op jit(solution)/shard_map/ppermute | solution.py:51
  4.5 21.1 %collective-permute-start.12 = (f32[448,128]{1,0:T(8,128)S(1)}, f32[448,128]{1,0:T(8,128)S(1)}, u32[]{:S(2)}, u32[]{:S(2)}) collective-permute-start(f32[448,128]{1,0:T(8,128)S(1)} %get-tuple-element.42), channel_id=1, source_target_pairs={{0,4},{2,6},{4,0},{6,2},{8,12},{10,14},{12,8},{14,10},{16,20},{18,... | collective-permute-start | bytes 688136 | tf_op jit(solution)/shard_map/ppermute | solution.py:51
  6.5 19.8 %collective-permute-start.15 = (f32[448,128]{1,0:T(8,128)S(1)}, f32[448,128]{1,0:T(8,128)S(1)}, u32[]{:S(2)}, u32[]{:S(2)}) collective-permute-start(f32[448,128]{1,0:T(8,128)S(1)} %get-tuple-element.43), channel_id=1, source_target_pairs={{6,14},{8,0},{14,22},{16,8},{22,30},{24,16},{7,15},{9,1},{15,23},{... | collective-permute-start | bytes 688136 | tf_op jit(solution)/shard_map/ppermute | solution.py:51
  8.8 31.7 %collective-permute-start.5 = (f32[448,256]{1,0:T(8,128)S(1)}, f32[448,256]{1,0:T(8,128)S(1)}, u32[]{:S(2)}, u32[]{:S(2)}) collective-permute-start(f32[448,256]{1,0:T(8,128)S(1)} %shard_map.51), channel_id=1, source_target_pairs={{0,4},{2,6},{4,0},{6,2},{8,12},{10,14},{12,8},{14,10},{16,20},{18,... | collective-permute-start | bytes 1376264 | tf_op jit(solution)/shard_map/ppermute | solution.py:51
  20.7 55.6 %collective-permute-start.4 = (f32[448,896]{1,0:T(8,128)}, f32[448,896]{1,0:T(8,128)S(1)}, u32[]{:S(2)}, u32[]{:S(2)}) collective-permute-start(f32[448,896]{1,0:T(8,128)} %bitcast.1), channel_id=1, source_target_pairs={{0,2},{2,0},{4,6},{6,4},{8,10},{10,8},{12,14},{14,12},{16,18},{18,... | collective-permute-start | bytes 4816904 | tf_op jit(solution)/shard_map/ppermute | solution.py:51
  26.3 12.5 %collective-permute-start.14 = (f32[448,128]{1,0:T(8,128)S(1)}, f32[448,128]{1,0:T(8,128)S(1)}, u32[]{:S(2)}, u32[]{:S(2)}) collective-permute-start(f32[448,128]{1,0:T(8,128)S(1)} %collective-permute-done.12.refs_0_.refs_7_.refs_2_.refs_8_), channel_id=1, source_target_pairs={{2,10},{10,18},{12,4},{18,26},{20,12},{28,20},{3,11},{11,19},{13,5... | collective-permute-start | bytes 688136 | tf_op jit(solution)/shard_map/ppermute | solution.py:51
  27.0 15.5 %collective-permute-start.9 = (f32[448,256]{1,0:T(8,128)S(1)}, f32[448,256]{1,0:T(8,128)S(1)}, u32[]{:S(2)}, u32[]{:S(2)}) collective-permute-start(f32[448,256]{1,0:T(8,128)S(1)} %collective-permute-done.6.refs_1_.refs_2_.refs_0_.refs_6_), channel_id=1, source_target_pairs={{2,10},{10,18},{12,4},{18,26},{20,12},{28,20},{3,11},{11,19},{13,5... | collective-permute-start | bytes 1376264 | tf_op jit(solution)/shard_map/ppermute | solution.py:51
  27.7 13.5 %collective-permute-start.16 = (f32[448,128]{1,0:T(8,128)S(1)}, f32[448,128]{1,0:T(8,128)S(1)}, u32[]{:S(2)}, u32[]{:S(2)}) collective-permute-start(f32[448,128]{1,0:T(8,128)S(1)} %collective-permute-done.15), channel_id=1, source_target_pairs={{0,4},{6,2},{8,12},{14,10},{16,20},{22,18},{24,28},{30,26},{1,5},{... | collective-permute-start | bytes 688136 | tf_op jit(solution)/shard_map/ppermute | solution.py:51
  38.9 21.4 %collective-permute-start = (f32[232,896]{1,0:T(8,128)S(1)}, f32[232,896]{1,0:T(8,128)S(1)}, u32[]{:S(2)}, u32[]{:S(2)}) collective-permute-start(f32[232,896]{1,0:T(8,128)S(1)} %shard_map.46.number.refs_0_), channel_id=1, source_target_pairs={{0,1},{1,0},{2,3},{3,2},{4,5},{5,4},{6,7},{7,6},{8,9},{9,8},{10,11... | collective-permute-start | bytes 2494472 | tf_op jit(solution)/shard_map/ppermute | solution.py:349
  40.5 4.6 %collective-permute-start.8 = (f32[448,256]{1,0:T(8,128)S(1)}, f32[448,256]{1,0:T(8,128)S(1)}, u32[]{:S(2)}, u32[]{:S(2)}) collective-permute-start(f32[448,256]{1,0:T(8,128)S(1)} %collective-permute-done.5.refs_0_.refs_1_.refs_5_), channel_id=1, source_target_pairs={{2,10},{10,18},{12,4},{18,26},{20,12},{28,20},{3,11},{11,19},{13,5... | collective-permute-start | bytes 1376264 | tf_op jit(solution)/shard_map/ppermute | solution.py:51
  41.3 32.8 %collective-permute-start.2 = (f32[224,896]{1,0:T(8,128)S(1)}, f32[224,896]{1,0:T(8,128)S(1)}, u32[]{:S(2)}, u32[]{:S(2)}) collective-permute-start(f32[224,896]{1,0:T(8,128)S(1)} %shard_map.48), channel_id=1, source_target_pairs={{0,1},{1,0},{2,3},{3,2},{4,5},{5,4},{6,7},{7,6},{8,9},{9,8},{10,11... | collective-permute-start | bytes 2408456 | tf_op jit(solution)/shard_map/ppermute | solution.py:350
  42.5 6.7 %collective-permute-start.13 = (f32[448,128]{1,0:T(8,128)S(1)}, f32[448,128]{1,0:T(8,128)S(1)}, u32[]{:S(2)}, u32[]{:S(2)}) collective-permute-start(f32[448,128]{1,0:T(8,128)S(1)} %get-tuple-element.43), channel_id=1, source_target_pairs={{0,4},{2,6},{4,0},{6,2},{8,12},{10,14},{12,8},{14,10},{16,20},{18,... | collective-permute-start | bytes 688136 | tf_op jit(solution)/shard_map/ppermute | solution.py:51
  45.1 31.4 %collective-permute-start.11 = (f32[448,640]{1,0:T(8,128)S(1)}, f32[448,640]{1,0:T(8,128)S(1)}, u32[]{:S(2)}, u32[]{:S(2)}) collective-permute-start(f32[448,640]{1,0:T(8,128)S(1)} %shard_map.53), channel_id=1, source_target_pairs={{0,2},{6,4},{8,10},{14,12},{16,18},{22,20},{24,26},{30,28},{1,3},{... | collective-permute-start | bytes 3440648 | tf_op jit(solution)/shard_map/ppermute | solution.py:51
  49.2 45.3 %collective-permute-start.20 = (f32[448,896]{1,0:T(8,128)S(1)}, f32[448,896]{1,0:T(8,128)S(1)}, u32[]{:S(2)}, u32[]{:S(2)}) collective-permute-start(f32[448,896]{1,0:T(8,128)S(1)} %shard_map.59), channel_id=1, source_target_pairs={{2,0},{4,6},{10,8},{12,14},{18,16},{20,22},{26,24},{28,30},{3,1},{... | collective-permute-start | bytes 4816904 | tf_op jit(solution)/shard_map/ppermute | solution.py:51
  60.3 18.6 %collective-permute-start.1 = (f32[232,896]{1,0:T(8,128)S(1)}, f32[232,896]{1,0:T(8,128)S(1)}, u32[]{:S(2)}, u32[]{:S(2)}) collective-permute-start(f32[232,896]{1,0:T(8,128)S(1)} %collective-permute-done.mine_ref.number.refs_1_), channel_id=1, source_target_pairs={{0,2},{2,0},{4,6},{6,4},{8,10},{10,8},{12,14},{14,12},{16,18},{18,... | collective-permute-start | bytes 2494472 | tf_op jit(solution)/shard_map/ppermute | solution.py:51
  74.1 20.4 %collective-permute-start.19 = (f32[448,640]{1,0:T(8,128)S(1)}, f32[448,640]{1,0:T(8,128)S(1)}, u32[]{:S(2)}, u32[]{:S(2)}) collective-permute-start(f32[448,640]{1,0:T(8,128)S(1)} %shard_map.58), channel_id=1, source_target_pairs={{0,8},{8,16},{14,6},{16,24},{22,14},{30,22},{1,9},{9,17},{15,7},{1... | collective-permute-start | bytes 3440648 | tf_op jit(solution)/shard_map/ppermute | solution.py:51
  76.3 5.4 %collective-permute-start.3 = (f32[224,896]{1,0:T(8,128)S(1)}, f32[224,896]{1,0:T(8,128)S(1)}, u32[]{:S(2)}, u32[]{:S(2)}) collective-permute-start(f32[224,896]{1,0:T(8,128)S(1)} %collective-permute-done.2.mine_ref), channel_id=1, source_target_pairs={{0,2},{2,0},{4,6},{6,4},{8,10},{10,8},{12,14},{14,12},{16,18},{18,... | collective-permute-start | bytes 2408456 | tf_op jit(solution)/shard_map/ppermute | solution.py:51
  76.5 5.5 %collective-permute-start.17 = (f32[448,256]{1,0:T(8,128)S(1)}, f32[448,256]{1,0:T(8,128)S(1)}, u32[]{:S(2)}, u32[]{:S(2)}) collective-permute-start(f32[448,256]{1,0:T(8,128)S(1)} %shard_map.56), channel_id=1, source_target_pairs={{0,2},{6,4},{8,10},{14,12},{16,18},{22,20},{24,26},{30,28},{1,3},{... | collective-permute-start | bytes 1376264 | tf_op jit(solution)/shard_map/ppermute | solution.py:51
  78.9 15.6 %collective-permute-start.18 = (f32[448,256]{1,0:T(8,128)S(1)}, f32[448,256]{1,0:T(8,128)S(1)}, u32[]{:S(2)}, u32[]{:S(2)}) collective-permute-start(f32[448,256]{1,0:T(8,128)S(1)} %collective-permute-done.5.refs_0_.refs_1_.refs_5_), channel_id=1, source_target_pairs={{0,8},{8,16},{14,6},{16,24},{22,14},{30,22},{1,9},{9,17},{15,7},{1... | collective-permute-start | bytes 1376264 | tf_op jit(solution)/shard_map/ppermute | solution.py:51
  82.1 42.0 %collective-permute-start.21 = (f32[448,512]{1,0:T(8,128)S(1)}, f32[448,512]{1,0:T(8,128)S(1)}, u32[]{:S(2)}, u32[]{:S(2)}) collective-permute-start(f32[448,512]{1,0:T(8,128)S(1)} %shard_map.62), channel_id=1, source_target_pairs={{2,3},{3,2},{4,5},{5,4},{10,11},{11,10},{12,13},{13,12},{18,19},{1... | collective-permute-start | bytes 2752520 | tf_op jit(solution)/shard_map/ppermute | solution.py:62
  98.2 25.9 %collective-permute-start.22 = (f32[448,512]{1,0:T(8,128)S(1)}, f32[448,512]{1,0:T(8,128)S(1)}, u32[]{:S(2)}, u32[]{:S(2)}) collective-permute-start(f32[448,512]{1,0:T(8,128)S(1)} %shard_map.63), channel_id=1, source_target_pairs={{0,1},{1,0},{6,7},{7,6},{8,9},{9,8},{14,15},{15,14},{16,17},{17,16... | collective-permute-start | bytes 2752520 | tf_op jit(solution)/shard_map/ppermute | solution.py:62
  101.6 6.3 %collective-permute-start.23 = (f32[448,384]{1,0:T(8,128)S(1)}, f32[448,384]{1,0:T(8,128)S(1)}, u32[]{:S(2)}, u32[]{:S(2)}) collective-permute-start(f32[448,384]{1,0:T(8,128)S(1)} %get-tuple-element.55), channel_id=1, source_target_pairs={{2,3},{3,2},{4,5},{5,4},{10,11},{11,10},{12,13},{13,12},{18,19},{1... | collective-permute-start | bytes 2064392 | tf_op jit(solution)/shard_map/ppermute | solution.py:62
  102.4 20.7 %collective-permute-start.24 = (f32[448,384]{1,0:T(8,128)S(1)}, f32[448,384]{1,0:T(8,128)S(1)}, u32[]{:S(2)}, u32[]{:S(2)}) collective-permute-start(f32[448,384]{1,0:T(8,128)S(1)} %get-tuple-element.56), channel_id=1, source_target_pairs={{0,1},{1,0},{6,7},{7,6},{8,9},{9,8},{14,15},{15,14},{16,17},{17,16... | collective-permute-start | bytes 2064392 | tf_op jit(solution)/shard_map/ppermute | solution.py:62
  (2 other events, 40.9 us)

commit v4 on v3

--- a/solution.py
+++ b/solution.py
@@ -219,9 +219,9 @@
         out[...] = jnp.dot(left[...], combined[...], preferred_element_type=jnp.float32).astype(jnp.bfloat16)
 
 
-def left_send_kernel(tiles, layout, early, scale, before, own_ref, near_ref, *refs):
+def left_send_kernel(tiles, layout, early, scale, many, own_ref, near_ref, *refs):
     numbers, lefts, refs = refs[:2], refs[2:4], refs[4:]
-    done, refs = refs[: 2 * len(before)], refs[2 * len(before) :]
+    before, refs = refs[:many], refs[many:]
     out_ref, outs, combined = refs[-5], refs[-4:-2], refs[-2:]
 
     @pl.when(is_early(lax.axis_index("energy")) == early)
@@ -232,9 +232,12 @@
             product = jnp.dot(lefts[mode][...], combined[mode][...], preferred_element_type=jnp.float32)
             product = product.astype(jnp.bfloat16)
             outs[mode][...] = product
-            pieces.append([each[...] for each in done[mode * len(before) : (mode + 1) * len(before)]] + [product])
-        columns = [*before, (tiles[0][0], tiles[-1][1])]
-        out_ref[...] = right_product(send_couplings(0, own_ref, near_ref, out_ref), pieces, columns) * scale
+            pieces.append([product])
+        columns = [(tiles[0][0], tiles[-1][1])]
+        total = right_product(send_couplings(0, own_ref, near_ref, out_ref), pieces, columns) * scale
+        for each in before:
+            total += each[...]
+        out_ref[...] = total
 
 
 def right_product(couplings, pieces, columns):
@@ -265,14 +268,14 @@
     return own, other_ref.at[pl.ds(pl.multiple_of(start, LANES // 2), width), :]
 
 
-def send_kernel(scale, columns, early, own_ref, other_ref, *refs):
+def send_kernel(scale, columns, index, early, own_ref, other_ref, *refs):
     pieces, out_ref = refs[:-1], refs[-1]
     many = len(columns)
 
     @pl.when(is_early(lax.axis_index("energy")) == early)
     def _():
         lefts = [[piece[...] for piece in pieces[mode * many : (mode + 1) * many]] for mode in range(2)]
-        out_ref[...] = right_product(send_couplings(1, own_ref, other_ref, out_ref), lefts, columns) * scale
+        out_ref[...] = right_product(send_couplings(index, own_ref, other_ref, out_ref), lefts, columns) * scale
 
 
 def keep_kernel(scale, variants, own_ref, other_ref, *refs):
@@ -303,15 +306,20 @@
 def finish_kernel(index, *refs):
     kept_ref, early_ref, late_ref = refs[:3]
     out_ref, piece_ref, sem = refs[-3:]
-    piece_ref[...] = kept_ref[...] + (early_ref[...] + late_ref[...])
     for mode in range(2):
 
         @pl.when(own_mode() == mode)
         def _(mode=mode):
             start, width = output_span(mode, index, out_ref.shape[1], out_ref.shape[2])
-            copy = pltpu.make_async_copy(piece_ref, out_ref.at[0, :, start : start + width], sem)
-            copy.start()
-            copy.wait()
+            copies = []
+            for which, at in enumerate(range(0, width, LANES)):
+                span = slice(at, at + LANES)
+                piece_ref[:, span] = kept_ref[:, span] + (early_ref[:, span] + late_ref[:, span])
+                target = out_ref.at[0, :, start + at : start + at + LANES]
+                copies.append(pltpu.make_async_copy(piece_ref.at[:, span], target, sem.at[which]))
+                copies[-1].start()
+            for copy in copies:
+                copy.wait()
 
 
 def finish(index, result, before, *arrays):
@@ -321,7 +329,10 @@
         out_shape=result,
         in_specs=[VMEM] * len(held) + [ANY] * len(before),
         out_specs=ANY,
-        scratch_shapes=[pltpu.VMEM(arrays[0].shape, arrays[0].dtype), pltpu.SemaphoreType.DMA],
+        scratch_shapes=[
+            pltpu.VMEM(arrays[0].shape, arrays[0].dtype),
+            pltpu.SemaphoreType.DMA((arrays[0].shape[1] // LANES,)),
+        ],
         input_output_aliases={len(held): 0} if before else {},
         compiler_params=LOCAL,
         name="finish",
@@ -378,44 +389,60 @@
     ready, last = sides
     ready_columns, last_columns = [(tiles[low][0], tiles[high - 1][1]) for low, high in sides]
 
-    def width(span):
-        return span[1] - span[0]
-
-    def left(which, low, high):
-        layout = ([0], starts[low:high], starts[low:high], [starts[low]])
+    def left(early, which, low, high, onward_pieces, onward_starts, back_piece, back_start):
+        layout = ([0], starts[low:high], onward_starts, [back_start])
         return local_call(
-            functools.partial(left_kernel, tiles[low:high], layout, 1),
-            [((rows, width(ready_columns)), jnp.bfloat16)] * 2,
+            functools.partial(left_kernel, tiles[low:high], layout, early),
+            [((rows, tiles[high - 1][1] - tiles[low][0]), jnp.bfloat16)] * 2,
             [],
             [
                 numbers[which], near_lefts[which], partner_piece,
-                *across_piece[low:high], *first_piece[low:high], straight_piece[0],
+                *across_piece[low:high], *onward_pieces, back_piece,
             ],
         )
 
-    def left_send(early, low, high, before, done, onward_pieces, onward_starts, back_piece):
-        layout = ([0], starts[low:high], onward_starts, [starts[low]])
+    def ahead(early, columns, coupled):
+        return local_call(
+            functools.partial(send_kernel, scale, [columns], 0, early),
+            [((rows, widths[0]), jnp.float32)],
+            [],
+            [matrix, near, *coupled],
+        )
+
+    def left_send(early, low, high, before, onward_pieces, onward_starts, back_piece, back_start):
+        layout = ([0], starts[low:high], onward_starts, [back_start])
         wide_columns = tiles[high - 1][1] - tiles[low][0]
         return local_call(
-            functools.partial(left_send_kernel, tiles[low:high], layout, early, scale, before),
+            functools.partial(left_send_kernel, tiles[low:high], layout, early, scale, len(before)),
             [((rows, widths[0]), jnp.float32)] + [((rows, wide_columns), jnp.bfloat16)] * 4,
             [],
             [
-                matrix, near, *numbers, *near_lefts, *done, partner_piece,
+                matrix, near, *numbers, *near_lefts, *before, partner_piece,
                 *across_piece[low:high], *onward_pieces, back_piece,
             ],
         )
 
-    early_left = [left(which, *ready) for which in range(2)]
+    early_left = [
+        left(1, which, *ready, first_piece[ready[0] : ready[1]], starts[ready[0] : ready[1]], straight_piece[0], 0)
+        for which in range(2)
+    ]
     early = left_send(
-        1, *last, [ready_columns], [each for each, combined in early_left],
-        first_piece[last[0] : last[1]], starts[last[0] : last[1]], straight_piece[1],
-    )
-    late = left_send(0, 0, many, [], [], second_piece, [starts[low] for low, high in seconds], crossed_piece)
-    early_columns, late_columns = [ready_columns, last_columns], [(0, orbitals)]
-    early_coupled = [early_left[0][0], early[1], early_left[1][0], early[2]]
-    early_combined = [early_left[0][1], early[3], early_left[1][1], early[4]]
-    late_coupled, late_combined = late[1:3], late[3:5]
+        1, *last, ahead(1, ready_columns, [each for each, combined in early_left]),
+        first_piece[last[0] : last[1]], starts[last[0] : last[1]], straight_piece[1], starts[last[0]],
+    )
+    late_left = [left(0, which, 0, 1, second_piece[:1], [0], crossed_piece, 0) for which in range(2)]
+    late = left_send(
+        0, 1, many, ahead(0, tiles[0], [each for each, combined in late_left]),
+        second_piece[1:], [starts[low] for low, high in seconds[1:]], crossed_piece, 0,
+    )
+    early_columns, late_columns = [ready_columns, last_columns], [tiles[0], (starts[1], orbitals)]
+    early_coupled, early_combined, late_coupled, late_combined = (
+        [early_left[0][which], early[1 + 2 * which], early_left[1][which], early[2 + 2 * which]]
+        if group == 1
+        else [late_left[0][which], late[1 + 2 * which], late_left[1][which], late[2 + 2 * which]]
+        for group in (1, 0)
+        for which in range(2)
+    )
 
     arrived = []
     for which, first_sent, columns, coupled in (
@@ -424,7 +451,7 @@
     ):
         got = [permute_mode(first_sent, which)]
         (sent,) = local_call(
-            functools.partial(send_kernel, scale, columns, which),
+            functools.partial(send_kernel, scale, columns, 1, which),
             [((rows, widths[1]), jnp.float32)],
             [],
             [matrix, other_matrix, *coupled],

time: 126 us -> 126 us (level)
    pallas_call x16 -> x20, Pallas kernels: 7.73 us -> 8.61 us  [local_call(): pl.pallas_call(kernel, out_shape=[pltpu.VMEM(shape, dtype) for shape, dty...]
where the time goes in v4:
time: 126 us; the launch traced here: 125 us
  waiting for transfers between devices  68.5 us (54%)
  starting transfers between devices  41.9 us (33%)
  Pallas kernels  13 us (10%)
  between operations  1.9 us (2%)
    ppermute x19, starting transfers between devices, permute_energy(): lax.ppermute(value, 'energy', [(source, target) for source, target in pai...  31.8 us
    ppermute x19, waiting for transfers between devices, permute_energy(): lax.ppermute(value, 'energy', [(source, target) for source, target in pai...  30.7 us
    ppermute x4, waiting for transfers between devices, permute_mode(): return lax.ppermute(value, ('energy', 'mode'), pairs)  14.4 us
    ppermute x1, waiting for transfers between devices, shards(): told_more = lax.ppermute(wide_more, 'mode', SWAP)  13.7 us
    ppermute x1, waiting for transfers between devices, shards(): told = lax.ppermute(wide, 'mode', SWAP)  9.81 us
    pallas_call x20, Pallas kernels, local_call(): pl.pallas_call(kernel, out_shape=[pltpu.VMEM(shape, dtype) for shape, dty...  8.61 us
    ppermute x4, starting transfers between devices, permute_mode(): return lax.ppermute(value, ('energy', 'mode'), pairs)  7.27 us
  transfers between devices with their start and end apart: 25, of which 7 were waited for; matrix products, arithmetic and copies ran while one was open for 0% of the time, Pallas kernels for 8%

profile of v4, /device:TPU:0, one launch (start us, length us, event | category | flops | bytes accessed | tf_op | source)
XLA Modules:
  0.0 125.4 jit_solution(8839169240576569468)
XLA Ops:
  0.0 1.4 %shard_map.52 = (f32[448,256]{1,0:T(8,128)S(1)}, f32[448,128]{1,0:T(8,128)S(1)}, f32[448,128]{1,0:T(8,128)S(1)}, f32[448,128]{1,0:T(8,128)S(1)}) custom-call(f32[1,448,896]{2,1,0:T(8,128)} %own_ref.3), custom_call_target="tpu_custom_call" | custom-call | tf_op jit(solution)/shard_map/pallas_call | solution.py:97
  1.4 3.0 %collective-permute-start.6 = (f32[448,256]{1,0:T(8,128)S(1)}, f32[448,256]{1,0:T(8,128)S(1)}, u32[]{:S(2)}, u32[]{:S(2)}) collective-permute-start(f32[448,256]{1,0:T(8,128)S(1)} %get-tuple-element.40), channel_id=1, source_target_pairs={{0,4},{2,6},{4,0},{6,2},{8,12},{10,14},{12,8},{14,10},{16,20},{18,... | collective-permute-start | bytes 1376264 | tf_op jit(solution)/shard_map/ppermute | solution.py:51
  4.5 1.9 %collective-permute-start.12 = (f32[448,128]{1,0:T(8,128)S(1)}, f32[448,128]{1,0:T(8,128)S(1)}, u32[]{:S(2)}, u32[]{:S(2)}) collective-permute-start(f32[448,128]{1,0:T(8,128)S(1)} %get-tuple-element.46), channel_id=1, source_target_pairs={{0,4},{2,6},{4,0},{6,2},{8,12},{10,14},{12,8},{14,10},{16,20},{18,... | collective-permute-start | bytes 688136 | tf_op jit(solution)/shard_map/ppermute | solution.py:51
  6.5 1.3 %collective-permute-start.15 = (f32[448,128]{1,0:T(8,128)S(1)}, f32[448,128]{1,0:T(8,128)S(1)}, u32[]{:S(2)}, u32[]{:S(2)}) collective-permute-start(f32[448,128]{1,0:T(8,128)S(1)} %get-tuple-element.47), channel_id=1, source_target_pairs={{6,14},{8,0},{14,22},{16,8},{22,30},{24,16},{7,15},{9,1},{15,23},{... | collective-permute-start | bytes 688136 | tf_op jit(solution)/shard_map/ppermute | solution.py:51
  8.9 11.9 %collective-permute-done.7.refs_2_.refs_3_.refs_1_.refs_7_ = f32[448,128]{1,0:T(8,128)S(1)} collective-permute-done((f32[448,128]{1,0:T(8,128)S(1)}, f32[448,128]{1,0:T(8,128)S(1)}, u32[]{:S(2)}, u32[]{:S(2)}) %collective-permute-start.7) | collective-permute-done | bytes 229408 | tf_op jit(solution)/shard_map/ppermute | solution.py:51
  20.8 4.9 %collective-permute-done.12.refs_0_.refs_6_.refs_2_.refs_8_ = f32[448,128]{1,0:T(8,128)S(1)} collective-permute-done((f32[448,128]{1,0:T(8,128)S(1)}, f32[448,128]{1,0:T(8,128)S(1)}, u32[]{:S(2)}, u32[]{:S(2)}) %collective-permute-start.12) | collective-permute-done | bytes 229408 | tf_op jit(solution)/shard_map/ppermute | solution.py:51
  27.7 9.7 %collective-permute-start.16 = (f32[448,128]{1,0:T(8,128)S(1)}, f32[448,128]{1,0:T(8,128)S(1)}, u32[]{:S(2)}, u32[]{:S(2)}) collective-permute-start(f32[448,128]{1,0:T(8,128)S(1)} %collective-permute-done.15), channel_id=1, source_target_pairs={{0,4},{6,2},{8,12},{14,10},{16,20},{22,18},{24,28},{30,26},{1,5},{... | collective-permute-start | bytes 688136 | tf_op jit(solution)/shard_map/ppermute | solution.py:51
  38.9 1.6 %collective-permute-start = (f32[232,896]{1,0:T(8,128)S(1)}, f32[232,896]{1,0:T(8,128)S(1)}, u32[]{:S(2)}, u32[]{:S(2)}) collective-permute-start(f32[232,896]{1,0:T(8,128)S(1)} %shard_map.46.number.refs_0_), channel_id=1, source_target_pairs={{0,1},{1,0},{2,3},{3,2},{4,5},{5,4},{6,7},{7,6},{8,9},{9,8},{10,11... | collective-permute-start | bytes 2494472 | tf_op jit(solution)/shard_map/ppermute | solution.py:360
  41.3 1.3 %collective-permute-start.2 = (f32[224,896]{1,0:T(8,128)S(1)}, f32[224,896]{1,0:T(8,128)S(1)}, u32[]{:S(2)}, u32[]{:S(2)}) collective-permute-start(f32[224,896]{1,0:T(8,128)S(1)} %shard_map.48), channel_id=1, source_target_pairs={{0,1},{1,0},{2,3},{3,2},{4,5},{5,4},{6,7},{7,6},{8,9},{9,8},{10,11... | collective-permute-start | bytes 2408456 | tf_op jit(solution)/shard_map/ppermute | solution.py:361
  42.5 2.5 %collective-permute-start.13 = (f32[448,128]{1,0:T(8,128)S(1)}, f32[448,128]{1,0:T(8,128)S(1)}, u32[]{:S(2)}, u32[]{:S(2)}) collective-permute-start(f32[448,128]{1,0:T(8,128)S(1)} %get-tuple-element.47), channel_id=1, source_target_pairs={{0,4},{2,6},{4,0},{6,2},{8,12},{10,14},{12,8},{14,10},{16,20},{18,... | collective-permute-start | bytes 688136 | tf_op jit(solution)/shard_map/ppermute | solution.py:51
  45.1 1.9 %collective-permute-start.11 = (f32[448,640]{1,0:T(8,128)S(1)}, f32[448,640]{1,0:T(8,128)S(1)}, u32[]{:S(2)}, u32[]{:S(2)}) collective-permute-start(f32[448,640]{1,0:T(8,128)S(1)} %shard_map.53), channel_id=1, source_target_pairs={{0,2},{6,4},{8,10},{14,12},{16,18},{22,20},{24,26},{30,28},{1,3},{... | collective-permute-start | bytes 3440648 | tf_op jit(solution)/shard_map/ppermute | solution.py:51
  47.1 2.1 %collective-permute-done.13.refs_1_.refs_7_.refs_3_.refs_9_ = f32[448,128]{1,0:T(8,128)S(1)} collective-permute-done((f32[448,128]{1,0:T(8,128)S(1)}, f32[448,128]{1,0:T(8,128)S(1)}, u32[]{:S(2)}, u32[]{:S(2)}) %collective-permute-start.13) | collective-permute-done | bytes 229408 | tf_op jit(solution)/shard_map/ppermute | solution.py:51
  49.2 1.3 %collective-permute-start.19 = (f32[448,896]{1,0:T(8,128)S(1)}, f32[448,896]{1,0:T(8,128)S(1)}, u32[]{:S(2)}, u32[]{:S(2)}) collective-permute-start(f32[448,896]{1,0:T(8,128)S(1)} %shard_map.59), channel_id=1, source_target_pairs={{2,0},{4,6},{10,8},{12,14},{18,16},{20,22},{26,24},{28,30},{3,1},{... | collective-permute-start | bytes 4816904 | tf_op jit(solution)/shard_map/ppermute | solution.py:51
  50.5 9.8 %collective-permute-done.mine_ref.number.refs_1_ = f32[232,896]{1,0:T(8,128)S(1)} collective-permute-done((f32[232,896]{1,0:T(8,128)S(1)}, f32[232,896]{1,0:T(8,128)S(1)}, u32[]{:S(2)}, u32[]{:S(2)}) %collective-permute-start) | collective-permute-done | bytes 831520 | tf_op jit(solution)/shard_map/ppermute | solution.py:360
  60.4 13.7 %collective-permute-done.2.mine_ref = f32[224,896]{1,0:T(8,128)S(1)} collective-permute-done((f32[224,896]{1,0:T(8,128)S(1)}, f32[224,896]{1,0:T(8,128)S(1)}, u32[]{:S(2)}, u32[]{:S(2)}) %collective-permute-start.2) | collective-permute-done | bytes 802848 | tf_op jit(solution)/shard_map/ppermute | solution.py:361
  74.1 2.2 %collective-permute-start.20 = (f32[448,640]{1,0:T(8,128)S(1)}, f32[448,640]{1,0:T(8,128)S(1)}, u32[]{:S(2)}, u32[]{:S(2)}) collective-permute-start(f32[448,640]{1,0:T(8,128)S(1)} %shard_map.63), channel_id=1, source_target_pairs={{0,8},{8,16},{14,6},{16,24},{22,14},{30,22},{1,9},{9,17},{15,7},{1... | collective-permute-start | bytes 3440648 | tf_op jit(solution)/shard_map/ppermute | solution.py:51
  76.5 2.4 %collective-permute-start.17 = (f32[448,256]{1,0:T(8,128)S(1)}, f32[448,256]{1,0:T(8,128)S(1)}, u32[]{:S(2)}, u32[]{:S(2)}) collective-permute-start(f32[448,256]{1,0:T(8,128)S(1)} %shard_map.57), channel_id=1, source_target_pairs={{0,2},{6,4},{8,10},{14,12},{16,18},{22,20},{24,26},{30,28},{1,3},{... | collective-permute-start | bytes 1376264 | tf_op jit(solution)/shard_map/ppermute | solution.py:51
  78.9 2.6 %collective-permute-start.18 = (f32[448,256]{1,0:T(8,128)S(1)}, f32[448,256]{1,0:T(8,128)S(1)}, u32[]{:S(2)}, u32[]{:S(2)}) collective-permute-start(f32[448,256]{1,0:T(8,128)S(1)} %collective-permute-done.5.refs_0_.refs_1_), channel_id=1, source_target_pairs={{0,8},{8,16},{14,6},{16,24},{22,14},{30,22},{1,9},{9,17},{15,7},{1... | collective-permute-start | bytes 1376264 | tf_op jit(solution)/shard_map/ppermute | solution.py:51
  82.8 11.7 %collective-permute-done.18.refs_2_ = f32[448,256]{1,0:T(8,128)S(1)} collective-permute-done((f32[448,256]{1,0:T(8,128)S(1)}, f32[448,256]{1,0:T(8,128)S(1)}, u32[]{:S(2)}, u32[]{:S(2)}) %collective-permute-start.18) | collective-permute-done | bytes 458784 | tf_op jit(solution)/shard_map/ppermute | solution.py:51
  95.9 2.0 %shard_map.64 = (f32[448,384]{1,0:T(8,128)S(1)}, bf16[448,640]{1,0:T(8,128)(2,1)S(1)}, bf16[448,640]{1,0:T(8,128)(2,1)S(1)}, bf16[448,640]{1,0:T(8,128)(2,1)S(1)}, bf16[448,640]{1,0:T(8,128)(2,1)S(1)}) custom-call(bf16[896,896]{1,0:T(8,128)(2,1)S(1)} %bitcast.9, bf16[448,896]{1,0:T(8,128)(2,1)S(1)} %get-tuple-element.35.near_ref.other_ref, ...), custom_call_target="tpu_custom_call" | custom-call | tf_op jit(solution)/shard_map/pallas_call | solution.py:67
  99.1 3.4 %collective-permute-start.22 = (f32[448,512]{1,0:T(8,128)S(1)}, f32[448,512]{1,0:T(8,128)S(1)}, u32[]{:S(2)}, u32[]{:S(2)}) collective-permute-start(f32[448,512]{1,0:T(8,128)S(1)} %shard_map.67), channel_id=1, source_target_pairs={{0,1},{1,0},{6,7},{7,6},{8,9},{9,8},{14,15},{15,14},{16,17},{17,16... | collective-permute-start | bytes 2752520 | tf_op jit(solution)/shard_map/ppermute | solution.py:62
  103.2 2.4 %collective-permute-start.24 = (f32[448,384]{1,0:T(8,128)S(1)}, f32[448,384]{1,0:T(8,128)S(1)}, u32[]{:S(2)}, u32[]{:S(2)}) collective-permute-start(f32[448,384]{1,0:T(8,128)S(1)} %get-tuple-element.64), channel_id=1, source_target_pairs={{0,1},{1,0},{6,7},{7,6},{8,9},{9,8},{14,15},{15,14},{16,17},{17,16... | collective-permute-start | bytes 2064392 | tf_op jit(solution)/shard_map/ppermute | solution.py:62
  105.7 3.2 %shard_map.65 = (f32[448,384]{1,0:T(8,128)S(1)}, f32[448,512]{1,0:T(8,128)S(1)}) custom-call(bf16[896,896]{1,0:T(8,128)(2,1)S(1)} %bitcast.11, bf16[896,896]{1,0:T(8,128)(2,1)S(1)} %get-tuple-element.36.other_ref, bf16[448,448]{1,0:T(8,128)(2,1)S(1)} %get-tuple-element.37.refs_0_, bf16[448,448]{1,0:T(8,128)(2,1)S(1)} %get-tuple-element.38.refs_1_, ...), custom_call_target="tpu_custom_call" | custom-call | tf_op jit(solution)/shard_map/pallas_call | solution.py:67
  108.9 14.4 %collective-permute-done.24.refs_2_ = f32[448,384]{1,0:T(8,128)S(1)} collective-permute-done((f32[448,384]{1,0:T(8,128)S(1)}, f32[448,384]{1,0:T(8,128)S(1)}, u32[]{:S(2)}, u32[]{:S(2)}) %collective-permute-start.24) | collective-permute-done | bytes 688160 | tf_op jit(solution)/shard_map/ppermute | solution.py:62
  (52 shorter events, 10.8 us)
Async XLA Ops:
  1.4 25.6 %collective-permute-start.6 = (f32[448,256]{1,0:T(8,128)S(1)}, f32[448,256]{1,0:T(8,128)S(1)}, u32[]{:S(2)}, u32[]{:S(2)}) collective-permute-start(f32[448,256]{1,0:T(8,128)S(1)} %get-tuple-element.40), channel_id=1, source_target_pairs={{0,4},{2,6},{4,0},{6,2},{8,12},{10,14},{12,8},{14,10},{16,20},{18,... | collective-permute-start | bytes 1376264 | tf_op jit(solution)/shard_map/ppermute | solution.py:51
  4.5 16.3 %collective-permute-start.7 = (f32[448,128]{1,0:T(8,128)S(1)}, f32[448,128]{1,0:T(8,128)S(1)}, u32[]{:S(2)}, u32[]{:S(2)}) collective-permute-start(f32[448,128]{1,0:T(8,128)S(1)} %get-tuple-element.41), channel_id=1, source_target_pairs={{0,4},{2,6},{4,0},{6,2},{8,12},{10,14},{12,8},{14,10},{16,20},{18,... | collective-permute-start | bytes 688136 | tf_op jit(solution)/shard_map/ppermute | solution.py:51
  4.5 21.1 %collective-permute-start.12 = (f32[448,128]{1,0:T(8,128)S(1)}, f32[448,128]{1,0:T(8,128)S(1)}, u32[]{:S(2)}, u32[]{:S(2)}) collective-permute-start(f32[448,128]{1,0:T(8,128)S(1)} %get-tuple-element.46), channel_id=1, source_target_pairs={{0,4},{2,6},{4,0},{6,2},{8,12},{10,14},{12,8},{14,10},{16,20},{18,... | collective-permute-start | bytes 688136 | tf_op jit(solution)/shard_map/ppermute | solution.py:51
  6.5 19.8 %collective-permute-start.15 = (f32[448,128]{1,0:T(8,128)S(1)}, f32[448,128]{1,0:T(8,128)S(1)}, u32[]{:S(2)}, u32[]{:S(2)}) collective-permute-start(f32[448,128]{1,0:T(8,128)S(1)} %get-tuple-element.47), channel_id=1, source_target_pairs={{6,14},{8,0},{14,22},{16,8},{22,30},{24,16},{7,15},{9,1},{15,23},{... | collective-permute-start | bytes 688136 | tf_op jit(solution)/shard_map/ppermute | solution.py:51
  8.8 31.7 %collective-permute-start.5 = (f32[448,256]{1,0:T(8,128)S(1)}, f32[448,256]{1,0:T(8,128)S(1)}, u32[]{:S(2)}, u32[]{:S(2)}) collective-permute-start(f32[448,256]{1,0:T(8,128)S(1)} %shard_map.51), channel_id=1, source_target_pairs={{0,4},{2,6},{4,0},{6,2},{8,12},{10,14},{12,8},{14,10},{16,20},{18,... | collective-permute-start | bytes 1376264 | tf_op jit(solution)/shard_map/ppermute | solution.py:51
  20.7 55.6 %collective-permute-start.4 = (f32[448,896]{1,0:T(8,128)}, f32[448,896]{1,0:T(8,128)S(1)}, u32[]{:S(2)}, u32[]{:S(2)}) collective-permute-start(f32[448,896]{1,0:T(8,128)} %bitcast.1), channel_id=1, source_target_pairs={{0,2},{2,0},{4,6},{6,4},{8,10},{10,8},{12,14},{14,12},{16,18},{18,... | collective-permute-start | bytes 4816904 | tf_op jit(solution)/shard_map/ppermute | solution.py:51
  26.3 12.5 %collective-permute-start.14 = (f32[448,128]{1,0:T(8,128)S(1)}, f32[448,128]{1,0:T(8,128)S(1)}, u32[]{:S(2)}, u32[]{:S(2)}) collective-permute-start(f32[448,128]{1,0:T(8,128)S(1)} %collective-permute-done.12.refs_0_.refs_6_.refs_2_.refs_8_), channel_id=1, source_target_pairs={{2,10},{10,18},{12,4},{18,26},{20,12},{28,20},{3,11},{11,19},{13,5... | collective-permute-start | bytes 688136 | tf_op jit(solution)/shard_map/ppermute | solution.py:51
  27.0 15.5 %collective-permute-start.9 = (f32[448,256]{1,0:T(8,128)S(1)}, f32[448,256]{1,0:T(8,128)S(1)}, u32[]{:S(2)}, u32[]{:S(2)}) collective-permute-start(f32[448,256]{1,0:T(8,128)S(1)} %collective-permute-done.6.refs_1_.refs_2_.refs_0_.refs_6_), channel_id=1, source_target_pairs={{2,10},{10,18},{12,4},{18,26},{20,12},{28,20},{3,11},{11,19},{13,5... | collective-permute-start | bytes 1376264 | tf_op jit(solution)/shard_map/ppermute | solution.py:51
  27.7 13.5 %collective-permute-start.16 = (f32[448,128]{1,0:T(8,128)S(1)}, f32[448,128]{1,0:T(8,128)S(1)}, u32[]{:S(2)}, u32[]{:S(2)}) collective-permute-start(f32[448,128]{1,0:T(8,128)S(1)} %collective-permute-done.15), channel_id=1, source_target_pairs={{0,4},{6,2},{8,12},{14,10},{16,20},{22,18},{24,28},{30,26},{1,5},{... | collective-permute-start | bytes 688136 | tf_op jit(solution)/shard_map/ppermute | solution.py:51
  38.9 21.4 %collective-permute-start = (f32[232,896]{1,0:T(8,128)S(1)}, f32[232,896]{1,0:T(8,128)S(1)}, u32[]{:S(2)}, u32[]{:S(2)}) collective-permute-start(f32[232,896]{1,0:T(8,128)S(1)} %shard_map.46.number.refs_0_), channel_id=1, source_target_pairs={{0,1},{1,0},{2,3},{3,2},{4,5},{5,4},{6,7},{7,6},{8,9},{9,8},{10,11... | collective-permute-start | bytes 2494472 | tf_op jit(solution)/shard_map/ppermute | solution.py:360
  40.5 4.6 %collective-permute-start.8 = (f32[448,256]{1,0:T(8,128)S(1)}, f32[448,256]{1,0:T(8,128)S(1)}, u32[]{:S(2)}, u32[]{:S(2)}) collective-permute-start(f32[448,256]{1,0:T(8,128)S(1)} %collective-permute-done.5.refs_0_.refs_1_), channel_id=1, source_target_pairs={{2,10},{10,18},{12,4},{18,26},{20,12},{28,20},{3,11},{11,19},{13,5... | collective-permute-start | bytes 1376264 | tf_op jit(solution)/shard_map/ppermute | solution.py:51
  41.3 32.8 %collective-permute-start.2 = (f32[224,896]{1,0:T(8,128)S(1)}, f32[224,896]{1,0:T(8,128)S(1)}, u32[]{:S(2)}, u32[]{:S(2)}) collective-permute-start(f32[224,896]{1,0:T(8,128)S(1)} %shard_map.48), channel_id=1, source_target_pairs={{0,1},{1,0},{2,3},{3,2},{4,5},{5,4},{6,7},{7,6},{8,9},{9,8},{10,11... | collective-permute-start | bytes 2408456 | tf_op jit(solution)/shard_map/ppermute | solution.py:361
  42.5 6.7 %collective-permute-start.13 = (f32[448,128]{1,0:T(8,128)S(1)}, f32[448,128]{1,0:T(8,128)S(1)}, u32[]{:S(2)}, u32[]{:S(2)}) collective-permute-start(f32[448,128]{1,0:T(8,128)S(1)} %get-tuple-element.47), channel_id=1, source_target_pairs={{0,4},{2,6},{4,0},{6,2},{8,12},{10,14},{12,8},{14,10},{16,20},{18,... | collective-permute-start | bytes 688136 | tf_op jit(solution)/shard_map/ppermute | solution.py:51
  45.1 31.4 %collective-permute-start.11 = (f32[448,640]{1,0:T(8,128)S(1)}, f32[448,640]{1,0:T(8,128)S(1)}, u32[]{:S(2)}, u32[]{:S(2)}) collective-permute-start(f32[448,640]{1,0:T(8,128)S(1)} %shard_map.53), channel_id=1, source_target_pairs={{0,2},{6,4},{8,10},{14,12},{16,18},{22,20},{24,26},{30,28},{1,3},{... | collective-permute-start | bytes 3440648 | tf_op jit(solution)/shard_map/ppermute | solution.py:51
  49.2 45.3 %collective-permute-start.19 = (f32[448,896]{1,0:T(8,128)S(1)}, f32[448,896]{1,0:T(8,128)S(1)}, u32[]{:S(2)}, u32[]{:S(2)}) collective-permute-start(f32[448,896]{1,0:T(8,128)S(1)} %shard_map.59), channel_id=1, source_target_pairs={{2,0},{4,6},{10,8},{12,14},{18,16},{20,22},{26,24},{28,30},{3,1},{... | collective-permute-start | bytes 4816904 | tf_op jit(solution)/shard_map/ppermute | solution.py:51
  60.3 18.6 %collective-permute-start.1 = (f32[232,896]{1,0:T(8,128)S(1)}, f32[232,896]{1,0:T(8,128)S(1)}, u32[]{:S(2)}, u32[]{:S(2)}) collective-permute-start(f32[232,896]{1,0:T(8,128)S(1)} %collective-permute-done.mine_ref.number.refs_1_), channel_id=1, source_target_pairs={{0,2},{2,0},{4,6},{6,4},{8,10},{10,8},{12,14},{14,12},{16,18},{18,... | collective-permute-start | bytes 2494472 | tf_op jit(solution)/shard_map/ppermute | solution.py:51
  74.1 21.8 %collective-permute-start.20 = (f32[448,640]{1,0:T(8,128)S(1)}, f32[448,640]{1,0:T(8,128)S(1)}, u32[]{:S(2)}, u32[]{:S(2)}) collective-permute-start(f32[448,640]{1,0:T(8,128)S(1)} %shard_map.63), channel_id=1, source_target_pairs={{0,8},{8,16},{14,6},{16,24},{22,14},{30,22},{1,9},{9,17},{15,7},{1... | collective-permute-start | bytes 3440648 | tf_op jit(solution)/shard_map/ppermute | solution.py:51
  76.3 5.5 %collective-permute-start.3 = (f32[224,896]{1,0:T(8,128)S(1)}, f32[224,896]{1,0:T(8,128)S(1)}, u32[]{:S(2)}, u32[]{:S(2)}) collective-permute-start(f32[224,896]{1,0:T(8,128)S(1)} %collective-permute-done.2.mine_ref), channel_id=1, source_target_pairs={{0,2},{2,0},{4,6},{6,4},{8,10},{10,8},{12,14},{14,12},{16,18},{18,... | collective-permute-start | bytes 2408456 | tf_op jit(solution)/shard_map/ppermute | solution.py:51
  76.5 5.5 %collective-permute-start.17 = (f32[448,256]{1,0:T(8,128)S(1)}, f32[448,256]{1,0:T(8,128)S(1)}, u32[]{:S(2)}, u32[]{:S(2)}) collective-permute-start(f32[448,256]{1,0:T(8,128)S(1)} %shard_map.57), channel_id=1, source_target_pairs={{0,2},{6,4},{8,10},{14,12},{16,18},{22,20},{24,26},{30,28},{1,3},{... | collective-permute-start | bytes 1376264 | tf_op jit(solution)/shard_map/ppermute | solution.py:51
  78.9 15.6 %collective-permute-start.18 = (f32[448,256]{1,0:T(8,128)S(1)}, f32[448,256]{1,0:T(8,128)S(1)}, u32[]{:S(2)}, u32[]{:S(2)}) collective-permute-start(f32[448,256]{1,0:T(8,128)S(1)} %collective-permute-done.5.refs_0_.refs_1_), channel_id=1, source_target_pairs={{0,8},{8,16},{14,6},{16,24},{22,14},{30,22},{1,9},{9,17},{15,7},{1... | collective-permute-start | bytes 1376264 | tf_op jit(solution)/shard_map/ppermute | solution.py:51
  82.1 42.1 %collective-permute-start.21 = (f32[448,512]{1,0:T(8,128)S(1)}, f32[448,512]{1,0:T(8,128)S(1)}, u32[]{:S(2)}, u32[]{:S(2)}) collective-permute-start(f32[448,512]{1,0:T(8,128)S(1)} %shard_map.66), channel_id=1, source_target_pairs={{2,3},{3,2},{4,5},{5,4},{10,11},{11,10},{12,13},{13,12},{18,19},{1... | collective-permute-start | bytes 2752520 | tf_op jit(solution)/shard_map/ppermute | solution.py:62
  99.1 25.1 %collective-permute-start.22 = (f32[448,512]{1,0:T(8,128)S(1)}, f32[448,512]{1,0:T(8,128)S(1)}, u32[]{:S(2)}, u32[]{:S(2)}) collective-permute-start(f32[448,512]{1,0:T(8,128)S(1)} %shard_map.67), channel_id=1, source_target_pairs={{0,1},{1,0},{6,7},{7,6},{8,9},{9,8},{14,15},{15,14},{16,17},{17,16... | collective-permute-start | bytes 2752520 | tf_op jit(solution)/shard_map/ppermute | solution.py:62
  102.5 6.3 %collective-permute-start.23 = (f32[448,384]{1,0:T(8,128)S(1)}, f32[448,384]{1,0:T(8,128)S(1)}, u32[]{:S(2)}, u32[]{:S(2)}) collective-permute-start(f32[448,384]{1,0:T(8,128)S(1)} %get-tuple-element.63), channel_id=1, source_target_pairs={{2,3},{3,2},{4,5},{5,4},{10,11},{11,10},{12,13},{13,12},{18,19},{1... | collective-permute-start | bytes 2064392 | tf_op jit(solution)/shard_map/ppermute | solution.py:62
  103.2 20.0 %collective-permute-start.24 = (f32[448,384]{1,0:T(8,128)S(1)}, f32[448,384]{1,0:T(8,128)S(1)}, u32[]{:S(2)}, u32[]{:S(2)}) collective-permute-start(f32[448,384]{1,0:T(8,128)S(1)} %get-tuple-element.64), channel_id=1, source_target_pairs={{0,1},{1,0},{6,7},{7,6},{8,9},{9,8},{14,15},{15,14},{16,17},{17,16... | collective-permute-start | bytes 2064392 | tf_op jit(solution)/shard_map/ppermute | solution.py:62
  (2 other events, 40.9 us)

commit v5 on v4

--- a/solution.py
+++ b/solution.py
@@ -208,15 +208,6 @@
             term = piece_view(pieces, starts, first, last) * factor
             total = term if total is None else total + term
         combined[:, first - tiles[0][0] : last - tiles[0][0]] = total.astype(jnp.bfloat16)
-
-
-def left_kernel(tiles, layout, early, number, left, *refs):
-    out, combined = refs[-2:]
-
-    @pl.when(is_early(lax.axis_index("energy")) == early)
-    def _():
-        combine(tiles, split_sources(refs, layout), number, combined)
-        out[...] = jnp.dot(left[...], combined[...], preferred_element_type=jnp.float32).astype(jnp.bfloat16)
 
 
 def left_send_kernel(tiles, layout, early, scale, many, own_ref, near_ref, *refs):
@@ -389,26 +380,6 @@
     ready, last = sides
     ready_columns, last_columns = [(tiles[low][0], tiles[high - 1][1]) for low, high in sides]
 
-    def left(early, which, low, high, onward_pieces, onward_starts, back_piece, back_start):
-        layout = ([0], starts[low:high], onward_starts, [back_start])
-        return local_call(
-            functools.partial(left_kernel, tiles[low:high], layout, early),
-            [((rows, tiles[high - 1][1] - tiles[low][0]), jnp.bfloat16)] * 2,
-            [],
-            [
-                numbers[which], near_lefts[which], partner_piece,
-                *across_piece[low:high], *onward_pieces, back_piece,
-            ],
-        )
-
-    def ahead(early, columns, coupled):
-        return local_call(
-            functools.partial(send_kernel, scale, [columns], 0, early),
-            [((rows, widths[0]), jnp.float32)],
-            [],
-            [matrix, near, *coupled],
-        )
-
     def left_send(early, low, high, before, onward_pieces, onward_starts, back_piece, back_start):
         layout = ([0], starts[low:high], onward_starts, [back_start])
         wide_columns = tiles[high - 1][1] - tiles[low][0]
@@ -422,26 +393,23 @@
             ],
         )
 
-    early_left = [
-        left(1, which, *ready, first_piece[ready[0] : ready[1]], starts[ready[0] : ready[1]], straight_piece[0], 0)
-        for which in range(2)
-    ]
+    early_ahead = left_send(
+        1, *ready, [], first_piece[ready[0] : ready[1]], starts[ready[0] : ready[1]], straight_piece[0], 0
+    )
     early = left_send(
-        1, *last, ahead(1, ready_columns, [each for each, combined in early_left]),
+        1, *last, early_ahead[:1],
         first_piece[last[0] : last[1]], starts[last[0] : last[1]], straight_piece[1], starts[last[0]],
     )
-    late_left = [left(0, which, 0, 1, second_piece[:1], [0], crossed_piece, 0) for which in range(2)]
+    late_ahead = left_send(0, 0, 1, [], second_piece[:1], [0], crossed_piece, 0)
     late = left_send(
-        0, 1, many, ahead(0, tiles[0], [each for each, combined in late_left]),
+        0, 1, many, late_ahead[:1],
         second_piece[1:], [starts[low] for low, high in seconds[1:]], crossed_piece, 0,
     )
     early_columns, late_columns = [ready_columns, last_columns], [tiles[0], (starts[1], orbitals)]
     early_coupled, early_combined, late_coupled, late_combined = (
-        [early_left[0][which], early[1 + 2 * which], early_left[1][which], early[2 + 2 * which]]
-        if group == 1
-        else [late_left[0][which], late[1 + 2 * which], late_left[1][which], late[2 + 2 * which]]
-        for group in (1, 0)
-        for which in range(2)
+        [group[at + mode] for mode in range(2) for group in groups]
+        for groups in ((early_ahead, early), (late_ahead, late))
+        for at in (1, 3)
     )
 
     arrived = []

time: 126 us -> 125 us (level)
  waiting for transfers between devices: 68.5 us -> 56.1 us
  starting transfers between devices: 41.9 us -> 53.7 us
    ppermute x19, starting transfers between devices: 31.8 us -> 44.3 us  [permute_energy(): lax.ppermute(value, 'energy', [(source, target) for source, target in pai...]
    ppermute x1, waiting for transfers between devices: 9.81 us -> 0.01 us  [shards(): told = lax.ppermute(wide, 'mode', SWAP)]
    ppermute x19, waiting for transfers between devices: 30.7 us -> 28.8 us  [permute_energy(): lax.ppermute(value, 'energy', [(source, target) for source, target in pai...]
    ppermute x4, waiting for transfers between devices: 14.4 us -> 12.9 us  [permute_mode(): return lax.ppermute(value, ('energy', 'mode'), pairs)]
    pallas_call x20 -> x16, Pallas kernels: 8.61 us -> 8 us  [local_call(): pl.pallas_call(kernel, out_shape=[pltpu.VMEM(shape, dtype) for shape, dty...]
  transfers between devices with their start and end apart: 25 -> 25, of which waited for: 7 -> 6; matrix products, arithmetic and copies ran while one was open for 0% -> 0% of each run, Pallas kernels for 8% -> 8%
where the time goes in v5:
time: 125 us; the launch traced here: 124 us
  waiting for transfers between devices  56.1 us (45%)
  starting transfers between devices  53.7 us (43%)
  Pallas kernels  12.4 us (10%)
  between operations  1.86 us (1%)
    ppermute x19, starting transfers between devices, permute_energy(): lax.ppermute(value, 'energy', [(source, target) for source, target in pai...  44.3 us
    ppermute x19, waiting for transfers between devices, permute_energy(): lax.ppermute(value, 'energy', [(source, target) for source, target in pai...  28.8 us
    ppermute x1, waiting for transfers between devices, shards(): told_more = lax.ppermute(wide_more, 'mode', SWAP)  14.4 us
    ppermute x4, waiting for transfers between devices, permute_mode(): return lax.ppermute(value, ('energy', 'mode'), pairs)  12.9 us
    pallas_call x16, Pallas kernels, local_call(): pl.pallas_call(kernel, out_shape=[pltpu.VMEM(shape, dtype) for shape, dty...  8 us
    ppermute x4, starting transfers between devices, permute_mode(): return lax.ppermute(value, ('energy', 'mode'), pairs)  7.27 us
  transfers between devices with their start and end apart: 25, of which 6 were waited for; matrix products, arithmetic and copies ran while one was open for 0% of the time, Pallas kernels for 8%

profile of v5, /device:TPU:0, one launch (start us, length us, event | category | flops | bytes accessed | tf_op | source)
XLA Modules:
  0.0 124.1 jit_solution(12500900397369827047)
XLA Ops:
  0.0 1.4 %shard_map.52 = (f32[448,256]{1,0:T(8,128)S(1)}, f32[448,128]{1,0:T(8,128)S(1)}, f32[448,128]{1,0:T(8,128)S(1)}, f32[448,128]{1,0:T(8,128)S(1)}) custom-call(f32[1,448,896]{2,1,0:T(8,128)} %own_ref.3), custom_call_target="tpu_custom_call" | custom-call | tf_op jit(solution)/shard_map/pallas_call | solution.py:97
  1.4 3.0 %collective-permute-start.6 = (f32[448,256]{1,0:T(8,128)S(1)}, f32[448,256]{1,0:T(8,128)S(1)}, u32[]{:S(2)}, u32[]{:S(2)}) collective-permute-start(f32[448,256]{1,0:T(8,128)S(1)} %get-tuple-element.43), channel_id=1, source_target_pairs={{0,4},{2,6},{4,0},{6,2},{8,12},{10,14},{12,8},{14,10},{16,20},{18,... | collective-permute-start | bytes 1376264 | tf_op jit(solution)/shard_map/ppermute | solution.py:51
  4.5 1.9 %collective-permute-start.12 = (f32[448,128]{1,0:T(8,128)S(1)}, f32[448,128]{1,0:T(8,128)S(1)}, u32[]{:S(2)}, u32[]{:S(2)}) collective-permute-start(f32[448,128]{1,0:T(8,128)S(1)} %get-tuple-element.47), channel_id=1, source_target_pairs={{0,4},{2,6},{4,0},{6,2},{8,12},{10,14},{12,8},{14,10},{16,20},{18,... | collective-permute-start | bytes 688136 | tf_op jit(solution)/shard_map/ppermute | solution.py:51
  6.5 1.3 %collective-permute-start.15 = (f32[448,128]{1,0:T(8,128)S(1)}, f32[448,128]{1,0:T(8,128)S(1)}, u32[]{:S(2)}, u32[]{:S(2)}) collective-permute-start(f32[448,128]{1,0:T(8,128)S(1)} %get-tuple-element.48), channel_id=1, source_target_pairs={{6,14},{8,0},{14,22},{16,8},{22,30},{24,16},{7,15},{9,1},{15,23},{... | collective-permute-start | bytes 688136 | tf_op jit(solution)/shard_map/ppermute | solution.py:51
  8.8 11.9 %collective-permute-done.7.refs_2_.refs_7_.refs_1_ = f32[448,128]{1,0:T(8,128)S(1)} collective-permute-done((f32[448,128]{1,0:T(8,128)S(1)}, f32[448,128]{1,0:T(8,128)S(1)}, u32[]{:S(2)}, u32[]{:S(2)}) %collective-permute-start.7) | collective-permute-done | bytes 229408 | tf_op jit(solution)/shard_map/ppermute | solution.py:51
  20.7 2.0 %collective-permute-start.5 = (f32[448,256]{1,0:T(8,128)S(1)}, f32[448,256]{1,0:T(8,128)S(1)}, u32[]{:S(2)}, u32[]{:S(2)}) collective-permute-start(f32[448,256]{1,0:T(8,128)S(1)} %shard_map.51), channel_id=1, source_target_pairs={{0,4},{2,6},{4,0},{6,2},{8,12},{10,14},{12,8},{14,10},{16,20},{18,... | collective-permute-start | bytes 1376264 | tf_op jit(solution)/shard_map/ppermute | solution.py:51
  22.8 2.9 %collective-permute-done.12.refs_0_.refs_6_.refs_2_.refs_8_ = f32[448,128]{1,0:T(8,128)S(1)} collective-permute-done((f32[448,128]{1,0:T(8,128)S(1)}, f32[448,128]{1,0:T(8,128)S(1)}, u32[]{:S(2)}, u32[]{:S(2)}) %collective-permute-start.12) | collective-permute-done | bytes 229408 | tf_op jit(solution)/shard_map/ppermute | solution.py:51
  27.0 5.2 %collective-permute-start.16 = (f32[448,128]{1,0:T(8,128)S(1)}, f32[448,128]{1,0:T(8,128)S(1)}, u32[]{:S(2)}, u32[]{:S(2)}) collective-permute-start(f32[448,128]{1,0:T(8,128)S(1)} %collective-permute-done.15), channel_id=1, source_target_pairs={{0,4},{6,2},{8,12},{14,10},{16,20},{22,18},{24,28},{30,26},{1,5},{... | collective-permute-start | bytes 688136 | tf_op jit(solution)/shard_map/ppermute | solution.py:51
  33.6 1.6 %collective-permute-start = (f32[232,896]{1,0:T(8,128)S(1)}, f32[232,896]{1,0:T(8,128)S(1)}, u32[]{:S(2)}, u32[]{:S(2)}) collective-permute-start(f32[232,896]{1,0:T(8,128)S(1)} %shard_map.46.refs_0_), channel_id=1, source_target_pairs={{0,1},{1,0},{2,3},{3,2},{4,5},{5,4},{6,7},{7,6},{8,9},{9,8},{10,11... | collective-permute-start | bytes 2494472 | tf_op jit(solution)/shard_map/ppermute | solution.py:351
  37.9 1.3 %collective-permute-start.19 = (f32[448,896]{1,0:T(8,128)S(1)}, f32[448,896]{1,0:T(8,128)S(1)}, u32[]{:S(2)}, u32[]{:S(2)}) collective-permute-start(f32[448,896]{1,0:T(8,128)S(1)} %shard_map.57), channel_id=1, source_target_pairs={{2,0},{4,6},{10,8},{12,14},{18,16},{20,22},{26,24},{28,30},{3,1},{... | collective-permute-start | bytes 4816904 | tf_op jit(solution)/shard_map/ppermute | solution.py:51
  39.2 17.2 %collective-permute-start.13 = (f32[448,128]{1,0:T(8,128)S(1)}, f32[448,128]{1,0:T(8,128)S(1)}, u32[]{:S(2)}, u32[]{:S(2)}) collective-permute-start(f32[448,128]{1,0:T(8,128)S(1)} %get-tuple-element.48), channel_id=1, source_target_pairs={{0,4},{2,6},{4,0},{6,2},{8,12},{10,14},{12,8},{14,10},{16,20},{18,... | collective-permute-start | bytes 688136 | tf_op jit(solution)/shard_map/ppermute | solution.py:51
  56.4 14.4 %collective-permute-done.2.mine_ref = f32[224,896]{1,0:T(8,128)S(1)} collective-permute-done((f32[224,896]{1,0:T(8,128)S(1)}, f32[224,896]{1,0:T(8,128)S(1)}, u32[]{:S(2)}, u32[]{:S(2)}) %collective-permute-start.2) | collective-permute-done | bytes 802848 | tf_op jit(solution)/shard_map/ppermute | solution.py:352
  71.0 2.5 %collective-permute-start.11 = (f32[448,640]{1,0:T(8,128)S(1)}, f32[448,640]{1,0:T(8,128)S(1)}, u32[]{:S(2)}, u32[]{:S(2)}) collective-permute-start(f32[448,640]{1,0:T(8,128)S(1)} %shard_map.53), channel_id=1, source_target_pairs={{0,2},{6,4},{8,10},{14,12},{16,18},{22,20},{24,26},{30,28},{1,3},{... | collective-permute-start | bytes 3440648 | tf_op jit(solution)/shard_map/ppermute | solution.py:51
  73.5 3.5 %collective-permute-start.20 = (f32[448,640]{1,0:T(8,128)S(1)}, f32[448,640]{1,0:T(8,128)S(1)}, u32[]{:S(2)}, u32[]{:S(2)}) collective-permute-start(f32[448,640]{1,0:T(8,128)S(1)} %shard_map.59), channel_id=1, source_target_pairs={{0,8},{8,16},{14,6},{16,24},{22,14},{30,22},{1,9},{9,17},{15,7},{1... | collective-permute-start | bytes 3440648 | tf_op jit(solution)/shard_map/ppermute | solution.py:51
  77.1 1.3 %collective-permute-start.17 = (f32[448,256]{1,0:T(8,128)S(1)}, f32[448,256]{1,0:T(8,128)S(1)}, u32[]{:S(2)}, u32[]{:S(2)}) collective-permute-start(f32[448,256]{1,0:T(8,128)S(1)} %shard_map.55), channel_id=1, source_target_pairs={{0,2},{6,4},{8,10},{14,12},{16,18},{22,20},{24,26},{30,28},{1,3},{... | collective-permute-start | bytes 1376264 | tf_op jit(solution)/shard_map/ppermute | solution.py:51
  78.5 2.2 %collective-permute-start.18 = (f32[448,256]{1,0:T(8,128)S(1)}, f32[448,256]{1,0:T(8,128)S(1)}, u32[]{:S(2)}, u32[]{:S(2)}) collective-permute-start(f32[448,256]{1,0:T(8,128)S(1)} %collective-permute-done.5.refs_0_.refs_5_), channel_id=1, source_target_pairs={{0,8},{8,16},{14,6},{16,24},{22,14},{30,22},{1,9},{9,17},{15,7},{1... | collective-permute-start | bytes 1376264 | tf_op jit(solution)/shard_map/ppermute | solution.py:51
  81.9 13.4 %collective-permute-done.18.refs_6_ = f32[448,256]{1,0:T(8,128)S(1)} collective-permute-done((f32[448,256]{1,0:T(8,128)S(1)}, f32[448,256]{1,0:T(8,128)S(1)}, u32[]{:S(2)}, u32[]{:S(2)}) %collective-permute-start.18) | collective-permute-done | bytes 458784 | tf_op jit(solution)/shard_map/ppermute | solution.py:51
  96.1 1.9 %shard_map.60 = (f32[448,384]{1,0:T(8,128)S(1)}, bf16[448,640]{1,0:T(8,128)(2,1)S(1)}, bf16[448,640]{1,0:T(8,128)(2,1)S(1)}, bf16[448,640]{1,0:T(8,128)(2,1)S(1)}, bf16[448,640]{1,0:T(8,128)(2,1)S(1)}) custom-call(bf16[896,896]{1,0:T(8,128)(2,1)S(1)} %bitcast.9, bf16[448,896]{1,0:T(8,128)(2,1)S(1)} %get-tuple-element.37.near_ref, ...), custom_call_target="tpu_custom_call" | custom-call | tf_op jit(solution)/shard_map/pallas_call | solution.py:67
  98.1 1.2 shard_map.63
  99.3 3.4 %collective-permute-start.22 = (f32[448,512]{1,0:T(8,128)S(1)}, f32[448,512]{1,0:T(8,128)S(1)}, u32[]{:S(2)}, u32[]{:S(2)}) collective-permute-start(f32[448,512]{1,0:T(8,128)S(1)} %shard_map.63), channel_id=1, source_target_pairs={{0,1},{1,0},{6,7},{7,6},{8,9},{9,8},{14,15},{15,14},{16,17},{17,16... | collective-permute-start | bytes 2752520 | tf_op jit(solution)/shard_map/ppermute | solution.py:62
  103.4 2.4 %collective-permute-start.24 = (f32[448,384]{1,0:T(8,128)S(1)}, f32[448,384]{1,0:T(8,128)S(1)}, u32[]{:S(2)}, u32[]{:S(2)}) collective-permute-start(f32[448,384]{1,0:T(8,128)S(1)} %get-tuple-element.68), channel_id=1, source_target_pairs={{0,1},{1,0},{6,7},{7,6},{8,9},{9,8},{14,15},{15,14},{16,17},{17,16... | collective-permute-start | bytes 2064392 | tf_op jit(solution)/shard_map/ppermute | solution.py:62
  105.8 3.2 %shard_map.61 = (f32[448,384]{1,0:T(8,128)S(1)}, f32[448,512]{1,0:T(8,128)S(1)}) custom-call(bf16[896,896]{1,0:T(8,128)(2,1)S(1)} %bitcast.11, bf16[896,896]{1,0:T(8,128)(2,1)S(1)} %get-tuple-element.38.other_ref, bf16[448,448]{1,0:T(8,128)(2,1)S(1)} %get-tuple-element.39.refs_0_, bf16[448,448]{1,0:T(8,128)(2,1)S(1)} %get-tuple-element.40.refs_1_, ...), custom_call_target="tpu_custom_call" | custom-call | tf_op jit(solution)/shard_map/pallas_call | solution.py:67
  109.0 12.9 %collective-permute-done.24.refs_2_ = f32[448,384]{1,0:T(8,128)S(1)} collective-permute-done((f32[448,384]{1,0:T(8,128)S(1)}, f32[448,384]{1,0:T(8,128)S(1)}, u32[]{:S(2)}, u32[]{:S(2)}) %collective-permute-start.24) | collective-permute-done | bytes 688160 | tf_op jit(solution)/shard_map/ppermute | solution.py:62
  122.9 1.1 finish.3
  (48 shorter events, 9.0 us)
Async XLA Ops:
  1.4 25.6 %collective-permute-start.6 = (f32[448,256]{1,0:T(8,128)S(1)}, f32[448,256]{1,0:T(8,128)S(1)}, u32[]{:S(2)}, u32[]{:S(2)}) collective-permute-start(f32[448,256]{1,0:T(8,128)S(1)} %get-tuple-element.43), channel_id=1, source_target_pairs={{0,4},{2,6},{4,0},{6,2},{8,12},{10,14},{12,8},{14,10},{16,20},{18,... | collective-permute-start | bytes 1376264 | tf_op jit(solution)/shard_map/ppermute | solution.py:51
  4.5 16.3 %collective-permute-start.7 = (f32[448,128]{1,0:T(8,128)S(1)}, f32[448,128]{1,0:T(8,128)S(1)}, u32[]{:S(2)}, u32[]{:S(2)}) collective-permute-start(f32[448,128]{1,0:T(8,128)S(1)} %get-tuple-element.44), channel_id=1, source_target_pairs={{0,4},{2,6},{4,0},{6,2},{8,12},{10,14},{12,8},{14,10},{16,20},{18,... | collective-permute-start | bytes 688136 | tf_op jit(solution)/shard_map/ppermute | solution.py:51
  4.5 69.0 %collective-permute-start.4 = (f32[448,896]{1,0:T(8,128)}, f32[448,896]{1,0:T(8,128)S(1)}, u32[]{:S(2)}, u32[]{:S(2)}) collective-permute-start(f32[448,896]{1,0:T(8,128)} %bitcast.1), channel_id=1, source_target_pairs={{0,2},{2,0},{4,6},{6,4},{8,10},{10,8},{12,14},{14,12},{16,18},{18,... | collective-permute-start | bytes 4816904 | tf_op jit(solution)/shard_map/ppermute | solution.py:51
  4.5 21.1 %collective-permute-start.12 = (f32[448,128]{1,0:T(8,128)S(1)}, f32[448,128]{1,0:T(8,128)S(1)}, u32[]{:S(2)}, u32[]{:S(2)}) collective-permute-start(f32[448,128]{1,0:T(8,128)S(1)} %get-tuple-element.47), channel_id=1, source_target_pairs={{0,4},{2,6},{4,0},{6,2},{8,12},{10,14},{12,8},{14,10},{16,20},{18,... | collective-permute-start | bytes 688136 | tf_op jit(solution)/shard_map/ppermute | solution.py:51
  6.5 19.8 %collective-permute-start.15 = (f32[448,128]{1,0:T(8,128)S(1)}, f32[448,128]{1,0:T(8,128)S(1)}, u32[]{:S(2)}, u32[]{:S(2)}) collective-permute-start(f32[448,128]{1,0:T(8,128)S(1)} %get-tuple-element.48), channel_id=1, source_target_pairs={{6,14},{8,0},{14,22},{16,8},{22,30},{24,16},{7,15},{9,1},{15,23},{... | collective-permute-start | bytes 688136 | tf_op jit(solution)/shard_map/ppermute | solution.py:51
  20.7 16.3 %collective-permute-start.5 = (f32[448,256]{1,0:T(8,128)S(1)}, f32[448,256]{1,0:T(8,128)S(1)}, u32[]{:S(2)}, u32[]{:S(2)}) collective-permute-start(f32[448,256]{1,0:T(8,128)S(1)} %shard_map.51), channel_id=1, source_target_pairs={{0,4},{2,6},{4,0},{6,2},{8,12},{10,14},{12,8},{14,10},{16,20},{18,... | collective-permute-start | bytes 1376264 | tf_op jit(solution)/shard_map/ppermute | solution.py:51
  25.7 7.9 %collective-permute-start.10 = (f32[448,128]{1,0:T(8,128)S(1)}, f32[448,128]{1,0:T(8,128)S(1)}, u32[]{:S(2)}, u32[]{:S(2)}) collective-permute-start(f32[448,128]{1,0:T(8,128)S(1)} %collective-permute-done.7.refs_2_.refs_7_.refs_1_), channel_id=1, source_target_pairs={{2,10},{10,18},{12,4},{18,26},{20,12},{28,20},{3,11},{11,19},{13,5... | collective-permute-start | bytes 688136 | tf_op jit(solution)/shard_map/ppermute | solution.py:51
  26.3 8.9 %collective-permute-start.14 = (f32[448,128]{1,0:T(8,128)S(1)}, f32[448,128]{1,0:T(8,128)S(1)}, u32[]{:S(2)}, u32[]{:S(2)}) collective-permute-start(f32[448,128]{1,0:T(8,128)S(1)} %collective-permute-done.12.refs_0_.refs_6_.refs_2_.refs_8_), channel_id=1, source_target_pairs={{2,10},{10,18},{12,4},{18,26},{20,12},{28,20},{3,11},{11,19},{13,5... | collective-permute-start | bytes 688136 | tf_op jit(solution)/shard_map/ppermute | solution.py:51
  27.0 9.3 %collective-permute-start.16 = (f32[448,128]{1,0:T(8,128)S(1)}, f32[448,128]{1,0:T(8,128)S(1)}, u32[]{:S(2)}, u32[]{:S(2)}) collective-permute-start(f32[448,128]{1,0:T(8,128)S(1)} %collective-permute-done.15), channel_id=1, source_target_pairs={{0,4},{6,2},{8,12},{14,10},{16,20},{22,18},{24,28},{30,26},{1,5},{... | collective-permute-start | bytes 688136 | tf_op jit(solution)/shard_map/ppermute | solution.py:51
  33.6 22.8 %collective-permute-start = (f32[232,896]{1,0:T(8,128)S(1)}, f32[232,896]{1,0:T(8,128)S(1)}, u32[]{:S(2)}, u32[]{:S(2)}) collective-permute-start(f32[232,896]{1,0:T(8,128)S(1)} %shard_map.46.refs_0_), channel_id=1, source_target_pairs={{0,1},{1,0},{2,3},{3,2},{4,5},{5,4},{6,7},{7,6},{8,9},{9,8},{10,11... | collective-permute-start | bytes 2494472 | tf_op jit(solution)/shard_map/ppermute | solution.py:351
  35.3 35.6 %collective-permute-start.2 = (f32[224,896]{1,0:T(8,128)S(1)}, f32[224,896]{1,0:T(8,128)S(1)}, u32[]{:S(2)}, u32[]{:S(2)}) collective-permute-start(f32[224,896]{1,0:T(8,128)S(1)} %shard_map.48), channel_id=1, source_target_pairs={{0,1},{1,0},{2,3},{3,2},{4,5},{5,4},{6,7},{7,6},{8,9},{9,8},{10,11... | collective-permute-start | bytes 2408456 | tf_op jit(solution)/shard_map/ppermute | solution.py:352
  36.4 1.4 %collective-permute-start.9 = (f32[448,256]{1,0:T(8,128)S(1)}, f32[448,256]{1,0:T(8,128)S(1)}, u32[]{:S(2)}, u32[]{:S(2)}) collective-permute-start(f32[448,256]{1,0:T(8,128)S(1)} %collective-permute-done.6.refs_1_.refs_6_.refs_0_), channel_id=1, source_target_pairs={{2,10},{10,18},{12,4},{18,26},{20,12},{28,20},{3,11},{11,19},{13,5... | collective-permute-start | bytes 1376264 | tf_op jit(solution)/shard_map/ppermute | solution.py:51
  37.9 57.4 %collective-permute-start.19 = (f32[448,896]{1,0:T(8,128)S(1)}, f32[448,896]{1,0:T(8,128)S(1)}, u32[]{:S(2)}, u32[]{:S(2)}) collective-permute-start(f32[448,896]{1,0:T(8,128)S(1)} %shard_map.57), channel_id=1, source_target_pairs={{2,0},{4,6},{10,8},{12,14},{18,16},{20,22},{26,24},{28,30},{3,1},{... | collective-permute-start | bytes 4816904 | tf_op jit(solution)/shard_map/ppermute | solution.py:51
  39.2 31.8 %collective-permute-start.13 = (f32[448,128]{1,0:T(8,128)S(1)}, f32[448,128]{1,0:T(8,128)S(1)}, u32[]{:S(2)}, u32[]{:S(2)}) collective-permute-start(f32[448,128]{1,0:T(8,128)S(1)} %get-tuple-element.48), channel_id=1, source_target_pairs={{0,4},{2,6},{4,0},{6,2},{8,12},{10,14},{12,8},{14,10},{16,20},{18,... | collective-permute-start | bytes 688136 | tf_op jit(solution)/shard_map/ppermute | solution.py:51
  56.4 22.0 %collective-permute-start.1 = (f32[232,896]{1,0:T(8,128)S(1)}, f32[232,896]{1,0:T(8,128)S(1)}, u32[]{:S(2)}, u32[]{:S(2)}) collective-permute-start(f32[232,896]{1,0:T(8,128)S(1)} %collective-permute-done.mine_ref.refs_1_), channel_id=1, source_target_pairs={{0,2},{2,0},{4,6},{6,4},{8,10},{10,8},{12,14},{14,12},{16,18},{18,... | collective-permute-start | bytes 2494472 | tf_op jit(solution)/shard_map/ppermute | solution.py:51
  70.9 6.3 %collective-permute-start.3 = (f32[224,896]{1,0:T(8,128)S(1)}, f32[224,896]{1,0:T(8,128)S(1)}, u32[]{:S(2)}, u32[]{:S(2)}) collective-permute-start(f32[224,896]{1,0:T(8,128)S(1)} %collective-permute-done.2.mine_ref), channel_id=1, source_target_pairs={{0,2},{2,0},{4,6},{6,4},{8,10},{10,8},{12,14},{14,12},{16,18},{18,... | collective-permute-start | bytes 2408456 | tf_op jit(solution)/shard_map/ppermute | solution.py:51
  71.0 10.1 %collective-permute-start.11 = (f32[448,640]{1,0:T(8,128)S(1)}, f32[448,640]{1,0:T(8,128)S(1)}, u32[]{:S(2)}, u32[]{:S(2)}) collective-permute-start(f32[448,640]{1,0:T(8,128)S(1)} %shard_map.53), channel_id=1, source_target_pairs={{0,2},{6,4},{8,10},{14,12},{16,18},{22,20},{24,26},{30,28},{1,3},{... | collective-permute-start | bytes 3440648 | tf_op jit(solution)/shard_map/ppermute | solution.py:51
  73.5 22.6 %collective-permute-start.20 = (f32[448,640]{1,0:T(8,128)S(1)}, f32[448,640]{1,0:T(8,128)S(1)}, u32[]{:S(2)}, u32[]{:S(2)}) collective-permute-start(f32[448,640]{1,0:T(8,128)S(1)} %shard_map.59), channel_id=1, source_target_pairs={{0,8},{8,16},{14,6},{16,24},{22,14},{30,22},{1,9},{9,17},{15,7},{1... | collective-permute-start | bytes 3440648 | tf_op jit(solution)/shard_map/ppermute | solution.py:51
  77.1 4.0 %collective-permute-start.17 = (f32[448,256]{1,0:T(8,128)S(1)}, f32[448,256]{1,0:T(8,128)S(1)}, u32[]{:S(2)}, u32[]{:S(2)}) collective-permute-start(f32[448,256]{1,0:T(8,128)S(1)} %shard_map.55), channel_id=1, source_target_pairs={{0,2},{6,4},{8,10},{14,12},{16,18},{22,20},{24,26},{30,28},{1,3},{... | collective-permute-start | bytes 1376264 | tf_op jit(solution)/shard_map/ppermute | solution.py:51
  78.5 16.8 %collective-permute-start.18 = (f32[448,256]{1,0:T(8,128)S(1)}, f32[448,256]{1,0:T(8,128)S(1)}, u32[]{:S(2)}, u32[]{:S(2)}) collective-permute-start(f32[448,256]{1,0:T(8,128)S(1)} %collective-permute-done.5.refs_0_.refs_5_), channel_id=1, source_target_pairs={{0,8},{8,16},{14,6},{16,24},{22,14},{30,22},{1,9},{9,17},{15,7},{1... | collective-permute-start | bytes 1376264 | tf_op jit(solution)/shard_map/ppermute | solution.py:51
  81.2 41.7 %collective-permute-start.21 = (f32[448,512]{1,0:T(8,128)S(1)}, f32[448,512]{1,0:T(8,128)S(1)}, u32[]{:S(2)}, u32[]{:S(2)}) collective-permute-start(f32[448,512]{1,0:T(8,128)S(1)} %shard_map.62), channel_id=1, source_target_pairs={{2,3},{3,2},{4,5},{5,4},{10,11},{11,10},{12,13},{13,12},{18,19},{1... | collective-permute-start | bytes 2752520 | tf_op jit(solution)/shard_map/ppermute | solution.py:62
  99.3 23.6 %collective-permute-start.22 = (f32[448,512]{1,0:T(8,128)S(1)}, f32[448,512]{1,0:T(8,128)S(1)}, u32[]{:S(2)}, u32[]{:S(2)}) collective-permute-start(f32[448,512]{1,0:T(8,128)S(1)} %shard_map.63), channel_id=1, source_target_pairs={{0,1},{1,0},{6,7},{7,6},{8,9},{9,8},{14,15},{15,14},{16,17},{17,16... | collective-permute-start | bytes 2752520 | tf_op jit(solution)/shard_map/ppermute | solution.py:62
  102.7 6.3 %collective-permute-start.23 = (f32[448,384]{1,0:T(8,128)S(1)}, f32[448,384]{1,0:T(8,128)S(1)}, u32[]{:S(2)}, u32[]{:S(2)}) collective-permute-start(f32[448,384]{1,0:T(8,128)S(1)} %get-tuple-element.67), channel_id=1, source_target_pairs={{2,3},{3,2},{4,5},{5,4},{10,11},{11,10},{12,13},{13,12},{18,19},{1... | collective-permute-start | bytes 2064392 | tf_op jit(solution)/shard_map/ppermute | solution.py:62
  103.4 18.5 %collective-permute-start.24 = (f32[448,384]{1,0:T(8,128)S(1)}, f32[448,384]{1,0:T(8,128)S(1)}, u32[]{:S(2)}, u32[]{:S(2)}) collective-permute-start(f32[448,384]{1,0:T(8,128)S(1)} %get-tuple-element.68), channel_id=1, source_target_pairs={{0,1},{1,0},{6,7},{7,6},{8,9},{9,8},{14,15},{15,14},{16,17},{17,16... | collective-permute-start | bytes 2064392 | tf_op jit(solution)/shard_map/ppermute | solution.py:62
  (2 other events, 34.2 us)
